TPU v7x, 512 devices: a whole 4x4x16 slice. The times are simulated.
512 devices in a mesh: member: 32 (over y, z_lo, core), tile: 16 (over x, z_hi).
Axes of the slice: x: 4, y: 4, z: 16 (z_hi: 4, z_lo: 4; z = z_hi * 4 + z_lo), core: 2. Of those that a mesh axis runs over, the one named last changes fastest.
Arguments:
- innovations: bfloat16 [32, 4, 256, 1024], P('member', None, None, 'tile'), may hold values from -6 to 6
- obs_column: int32 [4, 1024], P(None, 'tile'), may hold values from 0 to 511
- physics: float32 [4, 256, 256], replicated, as said below
- diffusion: float32 [256], replicated, may hold values from 0.05 to 0.24
- anomalies: bfloat16 [32, 256, 64, 128], P('member', None, 'tile'), may hold values from -6 to 6
- modes: float32 [256, 16], replicated, may hold values from -3 to 3
- bands: int32 [16], replicated, may hold values from 1 to 8
Outputs:
- gradient: float32 [32, 256, 64, 128], P('member', None, 'tile')
Inputs may be any that keep to these rules, and one draw needn't show every extreme that they name: `obs_column`: index c = x * 128 + y of an observed column within its tile's 4 by 128 columns; indices may repeat. `physics`: each step's matrix has a dominant diagonal near 0.6.
All inputs are finite; a program needn't handle non-finite values.
Results may differ from a plain program's by a relative error of at most 0.0003.
Values sent between devices are 32-bit elements; how exact they have to be, the bound alone decides.
No kernel may reach another device: no remote copies, remote signals or barrier semaphores. Data moves between devices by JAX's collectives and lax.ppermute only.
A program may use at most 64 MiB of HBM per device.

v0:
```python
import jax
import jax.numpy as jnp
from jax import lax
from jax.sharding import PartitionSpec as P

STEPS = 4


def copy_for_each(shard, axis):
    copies = jnp.broadcast_to(shard, (lax.axis_size(axis), *shard.shape))
    return lax.all_to_all(copies, axis, split_axis=0, concat_axis=0, tiled=True)


def taken_together(shard, axis):
    return copy_for_each(shard, axis).sum(axis=0)


def padded_2(block, sides, width):
    for axis, dim in sides:
        count = lax.axis_size(axis)
        forward = [(i, i + 1) for i in range(count - 1)]
        forward.append((count - 1, 0))
        backward = [(target, source) for source, target in forward]
        low = lax.ppermute(
            lax.slice_in_dim(block, block.shape[dim] - width, None, axis=dim), axis, forward
        )
        high = lax.ppermute(lax.slice_in_dim(block, 0, width, axis=dim), axis, backward)
        block = jnp.concatenate([low, block, high], axis=dim)
    return block


def smooth_modes(coeffs, bands):
    length = coeffs.shape[-1]
    padded = jnp.pad(coeffs, ((0, 0), (0, 0), (8, 8)))
    total = jnp.zeros(coeffs.shape, jnp.float32)
    for offset in range(-8, 9):
        weight = (jnp.abs(jnp.int32(offset)) <= bands).astype(jnp.float32)
        total = total + weight[:, None, None] * padded[:, :, 8 + offset : 8 + offset + length]
    return total / (2 * bands + 1).astype(jnp.float32)[:, None, None]


def column_physics(matrix, field):
    return jnp.einsum("rs,rxy->sxy", matrix, field, precision=lax.Precision.HIGHEST)


def diffuse(padded, nu):
    center = padded[:, 1:-1]
    ypad = jnp.pad(center, ((0, 0), (0, 0), (1, 1)))
    beside_all = padded[:, 2:] + padded[:, :-2] + ypad[:, :, 2:] + ypad[:, :, :-2]
    return center + nu[:, None, None] * (beside_all - 4.0 * center)


def per_device(innovations, obs_column, physics, diffusion, anomalies, modes, bands):
    members = lax.axis_size("member")
    spread = anomalies[0].astype(jnp.float32)
    state, width_x, width_y = spread.shape
    columns = jnp.arange(width_x * width_y, dtype=jnp.int32)
    lam = jnp.zeros((state, width_x, width_y), jnp.float32)
    for step in range(STEPS - 1, -1, -1):
        local = jnp.einsum("sk,sxy->kxy", modes, spread * lam, precision=lax.Precision.HIGHEST)
        coeffs = taken_together(local, "member") / jnp.float32(members - 1)
        moved = column_physics(physics[step], lam)
        padded = padded_2(moved, (("tile", 1),), 1)
        spread_out = diffuse(padded, diffusion)
        smooth = smooth_modes(coeffs, bands)
        lifted = jnp.einsum("sk,kxy->sxy", modes, smooth, precision=lax.Precision.HIGHEST)
        onehot = (obs_column[step][:, None] == columns[None, :]).astype(jnp.float32)
        forcing = jnp.dot(
            innovations[0, step].astype(jnp.float32), onehot, precision=lax.Precision.HIGHEST
        )
        forcing = forcing.reshape(state, width_x, width_y)
        lam = spread_out + spread * lifted + forcing
    return lam[None]


def solution(mesh):
    in_specs = (
        P("member", None, None, "tile"),
        P(None, "tile"),
        P(),
        P(),
        P("member", None, "tile", None),
        P(),
        P(),
    )
    out_specs = P("member", None, "tile", None)
    return jax.shard_map(
        per_device, mesh=mesh, in_specs=in_specs, out_specs=out_specs, check_vma=False
    )
```

profile of v0, /device:TPU:1, one launch (start us, length us, event | category | flops | bytes accessed | tf_op | source)
XLA Modules:
  0.0 207.2 jit_solution(4391093479460328919)
XLA Ops:
  0.0 1.1 copy.18
  1.7 1.2 broadcast_in_dim.13
  2.9 10.6 %all-to-all-start = ((f32[32,16,4,128]{3,1,2,0:T(8,128)}), f32[32,16,4,128]{3,1,2,0:T(8,128)S(1)}, u32[]{:S(2)}, u32[]{:S(2)}) async-start(f32[32,16,4,128]{3,1,2,0:T(8,128)} %broadcast_in_dim.13), calls=%async_computation | async-start | bytes 2097152 | tf_op jit(solution)/shard_map/all_to_all | solution.py:11
  14.1 11.8 %collective-permute-start = (f32[256,1,128]{0,2,1:T(8,128)S(1)}, f32[256,1,128]{0,2,1:T(8,128)S(1)}, u32[]{:S(2)}, u32[]{:S(2)}) collective-permute-start(f32[256,1,128]{0,2,1:T(8,128)S(1)} %get-tuple-element.11), channel_id=1, source_target_pairs={{1,0},{2,1},{3,2},{4,3},{5,4},{6,5},{7,6},{8,7},{9,8},{10,9},{11,1... | collective-permute-start | bytes 393224 | tf_op jit(solution)/shard_map/ppermute | solution.py:27
  25.9 1.9 collective-permute-start.1
  30.2 1.1 fusion.47
  31.3 18.7 %all-to-all-done = f32[32,16,4,128]{3,1,2,0:T(8,128)S(1)} async-done(((f32[32,16,4,128]{3,1,2,0:T(8,128)}), f32[32,16,4,128]{3,1,2,0:T(8,128)S(1)}, u32[]{:S(2)}, u32[]{:S(2)}) %all-to-all-start) | async-done | bytes 1048608 | tf_op jit(solution)/shard_map/all_to_all | solution.py:11
  51.5 2.1 %fusion.1 = f32[256,4,128]{0,2,1:T(8,128)S(1)} fusion(f32[256,4,128]{0,2,1:T(8,128)} %bitcast.145, f32[256,4,128]{0,2,1:T(8,128)S(1)} %convolution_bitcast_fusion.7, f32[256,1,128]{0,2,1:T(8,128)} %collective-permute-done.1, f32[256,1,128]{0,2,1:T(8,128)} %copy-done.44, bf16[1,256,4,128]{1,3,2,0:T(8,128)(2,1)S(1)} %copy.18, f32[256]{0:T(256)S(1)} %copy-done.47, ...), kind=kOutput, calls=%fused_computation.17 | convolution fusion | flops 27148288 | bytes 2180736 | tf_op jit(solution)/shard_map/sk,kxy->sxy/dot_general | solution.py:66
  54.3 1.2 broadcast_in_dim.14
  55.4 13.4 %all-to-all-start.1 = ((f32[32,16,4,128]{3,1,2,0:T(8,128)}), f32[32,16,4,128]{3,1,2,0:T(8,128)S(1)}, u32[]{:S(2)}, u32[]{:S(2)}) async-start(f32[32,16,4,128]{3,1,2,0:T(8,128)} %broadcast_in_dim.14), calls=%async_computation.1 | async-start | bytes 2097152 | tf_op jit(solution)/shard_map/all_to_all | solution.py:11
  69.4 1.1 fusion.48
  71.2 5.2 %collective-permute-start.2 = (f32[256,1,128]{0,2,1:T(8,128)S(1)}, f32[256,1,128]{0,2,1:T(8,128)S(1)}, u32[]{:S(2)}, u32[]{:S(2)}) collective-permute-start(f32[256,1,128]{0,2,1:T(8,128)S(1)} %get-tuple-element.9), channel_id=1, source_target_pairs={{1,0},{2,1},{3,2},{4,3},{5,4},{6,5},{7,6},{8,7},{9,8},{10,9},{11,1... | collective-permute-start | bytes 393224 | tf_op jit(solution)/shard_map/ppermute | solution.py:27
  76.4 4.0 %collective-permute-start.3 = (f32[256,1,128]{0,2,1:T(8,128)S(1)}, f32[256,1,128]{0,2,1:T(8,128)}, u32[]{:S(2)}, u32[]{:S(2)}) collective-permute-start(f32[256,1,128]{0,2,1:T(8,128)S(1)} %get-tuple-element.10), channel_id=1, source_target_pairs={{0,1},{1,2},{2,3},{3,4},{4,5},{5,6},{6,7},{7,8},{8,9},{9,10},{10,1... | collective-permute-start | bytes 393224 | tf_op jit(solution)/shard_map/ppermute | solution.py:24
  80.4 24.9 %all-to-all-done.1 = f32[32,16,4,128]{3,1,2,0:T(8,128)S(1)} async-done(((f32[32,16,4,128]{3,1,2,0:T(8,128)}), f32[32,16,4,128]{3,1,2,0:T(8,128)S(1)}, u32[]{:S(2)}, u32[]{:S(2)}) %all-to-all-start.1) | async-done | bytes 1048608 | tf_op jit(solution)/shard_map/all_to_all | solution.py:11
  106.8 2.2 %fusion.3 = f32[256,4,128]{0,2,1:T(8,128)S(1)} fusion(f32[256,4,128]{0,2,1:T(8,128)} %bitcast.143, f32[256,4,128]{0,2,1:T(8,128)S(1)} %convolution_bitcast_fusion.6, f32[256,1,128]{0,2,1:T(8,128)} %collective-permute-done.3, f32[256,1,128]{0,2,1:T(8,128)} %copy-done.45, bf16[1,256,4,128]{1,3,2,0:T(8,128)(2,1)S(1)} %copy.18, f32[256]{0:T(256)S(1)} %copy-done.48, ...), kind=kOutput, calls=%fused_computation.19 | convolution fusion | flops 27148288 | bytes 2180736 | tf_op jit(solution)/shard_map/sk,kxy->sxy/dot_general | solution.py:66
  109.5 1.2 broadcast_in_dim.15
  110.7 7.2 %all-to-all-start.2 = ((f32[32,16,4,128]{3,1,2,0:T(8,128)}), f32[32,16,4,128]{3,1,2,0:T(8,128)S(1)}, u32[]{:S(2)}, u32[]{:S(2)}) async-start(f32[32,16,4,128]{3,1,2,0:T(8,128)} %broadcast_in_dim.15), calls=%async_computation.2 | async-start | bytes 2097152 | tf_op jit(solution)/shard_map/all_to_all | solution.py:11
  117.9 0.7 copy-done.8
  118.5 1.1 fusion.49
  120.3 6.9 %collective-permute-start.4 = (f32[256,1,128]{0,2,1:T(8,128)S(1)}, f32[256,1,128]{0,2,1:T(8,128)S(1)}, u32[]{:S(2)}, u32[]{:S(2)}) collective-permute-start(f32[256,1,128]{0,2,1:T(8,128)S(1)} %get-tuple-element.7), channel_id=1, source_target_pairs={{1,0},{2,1},{3,2},{4,3},{5,4},{6,5},{7,6},{8,7},{9,8},{10,9},{11,1... | collective-permute-start | bytes 393224 | tf_op jit(solution)/shard_map/ppermute | solution.py:27
  127.2 2.3 %collective-permute-start.5 = (f32[256,1,128]{0,2,1:T(8,128)S(1)}, f32[256,1,128]{0,2,1:T(8,128)}, u32[]{:S(2)}, u32[]{:S(2)}) collective-permute-start(f32[256,1,128]{0,2,1:T(8,128)S(1)} %get-tuple-element.8), channel_id=1, source_target_pairs={{0,1},{1,2},{2,3},{3,4},{4,5},{5,6},{6,7},{7,8},{8,9},{9,10},{10,1... | collective-permute-start | bytes 393224 | tf_op jit(solution)/shard_map/ppermute | solution.py:24
  129.5 24.9 %all-to-all-done.2 = f32[32,16,4,128]{3,1,2,0:T(8,128)S(1)} async-done(((f32[32,16,4,128]{3,1,2,0:T(8,128)}), f32[32,16,4,128]{3,1,2,0:T(8,128)S(1)}, u32[]{:S(2)}, u32[]{:S(2)}) %all-to-all-start.2) | async-done | bytes 1048608 | tf_op jit(solution)/shard_map/all_to_all | solution.py:11
  155.8 2.2 %fusion.5 = f32[256,4,128]{0,2,1:T(8,128)S(1)} fusion(f32[256,4,128]{0,2,1:T(8,128)} %bitcast.144, f32[256,4,128]{0,2,1:T(8,128)S(1)} %convolution_bitcast_fusion.5, f32[256,1,128]{0,2,1:T(8,128)} %collective-permute-done.5, f32[256,1,128]{0,2,1:T(8,128)} %copy-done.46, bf16[1,256,4,128]{1,3,2,0:T(8,128)(2,1)S(1)} %copy.18, f32[256]{0:T(256)S(1)} %copy-done.49, ...), kind=kOutput, calls=%fused_computation.21 | convolution fusion | flops 27148288 | bytes 2180736 | tf_op jit(solution)/shard_map/sk,kxy->sxy/dot_general | solution.py:66
  158.5 1.2 broadcast_in_dim.16
  159.7 8.1 %all-to-all-start.3 = ((f32[32,16,4,128]{3,1,2,0:T(8,128)}), f32[32,16,4,128]{3,1,2,0:T(8,128)S(1)}, u32[]{:S(2)}, u32[]{:S(2)}) async-start(f32[32,16,4,128]{3,1,2,0:T(8,128)} %broadcast_in_dim.16), calls=%async_computation.3 | async-start | bytes 2097152 | tf_op jit(solution)/shard_map/all_to_all | solution.py:11
  167.8 0.6 copy-done.7
  168.5 1.1 fusion.50
  170.2 5.9 %collective-permute-start.6 = (f32[256,1,128]{0,2,1:T(8,128)S(1)}, f32[256,1,128]{0,2,1:T(8,128)S(1)}, u32[]{:S(2)}, u32[]{:S(2)}) collective-permute-start(f32[256,1,128]{0,2,1:T(8,128)S(1)} %get-tuple-element.5), channel_id=1, source_target_pairs={{1,0},{2,1},{3,2},{4,3},{5,4},{6,5},{7,6},{8,7},{9,8},{10,9},{11,1... | collective-permute-start | bytes 393224 | tf_op jit(solution)/shard_map/ppermute | solution.py:27
  176.2 3.4 %collective-permute-start.7 = (f32[256,1,128]{0,2,1:T(8,128)S(1)}, f32[256,1,128]{0,2,1:T(8,128)S(1)}, u32[]{:S(2)}, u32[]{:S(2)}) collective-permute-start(f32[256,1,128]{0,2,1:T(8,128)S(1)} %get-tuple-element.6), channel_id=1, source_target_pairs={{0,1},{1,2},{2,3},{3,4},{4,5},{5,6},{6,7},{7,8},{8,9},{9,10},{10,1... | collective-permute-start | bytes 393224 | tf_op jit(solution)/shard_map/ppermute | solution.py:24
  179.6 24.8 %all-to-all-done.3 = f32[32,16,4,128]{3,1,2,0:T(8,128)S(1)} async-done(((f32[32,16,4,128]{3,1,2,0:T(8,128)}), f32[32,16,4,128]{3,1,2,0:T(8,128)S(1)}, u32[]{:S(2)}, u32[]{:S(2)}) %all-to-all-start.3) | async-done | bytes 1048608 | tf_op jit(solution)/shard_map/all_to_all | solution.py:11
  205.2 1.0 fusion.8
  206.3 1.0 copy.23
  (148 shorter events, 12.2 us)
Async XLA Ops:
  2.9 10.6 %copy-start.1 = (f32[4,256,256]{2,1,0:T(8,128)S(1)}, f32[4,256,256]{2,1,0:T(8,128)}, u32[]{:S(2)}) copy-start(f32[4,256,256]{2,1,0:T(8,128)} %param.9) | copy-start | bytes 3145732
  2.9 47.2 %all-to-all-start = ((f32[32,16,4,128]{3,1,2,0:T(8,128)}), f32[32,16,4,128]{3,1,2,0:T(8,128)S(1)}, u32[]{:S(2)}, u32[]{:S(2)}) async-start(f32[32,16,4,128]{3,1,2,0:T(8,128)} %broadcast_in_dim.13), calls=%async_computation | async-start | bytes 2097152 | tf_op jit(solution)/shard_map/all_to_all | solution.py:11
  14.0 16.2 %copy-start.3 = (bf16[1,4,256,64]{2,3,1,0:T(8,128)(2,1)S(1)}, bf16[1,4,256,64]{2,3,1,0:T(8,128)(2,1)}, u32[]{:S(2)}) copy-start(bf16[1,4,256,64]{2,3,1,0:T(8,128)(2,1)} %param.7) | copy-start | bytes 393220
  14.1 13.8 %copy-start.11 = (s32[16]{0:T(128)S(1)}, s32[16]{0:T(128)}, u32[]{:S(2)}) copy-start(s32[16]{0:T(128)} %param.13) | copy-start | bytes 196
  14.1 36.1 %collective-permute-start = (f32[256,1,128]{0,2,1:T(8,128)S(1)}, f32[256,1,128]{0,2,1:T(8,128)S(1)}, u32[]{:S(2)}, u32[]{:S(2)}) collective-permute-start(f32[256,1,128]{0,2,1:T(8,128)S(1)} %get-tuple-element.11), channel_id=1, source_target_pairs={{1,0},{2,1},{3,2},{4,3},{5,4},{6,5},{7,6},{8,7},{9,8},{10,9},{11,1... | collective-permute-start | bytes 393224 | tf_op jit(solution)/shard_map/ppermute | solution.py:27
  25.9 3.0 %copy-start.10 = (s32[4,64]{1,0:T(4,128)S(1)}, s32[4,64]{1,0:T(4,128)}, u32[]{:S(2)}) copy-start(s32[4,64]{1,0:T(4,128)} %param.8) | copy-start | bytes 3076
  25.9 24.3 %collective-permute-start.1 = (f32[256,1,128]{0,2,1:T(8,128)S(1)}, f32[256,1,128]{0,2,1:T(8,128)}, u32[]{:S(2)}, u32[]{:S(2)}) collective-permute-start(f32[256,1,128]{0,2,1:T(8,128)S(1)} %get-tuple-element.12), channel_id=1, source_target_pairs={{0,1},{1,2},{2,3},{3,4},{4,5},{5,6},{6,7},{7,8},{8,9},{9,10},{10,1... | collective-permute-start | bytes 393224 | tf_op jit(solution)/shard_map/ppermute | solution.py:24
  55.4 49.9 %all-to-all-start.1 = ((f32[32,16,4,128]{3,1,2,0:T(8,128)}), f32[32,16,4,128]{3,1,2,0:T(8,128)S(1)}, u32[]{:S(2)}, u32[]{:S(2)}) async-start(f32[32,16,4,128]{3,1,2,0:T(8,128)} %broadcast_in_dim.14), calls=%async_computation.1 | async-start | bytes 2097152 | tf_op jit(solution)/shard_map/all_to_all | solution.py:11
  71.2 34.8 %collective-permute-start.2 = (f32[256,1,128]{0,2,1:T(8,128)S(1)}, f32[256,1,128]{0,2,1:T(8,128)S(1)}, u32[]{:S(2)}, u32[]{:S(2)}) collective-permute-start(f32[256,1,128]{0,2,1:T(8,128)S(1)} %get-tuple-element.9), channel_id=1, source_target_pairs={{1,0},{2,1},{3,2},{4,3},{5,4},{6,5},{7,6},{8,7},{9,8},{10,9},{11,1... | collective-permute-start | bytes 393224 | tf_op jit(solution)/shard_map/ppermute | solution.py:27
  76.4 29.7 %collective-permute-start.3 = (f32[256,1,128]{0,2,1:T(8,128)S(1)}, f32[256,1,128]{0,2,1:T(8,128)}, u32[]{:S(2)}, u32[]{:S(2)}) collective-permute-start(f32[256,1,128]{0,2,1:T(8,128)S(1)} %get-tuple-element.10), channel_id=1, source_target_pairs={{0,1},{1,2},{2,3},{3,4},{4,5},{5,6},{6,7},{7,8},{8,9},{9,10},{10,1... | collective-permute-start | bytes 393224 | tf_op jit(solution)/shard_map/ppermute | solution.py:24
  105.4 1.3 copy-start.25
  105.4 1.2 copy-start.29
  105.5 1.2 copy-start.33
  105.5 1.2 copy-start.37
  105.5 1.2 copy-start.41
  105.5 1.2 copy-start.48
  105.5 1.2 copy-start.52
  105.5 1.2 copy-start.56
  110.7 43.7 %all-to-all-start.2 = ((f32[32,16,4,128]{3,1,2,0:T(8,128)}), f32[32,16,4,128]{3,1,2,0:T(8,128)S(1)}, u32[]{:S(2)}, u32[]{:S(2)}) async-start(f32[32,16,4,128]{3,1,2,0:T(8,128)} %broadcast_in_dim.15), calls=%async_computation.2 | async-start | bytes 2097152 | tf_op jit(solution)/shard_map/all_to_all | solution.py:11
  120.3 34.8 %collective-permute-start.4 = (f32[256,1,128]{0,2,1:T(8,128)S(1)}, f32[256,1,128]{0,2,1:T(8,128)S(1)}, u32[]{:S(2)}, u32[]{:S(2)}) collective-permute-start(f32[256,1,128]{0,2,1:T(8,128)S(1)} %get-tuple-element.7), channel_id=1, source_target_pairs={{1,0},{2,1},{3,2},{4,3},{5,4},{6,5},{7,6},{8,7},{9,8},{10,9},{11,1... | collective-permute-start | bytes 393224 | tf_op jit(solution)/shard_map/ppermute | solution.py:27
  127.2 27.9 %collective-permute-start.5 = (f32[256,1,128]{0,2,1:T(8,128)S(1)}, f32[256,1,128]{0,2,1:T(8,128)}, u32[]{:S(2)}, u32[]{:S(2)}) collective-permute-start(f32[256,1,128]{0,2,1:T(8,128)S(1)} %get-tuple-element.8), channel_id=1, source_target_pairs={{0,1},{1,2},{2,3},{3,4},{4,5},{5,6},{6,7},{7,8},{8,9},{9,10},{10,1... | collective-permute-start | bytes 393224 | tf_op jit(solution)/shard_map/ppermute | solution.py:24
  154.5 1.3 copy-start.26
  154.5 1.2 copy-start.30
  154.5 1.2 copy-start.34
  154.5 1.2 copy-start.38
  154.5 1.2 copy-start.42
  154.5 1.2 copy-start.49
  154.5 1.2 copy-start.53
  159.7 44.7 %all-to-all-start.3 = ((f32[32,16,4,128]{3,1,2,0:T(8,128)}), f32[32,16,4,128]{3,1,2,0:T(8,128)S(1)}, u32[]{:S(2)}, u32[]{:S(2)}) async-start(f32[32,16,4,128]{3,1,2,0:T(8,128)} %broadcast_in_dim.16), calls=%async_computation.3 | async-start | bytes 2097152 | tf_op jit(solution)/shard_map/all_to_all | solution.py:11
  170.2 34.3 %collective-permute-start.6 = (f32[256,1,128]{0,2,1:T(8,128)S(1)}, f32[256,1,128]{0,2,1:T(8,128)S(1)}, u32[]{:S(2)}, u32[]{:S(2)}) collective-permute-start(f32[256,1,128]{0,2,1:T(8,128)S(1)} %get-tuple-element.5), channel_id=1, source_target_pairs={{1,0},{2,1},{3,2},{4,3},{5,4},{6,5},{7,6},{8,7},{9,8},{10,9},{11,1... | collective-permute-start | bytes 393224 | tf_op jit(solution)/shard_map/ppermute | solution.py:27
  176.2 28.4 %copy-start.2 = (f32[512,256]{1,0:T(8,128)S(1)}, f32[512,256]{1,0:T(8,128)}, u32[]{:S(2)}) copy-start(f32[512,256]{1,0:T(8,128)} %fusion.50) | copy-start | bytes 1572868
  176.2 28.4 %collective-permute-start.7 = (f32[256,1,128]{0,2,1:T(8,128)S(1)}, f32[256,1,128]{0,2,1:T(8,128)S(1)}, u32[]{:S(2)}, u32[]{:S(2)}) collective-permute-start(f32[256,1,128]{0,2,1:T(8,128)S(1)} %get-tuple-element.6), channel_id=1, source_target_pairs={{0,1},{1,2},{2,3},{3,4},{4,5},{5,6},{6,7},{7,8},{8,9},{9,10},{10,1... | collective-permute-start | bytes 393224 | tf_op jit(solution)/shard_map/ppermute | solution.py:24
  (39 other events, 27.5 us)
where the time goes:
time: 209 us; the launch traced here: 207 us
  waiting for transfers between devices  93.3 us (45%)
  starting transfers between devices  80.7 us (39%)
  matrix products  16.6 us (8%)
  local copies, waits for them, and re-layouts  13.7 us (7%)
    all_to_all x4, waiting for transfers between devices, copy_for_each(): return lax.all_to_all(copies, axis, split_axis=0, concat_axis=0, tiled=True)  93.3 us
    all_to_all x4, starting transfers between devices, copy_for_each(): return lax.all_to_all(copies, axis, split_axis=0, concat_axis=0, tiled=True)  39.3 us
    ppermute x4, starting transfers between devices, padded_2(): lax.ppermute(lax.slice_in_dim(block, 0, width, axis=dim), axis, backward)  29.8 us
    ppermute x4, starting transfers between devices, padded_2(): lax.ppermute(lax.slice_in_dim(block, block.shape[dim] - width, None, axis...  11.7 us
    dot_general x4, matrix products, per_device(): jnp.einsum('sk,kxy->sxy', modes, smooth, precision=lax.Precision.HIGHEST)  7.46 us
    unnamed x119, local copies, waits for them, and re-layouts  7.36 us
    broadcast_in_dim x4, local copies, waits for them, and re-layouts, copy_for_each(): copies = jnp.broadcast_to(shard, (lax.axis_size(axis), *shard.shape))  4.63 us
    dot_general x4, matrix products, per_device(): jnp.dot(innovations[0, step].astype(jnp.float32), onehot, precision=lax.P...  4.55 us
  transfers between devices with their start and end apart: 12, of which 4 were waited for; matrix products, arithmetic and copies ran while one was open for 5% of the time, Pallas kernels for 0%

commit v1 on v0

v1 whole, which is shorter than its diff:
```python
import jax
import jax.numpy as jnp
from jax import lax
from jax.sharding import PartitionSpec as P

STEPS = 4
HI = lax.Precision.HIGHEST


def band_matrix(band, length):
    pos = jnp.arange(length, dtype=jnp.int32)
    near = jnp.abs(pos[:, None] - pos[None, :]) <= band
    return near.astype(jnp.float32)


def summed_smooth(local, near, scale):
    members = lax.axis_size("member")
    modes, width_x, width_y = local.shape
    pieces = local.reshape(members, modes * width_x // members, width_y)
    mine = lax.all_to_all(pieces, "member", 0, 0, tiled=True).sum(axis=0)
    mine = jnp.dot(mine, near, precision=HI) * scale
    copies = jnp.broadcast_to(mine[None], (members, *mine.shape))
    whole = lax.all_to_all(copies, "member", 0, 0, tiled=True)
    return whole.reshape(modes, width_x, width_y)


def edges_from_neighbours(field, axis):
    count = lax.axis_size(axis)
    forward = [(i, (i + 1) % count) for i in range(count)]
    backward = [(target, source) for source, target in forward]
    low = lax.ppermute(field[:, -1:], axis, forward)
    high = lax.ppermute(field[:, :1], axis, backward)
    return low, high


def diffuse(padded, nu):
    center = padded[:, 1:-1]
    ypad = jnp.pad(center, ((0, 0), (0, 0), (1, 1)))
    beside_all = padded[:, 2:] + padded[:, :-2] + ypad[:, :, 2:] + ypad[:, :, :-2]
    return center + nu[:, None, None] * (beside_all - 4.0 * center)


def per_device(innovations, obs_column, physics, diffusion, anomalies, modes, bands):
    members = lax.axis_size("member")
    spread = anomalies[0].astype(jnp.float32)
    state, width_x, width_y = spread.shape
    columns = jnp.arange(width_x * width_y, dtype=jnp.int32)
    rows_each = modes.shape[1] * width_x // members
    mode = lax.axis_index("member") * rows_each // width_x
    band = lax.dynamic_index_in_dim(bands, mode, keepdims=False)
    near = band_matrix(band, width_y)
    scale = 1.0 / ((members - 1) * (2 * band + 1)).astype(jnp.float32)

    def forcing(step):
        onehot = (obs_column[step][:, None] == columns[None, :]).astype(jnp.bfloat16)
        out = jnp.dot(innovations[0, step], onehot, preferred_element_type=jnp.float32)
        return out.reshape(state, width_x, width_y)

    lam = forcing(STEPS - 1)
    for step in range(STEPS - 2, -1, -1):
        local = jnp.einsum("sk,sxy->kxy", modes, spread * lam, precision=HI)
        smooth = summed_smooth(local, near, scale)
        moved = jnp.einsum("rs,rxy->sxy", physics[step], lam, precision=HI)
        low, high = edges_from_neighbours(moved, "tile")
        padded = jnp.concatenate([low, moved, high], axis=1)
        spread_out = diffuse(padded, diffusion)
        lifted = jnp.einsum("sk,kxy->sxy", modes, smooth, precision=HI)
        lam = spread_out + spread * lifted + forcing(step)
    return lam[None]


def solution(mesh):
    in_specs = (
        P("member", None, None, "tile"),
        P(None, "tile"),
        P(),
        P(),
        P("member", None, "tile", None),
        P(),
        P(),
    )
    out_specs = P("member", None, "tile", None)
    return jax.shard_map(
        per_device, mesh=mesh, in_specs=in_specs, out_specs=out_specs, check_vma=False
    )
```

time: 209 us -> 124 us (0.59)
  waiting for transfers between devices: 93.3 us -> 21.5 us
  matrix products: 16.6 us -> 9.58 us
  local copies, waits for them, and re-layouts: 13.7 us -> 8.16 us
  starting transfers between devices: 80.7 us -> 83 us
    all_to_all x4 -> x6, waiting for transfers between devices: 93.3 us -> 16.2 us  [the longest x3 16.2 us: summed_smooth(): whole = lax.all_to_all(copies, 'member', 0, 0, tiled=True)]
    all_to_all x4 -> x6, starting transfers between devices: 39.3 us -> 50.9 us  [the longest x3 26.4 us: summed_smooth(): mine = lax.all_to_all(pieces, 'member', 0, 0, tiled=True).sum(axis=0)]
    ppermute x8 -> x6, starting transfers between devices: 41.5 us -> 32.1 us  [the longest x3 20.9 us: edges_from_neighbours(): high = lax.ppermute(field[:, :1], axis, backward)]
    dot_general x16, matrix products: 16.6 us -> 9.58 us  [the longest x3 2.47 us: summed_smooth(): mine = jnp.dot(mine, near, precision=HI) * scale]
    ppermute x8 -> x6, waiting for transfers between devices: 0.02 us -> 5.28 us  [the longest x3 5.28 us: edges_from_neighbours(): low = lax.ppermute(field[:, -1:], axis, forward)]
    unnamed x119 -> x13, local copies, waits for them, and re-layouts: 7.36 us -> 2.54 us
    broadcast_in_dim x4 -> x3, local copies, waits for them, and re-layouts: 4.63 us -> 1.97 us  [summed_smooth(): copies = jnp.broadcast_to(mine[None], (members, *mine.shape))]
  transfers between devices with their start and end apart: 12 -> 12, of which waited for: 4 -> 4; matrix products, arithmetic and copies ran while one was open for 5% -> 6% of each run, Pallas kernels for 0% -> 0%
where the time goes in v1:
time: 124 us; the launch traced here: 123 us
  starting transfers between devices  83 us (67%)
  waiting for transfers between devices  21.5 us (17%)
  matrix products  9.58 us (8%)
  local copies, waits for them, and re-layouts  8.16 us (7%)
    all_to_all x3, starting transfers between devices, summed_smooth(): mine = lax.all_to_all(pieces, 'member', 0, 0, tiled=True).sum(axis=0)  26.4 us
    all_to_all x3, starting transfers between devices, summed_smooth(): whole = lax.all_to_all(copies, 'member', 0, 0, tiled=True)  24.5 us
    ppermute x3, starting transfers between devices, edges_from_neighbours(): high = lax.ppermute(field[:, :1], axis, backward)  20.9 us
    all_to_all x3, waiting for transfers between devices, summed_smooth(): whole = lax.all_to_all(copies, 'member', 0, 0, tiled=True)  16.2 us
    ppermute x3, starting transfers between devices, edges_from_neighbours(): low = lax.ppermute(field[:, -1:], axis, forward)  11.2 us
    ppermute x3, waiting for transfers between devices, edges_from_neighbours(): low = lax.ppermute(field[:, -1:], axis, forward)  5.28 us
    unnamed x13, local copies, waits for them, and re-layouts  2.54 us
  transfers between devices with their start and end apart: 12, of which 4 were waited for; matrix products, arithmetic and copies ran while one was open for 6% of the time, Pallas kernels for 0%

profile of v1, /device:TPU:1, one launch (start us, length us, event | category | flops | bytes accessed | tf_op | source)
XLA Modules:
  0.0 123.4 jit_solution(8117222686979952102)
XLA Ops:
  0.0 1.2 copy.13
  2.2 0.6 copy.15
  2.8 10.3 %all-to-all-start = ((f32[32,2,128]{2,1,0:T(2,128)}), f32[32,2,128]{2,1,0:T(2,128)S(1)}, u32[]{:S(2)}, u32[]{:S(2)}) async-start(f32[32,2,128]{2,1,0:T(2,128)} %bitcast.12), calls=%async_computation | async-start | bytes 65536 | tf_op jit(solution)/shard_map/all_to_all | solution.py:20
  13.8 11.8 %collective-permute-start = (f32[256,1,128]{0,2,1:T(8,128)S(1)}, f32[256,1,128]{0,2,1:T(8,128)S(1)}, u32[]{:S(2)}, u32[]{:S(2)}) collective-permute-start(f32[256,1,128]{0,2,1:T(8,128)S(1)} %get-tuple-element.9), channel_id=1, source_target_pairs={{1,0},{2,1},{3,2},{4,3},{5,4},{6,5},{7,6},{8,7},{9,8},{10,9},{11,1... | collective-permute-start | bytes 393224 | tf_op jit(solution)/shard_map/ppermute | solution.py:32
  25.6 1.9 %collective-permute-start.1 = (f32[256,1,128]{0,2,1:T(8,128)S(1)}, f32[256,1,128]{0,2,1:T(8,128)S(1)}, u32[]{:S(2)}, u32[]{:S(2)}) collective-permute-start(f32[256,1,128]{0,2,1:T(8,128)S(1)} %get-tuple-element.10), channel_id=1, source_target_pairs={{0,1},{1,2},{2,3},{3,4},{4,5},{5,6},{6,7},{7,8},{8,9},{9,10},{10,1... | collective-permute-start | bytes 393224 | tf_op jit(solution)/shard_map/ppermute | solution.py:31
  27.6 0.6 copy-done.5
  28.2 0.7 dynamic_slice.4
  29.7 0.8 convolution_multiply_fusion.2
  30.5 0.7 broadcast_in_dim.8
  31.1 8.0 %all-to-all-start.1 = ((f32[32,2,128]{2,1,0:T(2,128)}), f32[32,2,128]{2,1,0:T(2,128)S(1)}, u32[]{:S(2)}, u32[]{:S(2)}) async-start(f32[32,2,128]{2,1,0:T(2,128)} %broadcast_in_dim.8), calls=%async_computation.1 | async-start | bytes 65536 | tf_op jit(solution)/shard_map/all_to_all | solution.py:23
  39.5 7.2 %all-to-all-done.1 = f32[32,2,128]{2,1,0:T(2,128)S(1)} async-done(((f32[32,2,128]{2,1,0:T(2,128)}), f32[32,2,128]{2,1,0:T(2,128)S(1)}, u32[]{:S(2)}, u32[]{:S(2)}) %all-to-all-start.1) | async-done | bytes 32800 | tf_op jit(solution)/shard_map/all_to_all | solution.py:23
  46.6 0.7 copy-done.4
  47.3 0.8 fusion.9
  49.2 0.6 copy.18
  49.9 8.6 %all-to-all-start.2 = ((f32[32,2,128]{2,1,0:T(2,128)}), f32[32,2,128]{2,1,0:T(2,128)S(1)}, u32[]{:S(2)}, u32[]{:S(2)}) async-start(f32[32,2,128]{2,1,0:T(2,128)} %bitcast.24), calls=%async_computation.2 | async-start | bytes 65536 | tf_op jit(solution)/shard_map/all_to_all | solution.py:20
  58.5 5.1 %collective-permute-start.2 = (f32[256,1,128]{0,2,1:T(8,128)S(1)}, f32[256,1,128]{0,2,1:T(8,128)S(1)}, u32[]{:S(2)}, u32[]{:S(2)}) collective-permute-start(f32[256,1,128]{0,2,1:T(8,128)S(1)} %get-tuple-element.7), channel_id=1, source_target_pairs={{1,0},{2,1},{3,2},{4,3},{5,4},{6,5},{7,6},{8,7},{9,8},{10,9},{11,1... | collective-permute-start | bytes 393224 | tf_op jit(solution)/shard_map/ppermute | solution.py:32
  63.6 4.1 %collective-permute-start.3 = (f32[256,1,128]{0,2,1:T(8,128)S(1)}, f32[256,1,128]{0,2,1:T(8,128)S(1)}, u32[]{:S(2)}, u32[]{:S(2)}) collective-permute-start(f32[256,1,128]{0,2,1:T(8,128)S(1)} %get-tuple-element.8), channel_id=1, source_target_pairs={{0,1},{1,2},{2,3},{3,4},{4,5},{5,6},{6,7},{7,8},{8,9},{9,10},{10,1... | collective-permute-start | bytes 393224 | tf_op jit(solution)/shard_map/ppermute | solution.py:31
  67.8 0.8 convolution_multiply_fusion.1
  68.6 0.7 broadcast_in_dim.9
  69.3 8.2 %all-to-all-start.3 = ((f32[32,2,128]{2,1,0:T(2,128)}), f32[32,2,128]{2,1,0:T(2,128)S(1)}, u32[]{:S(2)}, u32[]{:S(2)}) async-start(f32[32,2,128]{2,1,0:T(2,128)} %broadcast_in_dim.9), calls=%async_computation.3 | async-start | bytes 65536 | tf_op jit(solution)/shard_map/all_to_all | solution.py:23
  77.9 7.2 %all-to-all-done.3 = f32[32,2,128]{2,1,0:T(2,128)S(1)} async-done(((f32[32,2,128]{2,1,0:T(2,128)}), f32[32,2,128]{2,1,0:T(2,128)S(1)}, u32[]{:S(2)}, u32[]{:S(2)}) %all-to-all-start.3) | async-done | bytes 32800 | tf_op jit(solution)/shard_map/all_to_all | solution.py:23
  85.0 0.8 fusion.7
  87.6 7.5 %all-to-all-start.4 = ((f32[32,2,128]{2,1,0:T(2,128)}), f32[32,2,128]{2,1,0:T(2,128)S(1)}, u32[]{:S(2)}, u32[]{:S(2)}) async-start(f32[32,2,128]{2,1,0:T(2,128)} %bitcast.35), calls=%async_computation.4 | async-start | bytes 65536 | tf_op jit(solution)/shard_map/all_to_all | solution.py:20
  95.2 4.0 %collective-permute-start.4 = (f32[256,1,128]{0,2,1:T(8,128)S(1)}, f32[256,1,128]{0,2,1:T(8,128)S(1)}, u32[]{:S(2)}, u32[]{:S(2)}) collective-permute-start(f32[256,1,128]{0,2,1:T(8,128)S(1)} %get-tuple-element.5), channel_id=1, source_target_pairs={{1,0},{2,1},{3,2},{4,3},{5,4},{6,5},{7,6},{8,7},{9,8},{10,9},{11,1... | collective-permute-start | bytes 393224 | tf_op jit(solution)/shard_map/ppermute | solution.py:32
  99.2 5.2 %collective-permute-start.5 = (f32[256,1,128]{0,2,1:T(8,128)S(1)}, f32[256,1,128]{0,2,1:T(8,128)S(1)}, u32[]{:S(2)}, u32[]{:S(2)}) collective-permute-start(f32[256,1,128]{0,2,1:T(8,128)S(1)} %get-tuple-element.6), channel_id=1, source_target_pairs={{0,1},{1,2},{2,3},{3,4},{4,5},{5,6},{6,7},{7,8},{8,9},{9,10},{10,1... | collective-permute-start | bytes 393224 | tf_op jit(solution)/shard_map/ppermute | solution.py:31
  104.4 0.8 convolution_multiply_fusion
  105.2 0.7 broadcast_in_dim.10
  105.9 8.2 %all-to-all-start.5 = ((f32[32,2,128]{2,1,0:T(2,128)}), f32[32,2,128]{2,1,0:T(2,128)S(1)}, u32[]{:S(2)}, u32[]{:S(2)}) async-start(f32[32,2,128]{2,1,0:T(2,128)} %broadcast_in_dim.10), calls=%async_computation.5 | async-start | bytes 65536 | tf_op jit(solution)/shard_map/all_to_all | solution.py:23
  114.5 5.3 %collective-permute-done.5 = f32[256,1,128]{0,2,1:T(8,128)S(1)} collective-permute-done((f32[256,1,128]{0,2,1:T(8,128)S(1)}, f32[256,1,128]{0,2,1:T(8,128)S(1)}, u32[]{:S(2)}, u32[]{:S(2)}) %collective-permute-start.5) | collective-permute-done | bytes 131104 | tf_op jit(solution)/shard_map/ppermute | solution.py:31
  119.8 1.9 %all-to-all-done.5 = f32[32,2,128]{2,1,0:T(2,128)S(1)} async-done(((f32[32,2,128]{2,1,0:T(2,128)}), f32[32,2,128]{2,1,0:T(2,128)S(1)}, u32[]{:S(2)}, u32[]{:S(2)}) %all-to-all-start.5) | async-done | bytes 32800 | tf_op jit(solution)/shard_map/all_to_all | solution.py:23
  121.7 0.8 fusion.5
  122.4 1.0 copy.23
  (36 shorter events, 5.7 us)
Async XLA Ops:
  0.0 1.6 %copy-start = (f32[256,16]{0,1:T(8,128)S(1)}, f32[256,16]{0,1:T(8,128)}, u32[]{:S(2)}) copy-start(f32[256,16]{0,1:T(8,128)} %param.12) | copy-start | bytes 49156
  0.0 1.2 copy-start.3
  0.0 1.2 %copy-start.2 = (bf16[1,4,256,64]{2,3,1,0:T(8,128)(2,1)S(1)}, bf16[1,4,256,64]{2,3,1,0:T(8,128)(2,1)}, u32[]{:S(2)}) copy-start(bf16[1,4,256,64]{2,3,1,0:T(8,128)(2,1)} %param.7) | copy-start | bytes 393220
  0.0 13.2 %copy-start.1 = (f32[4,256,256]{2,1,0:T(8,128)S(1)}, f32[4,256,256]{2,1,0:T(8,128)}, u32[]{:S(2)}) copy-start(f32[4,256,256]{2,1,0:T(8,128)} %param.9) | copy-start | bytes 3145732
  2.8 26.8 %all-to-all-start = ((f32[32,2,128]{2,1,0:T(2,128)}), f32[32,2,128]{2,1,0:T(2,128)S(1)}, u32[]{:S(2)}, u32[]{:S(2)}) async-start(f32[32,2,128]{2,1,0:T(2,128)} %bitcast.12), calls=%async_computation | async-start | bytes 65536 | tf_op jit(solution)/shard_map/all_to_all | solution.py:20
  13.8 25.7 %collective-permute-start = (f32[256,1,128]{0,2,1:T(8,128)S(1)}, f32[256,1,128]{0,2,1:T(8,128)S(1)}, u32[]{:S(2)}, u32[]{:S(2)}) collective-permute-start(f32[256,1,128]{0,2,1:T(8,128)S(1)} %get-tuple-element.9), channel_id=1, source_target_pairs={{1,0},{2,1},{3,2},{4,3},{5,4},{6,5},{7,6},{8,7},{9,8},{10,9},{11,1... | collective-permute-start | bytes 393224 | tf_op jit(solution)/shard_map/ppermute | solution.py:32
  25.6 13.9 %collective-permute-start.1 = (f32[256,1,128]{0,2,1:T(8,128)S(1)}, f32[256,1,128]{0,2,1:T(8,128)S(1)}, u32[]{:S(2)}, u32[]{:S(2)}) collective-permute-start(f32[256,1,128]{0,2,1:T(8,128)S(1)} %get-tuple-element.10), channel_id=1, source_target_pairs={{0,1},{1,2},{2,3},{3,4},{4,5},{5,6},{6,7},{7,8},{8,9},{9,10},{10,1... | collective-permute-start | bytes 393224 | tf_op jit(solution)/shard_map/ppermute | solution.py:31
  27.5 0.7 copy-start.5
  31.1 15.5 %all-to-all-start.1 = ((f32[32,2,128]{2,1,0:T(2,128)}), f32[32,2,128]{2,1,0:T(2,128)S(1)}, u32[]{:S(2)}, u32[]{:S(2)}) async-start(f32[32,2,128]{2,1,0:T(2,128)} %broadcast_in_dim.8), calls=%async_computation.1 | async-start | bytes 65536 | tf_op jit(solution)/shard_map/all_to_all | solution.py:23
  46.6 0.7 copy-start.4
  49.9 17.8 %all-to-all-start.2 = ((f32[32,2,128]{2,1,0:T(2,128)}), f32[32,2,128]{2,1,0:T(2,128)S(1)}, u32[]{:S(2)}, u32[]{:S(2)}) async-start(f32[32,2,128]{2,1,0:T(2,128)} %bitcast.24), calls=%async_computation.2 | async-start | bytes 65536 | tf_op jit(solution)/shard_map/all_to_all | solution.py:20
  58.5 19.3 %collective-permute-start.2 = (f32[256,1,128]{0,2,1:T(8,128)S(1)}, f32[256,1,128]{0,2,1:T(8,128)S(1)}, u32[]{:S(2)}, u32[]{:S(2)}) collective-permute-start(f32[256,1,128]{0,2,1:T(8,128)S(1)} %get-tuple-element.7), channel_id=1, source_target_pairs={{1,0},{2,1},{3,2},{4,3},{5,4},{6,5},{7,6},{8,7},{9,8},{10,9},{11,1... | collective-permute-start | bytes 393224 | tf_op jit(solution)/shard_map/ppermute | solution.py:32
  63.6 14.2 %collective-permute-start.3 = (f32[256,1,128]{0,2,1:T(8,128)S(1)}, f32[256,1,128]{0,2,1:T(8,128)S(1)}, u32[]{:S(2)}, u32[]{:S(2)}) collective-permute-start(f32[256,1,128]{0,2,1:T(8,128)S(1)} %get-tuple-element.8), channel_id=1, source_target_pairs={{0,1},{1,2},{2,3},{3,4},{4,5},{5,6},{6,7},{7,8},{8,9},{9,10},{10,1... | collective-permute-start | bytes 393224 | tf_op jit(solution)/shard_map/ppermute | solution.py:31
  69.3 15.8 %all-to-all-start.3 = ((f32[32,2,128]{2,1,0:T(2,128)}), f32[32,2,128]{2,1,0:T(2,128)S(1)}, u32[]{:S(2)}, u32[]{:S(2)}) async-start(f32[32,2,128]{2,1,0:T(2,128)} %broadcast_in_dim.9), calls=%async_computation.3 | async-start | bytes 65536 | tf_op jit(solution)/shard_map/all_to_all | solution.py:23
  87.6 16.8 %all-to-all-start.4 = ((f32[32,2,128]{2,1,0:T(2,128)}), f32[32,2,128]{2,1,0:T(2,128)S(1)}, u32[]{:S(2)}, u32[]{:S(2)}) async-start(f32[32,2,128]{2,1,0:T(2,128)} %bitcast.35), calls=%async_computation.4 | async-start | bytes 65536 | tf_op jit(solution)/shard_map/all_to_all | solution.py:20
  95.2 19.3 %collective-permute-start.4 = (f32[256,1,128]{0,2,1:T(8,128)S(1)}, f32[256,1,128]{0,2,1:T(8,128)S(1)}, u32[]{:S(2)}, u32[]{:S(2)}) collective-permute-start(f32[256,1,128]{0,2,1:T(8,128)S(1)} %get-tuple-element.5), channel_id=1, source_target_pairs={{1,0},{2,1},{3,2},{4,3},{5,4},{6,5},{7,6},{8,7},{9,8},{10,9},{11,1... | collective-permute-start | bytes 393224 | tf_op jit(solution)/shard_map/ppermute | solution.py:32
  99.2 20.6 %collective-permute-start.5 = (f32[256,1,128]{0,2,1:T(8,128)S(1)}, f32[256,1,128]{0,2,1:T(8,128)S(1)}, u32[]{:S(2)}, u32[]{:S(2)}) collective-permute-start(f32[256,1,128]{0,2,1:T(8,128)S(1)} %get-tuple-element.6), channel_id=1, source_target_pairs={{0,1},{1,2},{2,3},{3,4},{4,5},{5,6},{6,7},{7,8},{8,9},{9,10},{10,1... | collective-permute-start | bytes 393224 | tf_op jit(solution)/shard_map/ppermute | solution.py:31
  105.9 15.8 %all-to-all-start.5 = ((f32[32,2,128]{2,1,0:T(2,128)}), f32[32,2,128]{2,1,0:T(2,128)S(1)}, u32[]{:S(2)}, u32[]{:S(2)}) async-start(f32[32,2,128]{2,1,0:T(2,128)} %broadcast_in_dim.10), calls=%async_computation.5 | async-start | bytes 65536 | tf_op jit(solution)/shard_map/all_to_all | solution.py:23

commit v2 on v1

v2 whole, which is shorter than its diff:
```python
import functools

import jax
import jax.numpy as jnp
from jax import lax
from jax.experimental import pallas as pl
from jax.experimental.pallas import tpu as pltpu
from jax.sharding import PartitionSpec as P

STEPS = 4
REACH = 8
HI = lax.Precision.HIGHEST
VMEM = 24 << 20
PLANES = 4


def dot(a, b, dims=(((1,), (0,)), ((), ()))):
    return lax.dot_general(a, b, dims, precision=HI, preferred_element_type=jnp.float32)


def forcing_of(core, obs_row, values, width_y):
    count = obs_row.shape[1]
    y = lax.broadcasted_iota(jnp.int32, (width_y, count), 0)
    hot = []
    for i in range(2):
        x = jnp.where(core == 0, i, 3 - i)
        hot.append((obs_row == x * width_y + y).astype(jnp.bfloat16))
    hot = jnp.concatenate(hot, axis=0)
    return lax.dot_general(values, hot, (((0,), (1,)), ((), ())), preferred_element_type=jnp.float32)


def forcings(step, core, obs_ref, mine_ref, other_ref, width_y):
    row = obs_ref[step : step + 1, :]
    count = row.shape[1]
    other = other_ref[step * count : (step + 1) * count, :].astype(jnp.bfloat16)
    return (
        forcing_of(core, row, mine_ref[0, step], width_y),
        forcing_of(core, row, other, width_y),
    )


def send_parts(step, lam, spread, physics_ref, modes_ref, far_ref, near_ref, kept_ref, sums_ref, width_y):
    product = spread[0] * lam[0] + spread[1] * lam[1]
    local = dot(modes_ref[...], product)
    for copy in range(PLANES):
        sums_ref[copy] = local
    w = width_y
    for m in range(2):
        moved = dot(physics_ref[step], lam[m], (((0,), (0,)), ((), ())))
        kept_ref[:, 2 * m * w : (2 * m + 2) * w] = moved
        far_ref[:, m * w : (m + 1) * w] = moved[:, :w]
        near_ref[:, m * w : (m + 1) * w] = moved[:, w:]


def prepare_kernel(width_y, core_ref, mine_ref, anomalies_ref, own_a_ref, given_ref):
    low = core_ref[0] == 0
    w = width_y
    rows = [anomalies_ref[0, :, x, :].astype(jnp.float32) for x in range(4)]
    state = rows[0].shape[0]
    for i in range(2):
        own_a_ref[:, i * w : (i + 1) * w] = jnp.where(low, rows[i], rows[3 - i])
        given_ref[:state, i * w : (i + 1) * w] = jnp.where(low, rows[3 - i], rows[i])
    count = mine_ref.shape[2]
    for t in range(STEPS):
        given_ref[state + t * count : state + (t + 1) * count, :] = mine_ref[0, t].astype(jnp.float32)


def first_kernel(step, width_y, core_ref, obs_ref, mine_ref, own_a_ref, given_ref, physics_ref, modes_ref,
                 far_ref, near_ref, kept_ref, sums_ref):
    core = core_ref[0]
    state = own_a_ref.shape[0]
    lam = forcings(step, core, obs_ref, mine_ref, given_ref.at[state:], width_y)
    spread = (own_a_ref[...], given_ref[:state])
    send_parts(step - 1, lam, spread, physics_ref, modes_ref, far_ref, near_ref, kept_ref, sums_ref, width_y)


def smooth_of(total, bands, width_y, members):
    lane = lax.broadcasted_iota(jnp.int32, (total.shape[0], width_y), 1)
    halves = []
    for i in range(2):
        here = total[:, i * width_y : (i + 1) * width_y]
        out = here
        for off in range(1, REACH + 1):
            up = jnp.where(lane >= off, pltpu.roll(here, off, 1), 0.0)
            down = jnp.where(lane < width_y - off, pltpu.roll(here, width_y - off, 1), 0.0)
            out = out + jnp.where(bands >= off, up + down, 0.0)
        halves.append(out)
    whole = jnp.concatenate(halves, axis=1)
    return whole / ((members - 1) * (2 * bands + 1)).astype(jnp.float32)


def beside(row, width_y):
    lane = lax.broadcasted_iota(jnp.int32, row.shape, 1)
    up = jnp.where(lane >= 1, pltpu.roll(row, 1, 1), 0.0)
    down = jnp.where(lane < width_y - 1, pltpu.roll(row, width_y - 1, 1), 0.0)
    return up + down


def next_lam(step, width_y, members, core_ref, obs_ref, mine_ref, own_a_ref, given_ref, modes_ref,
             bands_ref, nu_ref, sums_ref, kept_ref, far_ref, near_ref):
    w = width_y
    total = sums_ref[0] + sums_ref[1] + sums_ref[2] + sums_ref[3]
    smooth = smooth_of(total, bands_ref[...], w, members)
    lifted = dot(modes_ref[...], smooth, (((0,), (0,)), ((), ())))
    nu = nu_ref[...]
    state = own_a_ref.shape[0]
    spread = (own_a_ref[...], given_ref[:state])
    force = forcings(step, core_ref[0], obs_ref, mine_ref, given_ref.at[state:], w)
    lam = []
    for m in range(2):
        far = kept_ref[:, (2 * m) * w : (2 * m + 1) * w]
        near = kept_ref[:, (2 * m + 1) * w : (2 * m + 2) * w]
        out_far = far_ref[:, (1 - m) * w : (2 - m) * w]
        out_near = near_ref[:, (1 - m) * w : (2 - m) * w]
        v_far = far + nu * (out_far + near + beside(far, w) - 4.0 * far)
        v_near = near + nu * (far + out_near + beside(near, w) - 4.0 * near)
        lam.append(jnp.concatenate([v_far, v_near], axis=1) + spread[m] * lifted + force[m])
    return lam, spread


def step_kernel(step, width_y, members, core_ref, obs_ref, mine_ref, own_a_ref, given_ref, physics_ref,
                modes_ref, bands_ref, nu_ref, sums_ref, kept_ref, far_ref, near_ref,
                far_out, near_out, kept_out, sums_out):
    lam, spread = next_lam(step, width_y, members, core_ref, obs_ref, mine_ref, own_a_ref, given_ref,
                           modes_ref, bands_ref, nu_ref, sums_ref, kept_ref, far_ref, near_ref)
    send_parts(step - 1, lam, spread, physics_ref, modes_ref, far_out, near_out, kept_out, sums_out, width_y)


def last_kernel(step, width_y, members, core_ref, obs_ref, mine_ref, own_a_ref, given_ref,
                modes_ref, bands_ref, nu_ref, sums_ref, kept_ref, far_ref, near_ref, own_out, other_out):
    lam, _ = next_lam(step, width_y, members, core_ref, obs_ref, mine_ref, own_a_ref, given_ref,
                      modes_ref, bands_ref, nu_ref, sums_ref, kept_ref, far_ref, near_ref)
    own_out[...] = lam[0]
    other_out[...] = lam[1]


def finish_kernel(width_y, core_ref, own_ref, back_ref, out_ref):
    low = core_ref[0] == 0
    w = width_y
    mine = (own_ref[:, :w], own_ref[:, w:])
    got = (back_ref[:, :w], back_ref[:, w:])
    when_low = (mine[0], mine[1], got[1], got[0])
    when_high = (got[0], got[1], mine[1], mine[0])
    for x in range(4):
        out_ref[0, :, x, :] = jnp.where(low, when_low[x], when_high[x])


def call(kernel, args, outs, flops=400_000_000):
    return pl.pallas_call(
        kernel,
        in_specs=[pl.BlockSpec(memory_space=pltpu.SMEM)] + [pl.BlockSpec(memory_space=pltpu.VMEM)] * (len(args) - 1),
        out_specs=[pl.BlockSpec(memory_space=pltpu.VMEM)] * len(outs),
        out_shape=[jax.ShapeDtypeStruct(o, jnp.float32) for o in outs],
        cost_estimate=pl.CostEstimate(flops=flops, bytes_accessed=2_000_000, transcendentals=0),
        compiler_params=pltpu.CompilerParams(vmem_limit_bytes=VMEM),
    )(*args)


def per_device(innovations, obs_column, physics, diffusion, anomalies, modes, bands):
    members = lax.axis_size("member")
    tiles = lax.axis_size("tile")
    _, state, _, width_y = anomalies.shape
    core = (lax.axis_index("member") & 1).astype(jnp.int32)[None]
    mine = jnp.swapaxes(innovations, 2, 3)
    count = mine.shape[2]
    modes_t = modes.T
    n_modes = modes.shape[1]

    swap = [(i, i ^ 1) for i in range(members)]
    far_pairs = []
    for m in range(members):
        for t in range(tiles):
            target = (t + 1) % tiles if m % 2 else (t - 1) % tiles
            far_pairs.append((m * tiles + t, (m ^ 1) * tiles + target))
    side = 2 * PLANES
    first_groups = [[side * y + j for y in range(PLANES)] for j in range(side)]
    second_groups = [[side * y + 2 * z + c for z in range(PLANES)] for y in range(PLANES) for c in range(2)]

    half = (state, 2 * width_y)
    full = (state, 4 * width_y)
    sums_shape = (PLANES, n_modes, 2 * width_y)
    own_a, given = call(
        functools.partial(prepare_kernel, width_y),
        (core, mine, anomalies),
        [half, (state + STEPS * count, 2 * width_y)],
    )
    given = lax.ppermute(given, "member", swap)
    bands_col = bands[:, None]
    nu_col = diffusion[:, None]

    step = STEPS - 1
    sent = call(
        functools.partial(first_kernel, step, width_y),
        (core, obs_column, mine, own_a, given, physics, modes_t),
        [half, half, full, sums_shape],
    )
    for step in range(STEPS - 2, -1, -1):
        far, near, kept, sums = sent
        sums = lax.all_to_all(sums, "member", 0, 0, tiled=True, axis_index_groups=first_groups)
        far = lax.ppermute(far, ("member", "tile"), far_pairs)
        near = lax.ppermute(near, "member", swap)
        sums = jnp.broadcast_to(sums.sum(axis=0)[None], sums_shape)
        sums = lax.all_to_all(sums, "member", 0, 0, tiled=True, axis_index_groups=second_groups)
        tail = (modes_t, bands_col, nu_col, sums, kept, far, near)
        if step > 0:
            sent = call(
                functools.partial(step_kernel, step, width_y, members),
                (core, obs_column, mine, own_a, given, physics) + tail,
                [half, half, full, sums_shape],
            )
        else:
            own, other = call(
                functools.partial(last_kernel, step, width_y, members),
                (core, obs_column, mine, own_a, given) + tail,
                [half, half],
            )
    back = lax.ppermute(other, "member", swap)
    return call(functools.partial(finish_kernel, width_y), (core, own, back), [(1, *anomalies.shape[1:])])[0]


def solution(mesh):
    in_specs = (
        P("member", None, None, "tile"),
        P(None, "tile"),
        P(),
        P(),
        P("member", None, "tile", None),
        P(),
        P(),
    )
    out_specs = P("member", None, "tile", None)
    return jax.shard_map(
        per_device, mesh=mesh, in_specs=in_specs, out_specs=out_specs, check_vma=False
    )
```

time: 124 us -> 105 us (0.85)
  starting transfers between devices: 83 us -> 45.6 us
  blocking collectives: 0 us -> 36.7 us
  waiting for transfers between devices: 21.5 us -> 5.68 us
  matrix products: 9.58 us -> 0 us
  Pallas kernels: 0 us -> 9.12 us
    all_to_all x6 -> x1, starting transfers between devices: 50.9 us -> 3.41 us  [per_device(): lax.all_to_all(sums, 'member', 0, 0, tiled=True, axis_index_groups=second...]
    all_to_all x0 -> x5, blocking collectives: none -> 36.7 us  [the longest x3 22.7 us: per_device(): lax.all_to_all(sums, 'member', 0, 0, tiled=True, axis_index_groups=first_...]
    all_to_all x6 -> x1, waiting for transfers between devices: 16.2 us -> 3.01 us  [per_device(): lax.all_to_all(sums, 'member', 0, 0, tiled=True, axis_index_groups=second...]
    ppermute x6 -> x8, starting transfers between devices: 32.1 us -> 42.2 us  [the longest x3 15.9 us: per_device(): far = lax.ppermute(far, ('member', 'tile'), far_pairs)]
    dot_general x16 -> x0, matrix products: 9.58 us -> none  [the longest x3 2.47 us: summed_smooth(): mine = jnp.dot(mine, near, precision=HI) * scale]
    pallas_call x0 -> x6, Pallas kernels: none -> 9.12 us  [call(): pl.pallas_call(kernel, in_specs=[pl.BlockSpec(memory_space=pltpu.SMEM)] +...]
    unnamed x13 -> x24, local copies, waits for them, and re-layouts: 2.54 us -> 6.59 us
    ppermute x6 -> x8, waiting for transfers between devices: 5.28 us -> 2.67 us  [the longest x1 1.51 us: per_device(): given = lax.ppermute(given, 'member', swap)]
  transfers between devices with their start and end apart: 12 -> 9, of which waited for: 4 -> 3; matrix products, arithmetic and copies ran while one was open for 6% -> 1% of each run, Pallas kernels for 0% -> 0%
where the time goes in v2:
time: 105 us
  starting transfers between devices  45.6 us (43%)
  blocking collectives  36.7 us (35%)
  Pallas kernels  9.12 us (9%)
  local copies, waits for them, and re-layouts  7.46 us (7%)
  waiting for transfers between devices  5.68 us (5%)
    all_to_all x3, blocking collectives, per_device(): lax.all_to_all(sums, 'member', 0, 0, tiled=True, axis_index_groups=first_...  22.7 us
    ppermute x3, starting transfers between devices, per_device(): far = lax.ppermute(far, ('member', 'tile'), far_pairs)  15.9 us
    all_to_all x2, blocking collectives, per_device(): lax.all_to_all(sums, 'member', 0, 0, tiled=True, axis_index_groups=second...  13.9 us
    ppermute x3, starting transfers between devices, per_device(): near = lax.ppermute(near, 'member', swap)  13.7 us
    pallas_call x6, Pallas kernels, call(): pl.pallas_call(kernel, in_specs=[pl.BlockSpec(memory_space=pltpu.SMEM)] +...  9.12 us
    ppermute x1, starting transfers between devices, per_device(): given = lax.ppermute(given, 'member', swap)  8.75 us
    unnamed x24, local copies, waits for them, and re-layouts  6.59 us
    ppermute x1, starting transfers between devices, per_device(): back = lax.ppermute(other, 'member', swap)  3.92 us
  transfers between devices with their start and end apart: 9, of which 3 were waited for; matrix products, arithmetic and copies ran while one was open for 1% of the time, Pallas kernels for 0%

profile of v2, /device:TPU:1, one launch (start us, length us, event | category | flops | bytes accessed | tf_op | source)
XLA Modules:
  0.0 104.7 jit_solution(6597581958120212047)
XLA Ops:
  0.0 1.0 copy-done.1
  1.0 0.9 copy-done.9
  1.9 0.7 shard_map.73
  2.6 8.7 %collective-permute-start = (f32[512,256]{1,0:T(8,128)S(1)}, f32[512,256]{1,0:T(8,128)S(1)}, u32[]{:S(2)}, u32[]{:S(2)}) collective-permute-start(f32[512,256]{1,0:T(8,128)S(1)} %get-tuple-element.22), channel_id=1, source_target_pairs={{0,16},{16,0},{32,48},{48,32},{64,80},{80,64},{96,112},{112,96},{1... | collective-permute-start | bytes 1572872 | tf_op jit(solution)/shard_map/ppermute | solution.py:187
  11.4 1.5 %collective-permute-done.given_ref = f32[512,256]{1,0:T(8,128)S(1)} collective-permute-done((f32[512,256]{1,0:T(8,128)S(1)}, f32[512,256]{1,0:T(8,128)S(1)}, u32[]{:S(2)}, u32[]{:S(2)}) %collective-permute-start) | collective-permute-done | bytes 524320 | tf_op jit(solution)/shard_map/ppermute | solution.py:187
  12.9 1.8 %shard_map.74 = (f32[256,256]{1,0:T(8,128)}, f32[256,256]{1,0:T(8,128)S(1)}, f32[256,512]{1,0:T(8,128)S(1)}, f32[4,16,256]{2,1,0:T(8,128)S(1)}) custom-call(s32[1]{0:T(128)} %bitcast.core_ref, s32[4,64]{1,0:T(4,128)S(1)} %copy-done.8, bf16[1,4,64,256]{3,2,1,0:T(8,128)(2,1)S(1)} %bitcast.6, f32[256,256]{1,0:T(8,128)S(1)} %get-tuple-element.21.own_a_ref, ...), custom_call_target="tpu_custom_call" | custom-call | flops 400000000 | bytes 2000000 | tf_op jit(solution)/shard_map/pallas_call | solution.py:149
  14.7 3.7 %collective-permute-start.1 = (f32[256,256]{1,0:T(8,128)}, f32[256,256]{1,0:T(8,128)S(1)}, u32[]{:S(2)}, u32[]{:S(2)}) collective-permute-start(f32[256,256]{1,0:T(8,128)} %get-tuple-element.25), channel_id=1, source_target_pairs={{0,31},{1,16},{2,17},{3,18},{4,19},{5,20},{6,21},{7,22},{8,23},{9,... | collective-permute-start | bytes 786440 | tf_op jit(solution)/shard_map/ppermute | solution.py:200
  18.4 7.9 %collective-permute-start.2 = (f32[256,256]{1,0:T(8,128)S(1)}, f32[256,256]{1,0:T(8,128)S(1)}, u32[]{:S(2)}, u32[]{:S(2)}) collective-permute-start(f32[256,256]{1,0:T(8,128)S(1)} %get-tuple-element.26), channel_id=1, source_target_pairs={{0,16},{16,0},{32,48},{48,32},{64,80},{80,64},{96,112},{112,96},{1... | collective-permute-start | bytes 786440 | tf_op jit(solution)/shard_map/ppermute | solution.py:201
  26.3 8.5 %all_to_all.30 = f32[4,16,256]{2,1,0:T(8,128)S(1)} all-to-all(f32[4,16,256]{2,1,0:T(8,128)S(1)} %get-tuple-element.23), channel_id=1, replica_groups={{0,128,256,384},{16,144,272,400},{32,160,288,416},{48,176,304,432},{64,..., dimensions={0} | all-to-all | bytes 131072 | tf_op jit(solution)/shard_map/all_to_all | solution.py:199
  34.8 0.6 broadcast_in_dim.30
  35.4 3.4 %all-to-all-start.1 = ((f32[4,16,256]{2,1,0:T(8,128)}), f32[4,16,256]{2,1,0:T(8,128)S(1)}, u32[]{:S(2)}, u32[]{:S(2)}) async-start(f32[4,16,256]{2,1,0:T(8,128)} %broadcast_in_dim.30), calls=%async_computation.1 | async-start | bytes 131072 | tf_op jit(solution)/shard_map/all_to_all | solution.py:203
  38.9 0.6 copy-done.11
  39.6 0.7 copy-done.10
  40.4 3.0 %all-to-all-done.1.sums_ref = f32[4,16,256]{2,1,0:T(8,128)S(1)} async-done(((f32[4,16,256]{2,1,0:T(8,128)}), f32[4,16,256]{2,1,0:T(8,128)S(1)}, u32[]{:S(2)}, u32[]{:S(2)}) %all-to-all-start.1) | async-done | bytes 65568 | tf_op jit(solution)/shard_map/all_to_all | solution.py:203
  43.4 0.7 copy-done.4
  44.1 0.9 copy-done.5
  45.1 2.4 %shard_map.75 = (f32[256,256]{1,0:T(8,128)}, f32[256,256]{1,0:T(8,128)}, f32[256,512]{1,0:T(8,128)S(1)}, f32[4,16,256]{2,1,0:T(8,128)S(1)}) custom-call(s32[1]{0:T(128)} %bitcast.core_ref, s32[4,64]{1,0:T(4,128)S(1)} %copy-done.8, bf16[1,4,64,256]{3,2,1,0:T(8,128)(2,1)S(1)} %bitcast.7, f32[256,256]{1,0:T(8,128)S(1)} %get-tuple-element.21.own_a_ref, ...), custom_call_target="tpu_custom_call" | custom-call | flops 400000000 | bytes 2000000 | tf_op jit(solution)/shard_map/pallas_call | solution.py:149
  47.5 5.8 %collective-permute-start.3 = (f32[256,256]{1,0:T(8,128)}, f32[256,256]{1,0:T(8,128)S(1)}, u32[]{:S(2)}, u32[]{:S(2)}) collective-permute-start(f32[256,256]{1,0:T(8,128)} %get-tuple-element.29), channel_id=1, source_target_pairs={{0,31},{1,16},{2,17},{3,18},{4,19},{5,20},{6,21},{7,22},{8,23},{9,... | collective-permute-start | bytes 786440 | tf_op jit(solution)/shard_map/ppermute | solution.py:200
  53.3 1.9 %collective-permute-start.4 = (f32[256,256]{1,0:T(8,128)}, f32[256,256]{1,0:T(8,128)S(1)}, u32[]{:S(2)}, u32[]{:S(2)}) collective-permute-start(f32[256,256]{1,0:T(8,128)} %get-tuple-element.30), channel_id=1, source_target_pairs={{0,16},{16,0},{32,48},{48,32},{64,80},{80,64},{96,112},{112,96},{1... | collective-permute-start | bytes 786440 | tf_op jit(solution)/shard_map/ppermute | solution.py:201
  55.3 7.1 %all_to_all.31 = f32[4,16,256]{2,1,0:T(8,128)S(1)} all-to-all(f32[4,16,256]{2,1,0:T(8,128)S(1)} %get-tuple-element.27), channel_id=1, replica_groups={{0,128,256,384},{16,144,272,400},{32,160,288,416},{48,176,304,432},{64,..., dimensions={0} | all-to-all | bytes 131072 | tf_op jit(solution)/shard_map/all_to_all | solution.py:199
  62.4 7.0 %all_to_all.32.sums_ref = f32[4,16,256]{2,1,0:T(8,128)S(1)} all-to-all(f32[4,16,256]{2,1,0:T(8,128)S(1)} %broadcast_in_dim.31), channel_id=1, replica_groups={{0,32,64,96},{16,48,80,112},{128,160,192,224},{144,176,208,240},{256,28..., dimensions={0} | all-to-all | bytes 131072 | tf_op jit(solution)/shard_map/all_to_all | solution.py:203
  69.4 0.7 copy-done.6
  70.1 0.9 copy-done.7
  71.1 2.4 %shard_map.76 = (f32[256,256]{1,0:T(8,128)}, f32[256,256]{1,0:T(8,128)}, f32[256,512]{1,0:T(8,128)S(1)}, f32[4,16,256]{2,1,0:T(8,128)S(1)}) custom-call(s32[1]{0:T(128)} %bitcast.core_ref, s32[4,64]{1,0:T(4,128)S(1)} %copy-done.8, bf16[1,4,64,256]{3,2,1,0:T(8,128)(2,1)S(1)} %bitcast.8, f32[256,256]{1,0:T(8,128)S(1)} %get-tuple-element.21.own_a_ref, ...), custom_call_target="tpu_custom_call" | custom-call | flops 400000000 | bytes 2000000 | tf_op jit(solution)/shard_map/pallas_call | solution.py:149
  73.5 6.4 %collective-permute-start.5 = (f32[256,256]{1,0:T(8,128)}, f32[256,256]{1,0:T(8,128)S(1)}, u32[]{:S(2)}, u32[]{:S(2)}) collective-permute-start(f32[256,256]{1,0:T(8,128)} %get-tuple-element.33), channel_id=1, source_target_pairs={{0,31},{1,16},{2,17},{3,18},{4,19},{5,20},{6,21},{7,22},{8,23},{9,... | collective-permute-start | bytes 786440 | tf_op jit(solution)/shard_map/ppermute | solution.py:200
  79.9 3.9 %collective-permute-start.6 = (f32[256,256]{1,0:T(8,128)}, f32[256,256]{1,0:T(8,128)S(1)}, u32[]{:S(2)}, u32[]{:S(2)}) collective-permute-start(f32[256,256]{1,0:T(8,128)} %get-tuple-element.34), channel_id=1, source_target_pairs={{0,16},{16,0},{32,48},{48,32},{64,80},{80,64},{96,112},{112,96},{1... | collective-permute-start | bytes 786440 | tf_op jit(solution)/shard_map/ppermute | solution.py:201
  83.7 7.1 %all_to_all.33 = f32[4,16,256]{2,1,0:T(8,128)S(1)} all-to-all(f32[4,16,256]{2,1,0:T(8,128)S(1)} %get-tuple-element.31), channel_id=1, replica_groups={{0,128,256,384},{16,144,272,400},{32,160,288,416},{48,176,304,432},{64,..., dimensions={0} | all-to-all | bytes 131072 | tf_op jit(solution)/shard_map/all_to_all | solution.py:199
  90.9 7.0 %all_to_all.34.sums_ref = f32[4,16,256]{2,1,0:T(8,128)S(1)} all-to-all(f32[4,16,256]{2,1,0:T(8,128)S(1)} %broadcast_in_dim.32), channel_id=1, replica_groups={{0,32,64,96},{16,48,80,112},{128,160,192,224},{144,176,208,240},{256,28..., dimensions={0} | all-to-all | bytes 131072 | tf_op jit(solution)/shard_map/all_to_all | solution.py:203
  97.9 0.7 shard_map.77
  98.6 3.9 %collective-permute-start.7 = (f32[256,256]{1,0:T(8,128)S(1)}, f32[256,256]{1,0:T(8,128)S(1)}, u32[]{:S(2)}, u32[]{:S(2)}) collective-permute-start(f32[256,256]{1,0:T(8,128)S(1)} %get-tuple-element.36), channel_id=1, source_target_pairs={{0,16},{16,0},{32,48},{48,32},{64,80},{80,64},{96,112},{112,96},{1... | collective-permute-start | bytes 786440 | tf_op jit(solution)/shard_map/ppermute | solution.py:217
  102.5 1.1 %collective-permute-done.7.back_ref = f32[256,256]{1,0:T(8,128)S(1)} collective-permute-done((f32[256,256]{1,0:T(8,128)S(1)}, f32[256,256]{1,0:T(8,128)S(1)}, u32[]{:S(2)}, u32[]{:S(2)}) %collective-permute-start.7) | collective-permute-done | bytes 262176 | tf_op jit(solution)/shard_map/ppermute | solution.py:217
  103.6 1.1 %shard_map.78 = f32[1,256,4,128]{3,2,1,0:T(4,128)} custom-call(s32[1]{0:T(128)} %bitcast.core_ref, f32[256,256]{1,0:T(8,128)S(1)} %get-tuple-element.35.own_ref, f32[256,256]{1,0:T(8,128)S(1)} %collective-permute-done.7.back_ref), custom_call_target="tpu_custom_call" | custom-call | flops 400000000 | bytes 2000000 | tf_op jit(solution)/shard_map/pallas_call | solution.py:149
  (29 shorter events, 0.3 us)
Async XLA Ops:
  0.0 12.9 %copy-start = (f32[4,256,256]{2,1,0:T(8,128)S(1)}, f32[4,256,256]{2,1,0:T(8,128)}, u32[]{:S(2)}) copy-start(f32[4,256,256]{2,1,0:T(8,128)} %physics_ref.5) | copy-start | bytes 3145732
  0.0 1.0 copy-start.1
  1.0 0.9 copy-start.9
  1.9 11.0 %copy-start.3 = (f32[256,16]{0,1:T(8,128)S(1)}, f32[256,16]{0,1:T(8,128)}, u32[]{:S(2)}) copy-start(f32[256,16]{0,1:T(8,128)} %param.12) | copy-start | bytes 49156
  2.6 10.3 %copy-start.8 = (s32[4,64]{1,0:T(4,128)S(1)}, s32[4,64]{1,0:T(4,128)}, u32[]{:S(2)}) copy-start(s32[4,64]{1,0:T(4,128)} %obs_ref.7) | copy-start | bytes 3076
  2.6 10.3 %collective-permute-start = (f32[512,256]{1,0:T(8,128)S(1)}, f32[512,256]{1,0:T(8,128)S(1)}, u32[]{:S(2)}, u32[]{:S(2)}) collective-permute-start(f32[512,256]{1,0:T(8,128)S(1)} %get-tuple-element.22), channel_id=1, source_target_pairs={{0,16},{16,0},{32,48},{48,32},{64,80},{80,64},{96,112},{112,96},{1... | collective-permute-start | bytes 1572872 | tf_op jit(solution)/shard_map/ppermute | solution.py:187
  14.7 28.7 %collective-permute-start.1 = (f32[256,256]{1,0:T(8,128)}, f32[256,256]{1,0:T(8,128)S(1)}, u32[]{:S(2)}, u32[]{:S(2)}) collective-permute-start(f32[256,256]{1,0:T(8,128)} %get-tuple-element.25), channel_id=1, source_target_pairs={{0,31},{1,16},{2,17},{3,18},{4,19},{5,20},{6,21},{7,22},{8,23},{9,... | collective-permute-start | bytes 786440 | tf_op jit(solution)/shard_map/ppermute | solution.py:200
  18.4 25.0 %collective-permute-start.2 = (f32[256,256]{1,0:T(8,128)S(1)}, f32[256,256]{1,0:T(8,128)S(1)}, u32[]{:S(2)}, u32[]{:S(2)}) collective-permute-start(f32[256,256]{1,0:T(8,128)S(1)} %get-tuple-element.26), channel_id=1, source_target_pairs={{0,16},{16,0},{32,48},{48,32},{64,80},{80,64},{96,112},{112,96},{1... | collective-permute-start | bytes 786440 | tf_op jit(solution)/shard_map/ppermute | solution.py:201
  35.4 8.7 %copy-start.2 = (bf16[1,4,256,64]{2,3,1,0:T(8,128)(2,1)S(1)}, bf16[1,4,256,64]{2,3,1,0:T(8,128)(2,1)}, u32[]{:S(2)}) copy-start(bf16[1,4,256,64]{2,3,1,0:T(8,128)(2,1)} %param.7) | copy-start | bytes 393220
  35.4 8.0 %all-to-all-start.1 = ((f32[4,16,256]{2,1,0:T(8,128)}), f32[4,16,256]{2,1,0:T(8,128)S(1)}, u32[]{:S(2)}, u32[]{:S(2)}) async-start(f32[4,16,256]{2,1,0:T(8,128)} %broadcast_in_dim.30), calls=%async_computation.1 | async-start | bytes 131072 | tf_op jit(solution)/shard_map/all_to_all | solution.py:203
  38.9 0.7 copy-start.11
  39.6 0.7 copy-start.10
  43.4 0.7 copy-start.4
  44.1 1.0 copy-start.5
  47.5 21.9 %collective-permute-start.3 = (f32[256,256]{1,0:T(8,128)}, f32[256,256]{1,0:T(8,128)S(1)}, u32[]{:S(2)}, u32[]{:S(2)}) collective-permute-start(f32[256,256]{1,0:T(8,128)} %get-tuple-element.29), channel_id=1, source_target_pairs={{0,31},{1,16},{2,17},{3,18},{4,19},{5,20},{6,21},{7,22},{8,23},{9,... | collective-permute-start | bytes 786440 | tf_op jit(solution)/shard_map/ppermute | solution.py:200
  53.3 16.1 %collective-permute-start.4 = (f32[256,256]{1,0:T(8,128)}, f32[256,256]{1,0:T(8,128)S(1)}, u32[]{:S(2)}, u32[]{:S(2)}) collective-permute-start(f32[256,256]{1,0:T(8,128)} %get-tuple-element.30), channel_id=1, source_target_pairs={{0,16},{16,0},{32,48},{48,32},{64,80},{80,64},{96,112},{112,96},{1... | collective-permute-start | bytes 786440 | tf_op jit(solution)/shard_map/ppermute | solution.py:201
  69.4 0.7 copy-start.6
  70.1 0.9 copy-start.7
  73.5 24.4 %collective-permute-start.5 = (f32[256,256]{1,0:T(8,128)}, f32[256,256]{1,0:T(8,128)S(1)}, u32[]{:S(2)}, u32[]{:S(2)}) collective-permute-start(f32[256,256]{1,0:T(8,128)} %get-tuple-element.33), channel_id=1, source_target_pairs={{0,31},{1,16},{2,17},{3,18},{4,19},{5,20},{6,21},{7,22},{8,23},{9,... | collective-permute-start | bytes 786440 | tf_op jit(solution)/shard_map/ppermute | solution.py:200
  79.9 18.0 %collective-permute-start.6 = (f32[256,256]{1,0:T(8,128)}, f32[256,256]{1,0:T(8,128)S(1)}, u32[]{:S(2)}, u32[]{:S(2)}) collective-permute-start(f32[256,256]{1,0:T(8,128)} %get-tuple-element.34), channel_id=1, source_target_pairs={{0,16},{16,0},{32,48},{48,32},{64,80},{80,64},{96,112},{112,96},{1... | collective-permute-start | bytes 786440 | tf_op jit(solution)/shard_map/ppermute | solution.py:201
  98.6 5.1 %collective-permute-start.7 = (f32[256,256]{1,0:T(8,128)S(1)}, f32[256,256]{1,0:T(8,128)S(1)}, u32[]{:S(2)}, u32[]{:S(2)}) collective-permute-start(f32[256,256]{1,0:T(8,128)S(1)} %get-tuple-element.36), channel_id=1, source_target_pairs={{0,16},{16,0},{32,48},{48,32},{64,80},{80,64},{96,112},{112,96},{1... | collective-permute-start | bytes 786440 | tf_op jit(solution)/shard_map/ppermute | solution.py:217

commit v3 on v2

v3 whole, which is shorter than its diff:
```python
import functools

import jax
import jax.numpy as jnp
from jax import lax
from jax.experimental import pallas as pl
from jax.experimental.pallas import tpu as pltpu
from jax.sharding import PartitionSpec as P

STEPS = 4
REACH = 8
VMEM = 24 << 20
PLANES = 4


MM = (((1,), (0,)), ((), ()))
TM = (((0,), (0,)), ((), ()))


def halves(x):
    high = x.astype(jnp.bfloat16)
    return high, (x - high.astype(jnp.float32)).astype(jnp.bfloat16)


def dot(a, b, dims=MM):
    part = lambda p, q: lax.dot_general(p, q, dims, preferred_element_type=jnp.float32)
    a_high, a_low = halves(a)
    b_high, b_low = halves(b)
    return part(a_high, b_high) + (part(a_high, b_low) + part(a_low, b_high))


def forcing_of(core, obs_row, values, width_y):
    count = obs_row.shape[1]
    y = lax.broadcasted_iota(jnp.int32, (width_y, count), 0)
    hot = []
    for i in range(2):
        x = jnp.where(core == 0, i, 3 - i)
        hot.append((obs_row == x * width_y + y).astype(jnp.bfloat16))
    hot = jnp.concatenate(hot, axis=0)
    return lax.dot_general(values, hot, (((0,), (1,)), ((), ())), preferred_element_type=jnp.float32)


def forcings(step, core, obs_ref, mine_ref, other_ref, width_y):
    row = obs_ref[step : step + 1, :]
    count = row.shape[1]
    other = other_ref[step * count : (step + 1) * count, :].astype(jnp.bfloat16)
    return (
        forcing_of(core, row, mine_ref[0, step], width_y),
        forcing_of(core, row, other, width_y),
    )


def fetch(step, physics_ref, matrix, sem):
    return pltpu.make_async_copy(physics_ref.at[step], matrix, sem)


def send_parts(lam, spread, physics, modes_ref, far_ref, near_ref, sums_ref, width_y):
    product = spread[0] * lam[0] + spread[1] * lam[1]
    local = dot(modes_ref[...], product)
    for copy in range(PLANES):
        sums_ref[copy] = local
    w = width_y
    physics[0].wait()
    matrix = physics[1][...]
    for m in range(2):
        moved = dot(matrix, lam[m], TM)
        far_ref[:, m * w : (m + 1) * w] = moved[:, :w]
        near_ref[:, m * w : (m + 1) * w] = moved[:, w:]


def prepare_kernel(width_y, core_ref, mine_hbm, anomalies_hbm, own_a_ref, given_ref, mine_ref, anomalies_ref, sems):
    copies = (
        pltpu.make_async_copy(anomalies_hbm, anomalies_ref, sems.at[0]),
        pltpu.make_async_copy(mine_hbm, mine_ref, sems.at[1]),
    )
    for copy in copies:
        copy.start()
    low = core_ref[0] == 0
    w = width_y
    copies[0].wait()
    rows = [anomalies_ref[0, :, x, :].astype(jnp.float32) for x in range(4)]
    state = rows[0].shape[0]
    for i in range(2):
        own_a_ref[:, i * w : (i + 1) * w] = jnp.where(low, rows[i], rows[3 - i]).astype(jnp.bfloat16)
        given_ref[:state, i * w : (i + 1) * w] = jnp.where(low, rows[3 - i], rows[i])
    count = mine_ref.shape[2]
    copies[1].wait()
    for t in range(STEPS):
        given_ref[state + t * count : state + (t + 1) * count, :] = mine_ref[0, t].astype(jnp.float32)


def both_spreads(own_a_ref, other_a_ref):
    return own_a_ref[...].astype(jnp.float32), other_a_ref[...].astype(jnp.float32)


def first_kernel(step, width_y, core_ref, obs_ref, mine_ref, own_a_ref, given_ref, physics_ref, modes_ref,
                 far_ref, near_ref, sums_ref, other_a_ref, other_ref, matrix, sem):
    copy = fetch(step - 1, physics_ref, matrix, sem)
    copy.start()
    state = own_a_ref.shape[0]
    other_a_ref[...] = given_ref[:state, :].astype(jnp.bfloat16)
    other_ref[...] = given_ref[state:, :].astype(jnp.bfloat16)
    lam = forcings(step, core_ref[0], obs_ref, mine_ref, other_ref, width_y)
    spread = both_spreads(own_a_ref, other_a_ref)
    send_parts(lam, spread, (copy, matrix), modes_ref, far_ref, near_ref, sums_ref, width_y)


def smooth_of(total, bands, width_y, members):
    lane = lax.broadcasted_iota(jnp.int32, (total.shape[0], width_y), 1)
    halves = []
    for i in range(2):
        here = total[:, i * width_y : (i + 1) * width_y]
        out = here
        for off in range(1, REACH + 1):
            up = jnp.where(lane >= off, pltpu.roll(here, off, 1), 0.0)
            down = jnp.where(lane < width_y - off, pltpu.roll(here, width_y - off, 1), 0.0)
            out = out + jnp.where(bands >= off, up + down, 0.0)
        halves.append(out)
    whole = jnp.concatenate(halves, axis=1)
    return whole / ((members - 1) * (2 * bands + 1)).astype(jnp.float32)


def beside(row, width_y):
    lane = lax.broadcasted_iota(jnp.int32, row.shape, 1)
    up = jnp.where(lane >= 1, pltpu.roll(row, 1, 1), 0.0)
    down = jnp.where(lane < width_y - 1, pltpu.roll(row, width_y - 1, 1), 0.0)
    return up + down


def next_lam(step, width_y, members, core_ref, obs_ref, mine_ref, own_a_ref, other_a_ref, other_ref, modes_ref,
             bands_ref, nu_ref, sums_ref, far_sent, near_sent, far_ref, near_ref):
    w = width_y
    total = sums_ref[0] + sums_ref[1] + sums_ref[2] + sums_ref[3]
    smooth = smooth_of(total, bands_ref[...], w, members)
    lifted = dot(modes_ref[...], smooth, TM)
    nu = nu_ref[...]
    spread = both_spreads(own_a_ref, other_a_ref)
    force = forcings(step, core_ref[0], obs_ref, mine_ref, other_ref, w)
    lam = []
    for m in range(2):
        far = far_sent[:, m * w : (m + 1) * w]
        near = near_sent[:, m * w : (m + 1) * w]
        out_far = far_ref[:, (1 - m) * w : (2 - m) * w]
        out_near = near_ref[:, (1 - m) * w : (2 - m) * w]
        v_far = far + nu * (out_far + near + beside(far, w) - 4.0 * far)
        v_near = near + nu * (far + out_near + beside(near, w) - 4.0 * near)
        lam.append(jnp.concatenate([v_far, v_near], axis=1) + spread[m] * lifted + force[m])
    return lam, spread


def step_kernel(step, width_y, members, core_ref, obs_ref, mine_ref, own_a_ref, other_a_ref, other_ref, physics_ref,
                modes_ref, bands_ref, nu_ref, sums_ref, far_sent, near_sent, far_ref, near_ref,
                far_out, near_out, sums_out, matrix, sem):
    copy = fetch(step - 1, physics_ref, matrix, sem)
    copy.start()
    lam, spread = next_lam(step, width_y, members, core_ref, obs_ref, mine_ref, own_a_ref, other_a_ref, other_ref,
                           modes_ref, bands_ref, nu_ref, sums_ref, far_sent, near_sent, far_ref, near_ref)
    send_parts(lam, spread, (copy, matrix), modes_ref, far_out, near_out, sums_out, width_y)


def last_kernel(step, width_y, members, core_ref, obs_ref, mine_ref, own_a_ref, other_a_ref, other_ref,
                modes_ref, bands_ref, nu_ref, sums_ref, far_sent, near_sent, far_ref, near_ref, own_out, other_out):
    lam, _ = next_lam(step, width_y, members, core_ref, obs_ref, mine_ref, own_a_ref, other_a_ref, other_ref,
                      modes_ref, bands_ref, nu_ref, sums_ref, far_sent, near_sent, far_ref, near_ref)
    own_out[...] = lam[0]
    other_out[...] = lam[1]


def finish_kernel(width_y, core_ref, own_ref, back_ref, out_ref):
    low = core_ref[0] == 0
    w = width_y
    mine = (own_ref[:, :w], own_ref[:, w:])
    got = (back_ref[:, :w], back_ref[:, w:])
    when_low = (mine[0], mine[1], got[1], got[0])
    when_high = (got[0], got[1], mine[1], mine[0])
    for x in range(4):
        out_ref[0, :, x, :] = jnp.where(low, when_low[x], when_high[x])


def call(kernel, name, args, outs, types=(), hbm=(), scratch=(), flops=400_000_000):
    spaces = [pltpu.SMEM] + [pltpu.HBM if i in hbm else pltpu.VMEM for i in range(1, len(args))]
    types = tuple(types) or (jnp.float32,) * len(outs)
    return pl.pallas_call(
        kernel,
        in_specs=[pl.BlockSpec(memory_space=space) for space in spaces],
        out_specs=[pl.BlockSpec(memory_space=pltpu.VMEM)] * len(outs),
        out_shape=[jax.ShapeDtypeStruct(o, t) for o, t in zip(outs, types)],
        scratch_shapes=list(scratch),
        cost_estimate=pl.CostEstimate(flops=flops, bytes_accessed=2_000_000, transcendentals=0),
        compiler_params=pltpu.CompilerParams(vmem_limit_bytes=None if name == "prepare" else VMEM),
    )(*args)


def per_device(innovations, obs_column, physics, diffusion, anomalies, modes, bands):
    members = lax.axis_size("member")
    tiles = lax.axis_size("tile")
    _, state, _, width_y = anomalies.shape
    core = (lax.axis_index("member") & 1).astype(jnp.int32)[None]
    mine = jnp.swapaxes(innovations, 2, 3)
    count = mine.shape[2]
    modes_t = modes.T
    n_modes = modes.shape[1]

    swap = [(i, i ^ 1) for i in range(members)]
    far_pairs = []
    for m in range(members):
        for t in range(tiles):
            target = (t + 1) % tiles if m % 2 else (t - 1) % tiles
            far_pairs.append((m * tiles + t, (m ^ 1) * tiles + target))
    side = 2 * PLANES
    first_groups = [[side * y + j for y in range(PLANES)] for j in range(side)]
    second_groups = [[side * y + 2 * z + c for z in range(PLANES)] for y in range(PLANES) for c in range(2)]

    half = (state, 2 * width_y)
    sums_shape = (PLANES, n_modes, 2 * width_y)
    own_a, given = call(
        functools.partial(prepare_kernel, width_y),
        "prepare",
        (core, mine, anomalies),
        [half, (state + STEPS * count, 2 * width_y)],
        types=(jnp.bfloat16, jnp.float32),
        hbm=(1, 2),
        scratch=(
            pltpu.VMEM(mine.shape, mine.dtype),
            pltpu.VMEM(anomalies.shape, anomalies.dtype),
            pltpu.SemaphoreType.DMA((2,)),
        ),
    )
    matrix = (pltpu.VMEM((state, state), jnp.float32), pltpu.SemaphoreType.DMA)
    given = lax.ppermute(given, "member", swap)
    bands_col = bands[:, None]
    nu_col = diffusion[:, None]

    step = STEPS - 1
    *sent, other_a, other_innov = call(
        functools.partial(first_kernel, step, width_y),
        "first",
        (core, obs_column, mine, own_a, given, physics, modes_t),
        [half, half, sums_shape, half, (STEPS * count, state)],
        types=(jnp.float32,) * 3 + (jnp.bfloat16,) * 2,
        hbm=(5,),
        scratch=matrix,
    )
    known = (core, obs_column, mine, own_a, other_a, other_innov)
    for step in range(STEPS - 2, -1, -1):
        far_sent, near_sent, sums = sent
        sums = lax.all_to_all(sums, "member", 0, 0, tiled=True, axis_index_groups=first_groups)
        far = lax.ppermute(far_sent, ("member", "tile"), far_pairs)
        near = lax.ppermute(near_sent, "member", swap)
        sums = jnp.broadcast_to(sums.sum(axis=0)[None], sums_shape)
        sums = lax.all_to_all(sums, "member", 0, 0, tiled=True, axis_index_groups=second_groups)
        tail = (modes_t, bands_col, nu_col, sums, far_sent, near_sent, far, near)
        if step > 0:
            sent = call(
                functools.partial(step_kernel, step, width_y, members),
                f"step{step}",
                known + (physics,) + tail,
                [half, half, sums_shape],
                hbm=(6,),
                scratch=matrix,
            )
        else:
            own, other = call(
                functools.partial(last_kernel, step, width_y, members),
                "last",
                known + tail,
                [half, half],
            )
    back = lax.ppermute(other, "member", swap)
    return call(functools.partial(finish_kernel, width_y), "finish", (core, own, back), [(1, *anomalies.shape[1:])])[0]


def solution(mesh):
    in_specs = (
        P("member", None, None, "tile"),
        P(None, "tile"),
        P(),
        P(),
        P("member", None, "tile", None),
        P(),
        P(),
    )
    out_specs = P("member", None, "tile", None)
    return jax.shard_map(
        per_device, mesh=mesh, in_specs=in_specs, out_specs=out_specs, check_vma=False
    )
```

time: 105 us -> 100 us (0.952)
  local copies, waits for them, and re-layouts: 7.46 us -> 3.11 us
  Pallas kernels: 9.12 us -> 7.98 us
    unnamed x24 -> x16, local copies, waits for them, and re-layouts: 6.59 us -> 2.25 us
    pallas_call x6, Pallas kernels: 9.12 us -> 7.98 us  [call(): pl.pallas_call(kernel, in_specs=[pl.BlockSpec(memory_space=space) for spa...]
where the time goes in v3:
time: 100 us; the launch traced here: 99.5 us
  starting transfers between devices  45.7 us (46%)
  blocking collectives  36.7 us (37%)
  Pallas kernels  7.98 us (8%)
  waiting for transfers between devices  5.89 us (6%)
  local copies, waits for them, and re-layouts  3.11 us (3%)
    all_to_all x3, blocking collectives, per_device(): lax.all_to_all(sums, 'member', 0, 0, tiled=True, axis_index_groups=first_...  22.7 us
    ppermute x3, starting transfers between devices, per_device(): far = lax.ppermute(far_sent, ('member', 'tile'), far_pairs)  15.9 us
    all_to_all x2, blocking collectives, per_device(): lax.all_to_all(sums, 'member', 0, 0, tiled=True, axis_index_groups=second...  13.9 us
    ppermute x3, starting transfers between devices, per_device(): near = lax.ppermute(near_sent, 'member', swap)  13.7 us
    ppermute x1, starting transfers between devices, per_device(): given = lax.ppermute(given, 'member', swap)  8.74 us
    pallas_call x6, Pallas kernels, call(): pl.pallas_call(kernel, in_specs=[pl.BlockSpec(memory_space=space) for spa...  7.98 us
    ppermute x1, starting transfers between devices, per_device(): back = lax.ppermute(other, 'member', swap)  3.92 us
    all_to_all x1, starting transfers between devices, per_device(): lax.all_to_all(sums, 'member', 0, 0, tiled=True, axis_index_groups=second...  3.42 us
  transfers between devices with their start and end apart: 9, of which 3 were waited for; matrix products, arithmetic and copies ran while one was open for 1% of the time, Pallas kernels for 0%

profile of v3, /device:TPU:1, one launch (start us, length us, event | category | flops | bytes accessed | tf_op | source)
XLA Modules:
  0.0 99.5 jit_solution(2398204097762009116)
XLA Ops:
  0.0 2.7 %shard_map.73 = (bf16[256,256]{1,0:T(8,128)(2,1)}, f32[512,256]{1,0:T(8,128)}) custom-call(s32[1]{0:T(128)} %bitcast.core_ref, bf16[1,4,64,256]{3,2,1,0:T(8,128)(2,1)} %bitcast.5, bf16[1,256,4,128]{3,2,1,0:T(4,128)(2,1)} %anomalies_hbm.1), custom_call_target="tpu_custom_call" | custom-call | flops 400000000 | bytes 2000000 | tf_op jit(solution)/shard_map/pallas_call | solution.py:183
  2.7 0.0 copy-start.5
  2.7 8.7 %collective-permute-start = (f32[512,256]{1,0:T(8,128)}, f32[512,256]{1,0:T(8,128)S(1)}, u32[]{:S(2)}, u32[]{:S(2)}) collective-permute-start(f32[512,256]{1,0:T(8,128)} %get-tuple-element.21), channel_id=1, source_target_pairs={{0,16},{16,0},{32,48},{48,32},{64,80},{80,64},{96,112},{112,96},{1... | collective-permute-start | bytes 1572872 | tf_op jit(solution)/shard_map/ppermute | solution.py:230
  11.4 1.7 %collective-permute-done.given_ref = f32[512,256]{1,0:T(8,128)S(1)} collective-permute-done((f32[512,256]{1,0:T(8,128)}, f32[512,256]{1,0:T(8,128)S(1)}, u32[]{:S(2)}, u32[]{:S(2)}) %collective-permute-start) | collective-permute-done | bytes 524320 | tf_op jit(solution)/shard_map/ppermute | solution.py:230
  13.2 0.9 copy-done.2
  14.1 0.9 shard_map.74
  15.0 3.7 %collective-permute-start.1 = (f32[256,256]{1,0:T(8,128)S(1)}, f32[256,256]{1,0:T(8,128)S(1)}, u32[]{:S(2)}, u32[]{:S(2)}) collective-permute-start(f32[256,256]{1,0:T(8,128)S(1)} %get-tuple-element.25.far_sent), channel_id=1, source_target_pairs={{0,31},{1,16},{2,17},{3,18},{4,19},{5,20},{6,21},{7,22},{8,23},{9,... | collective-permute-start | bytes 786440 | tf_op jit(solution)/shard_map/ppermute | solution.py:248
  18.8 7.9 %collective-permute-start.2 = (f32[256,256]{1,0:T(8,128)S(1)}, f32[256,256]{1,0:T(8,128)S(1)}, u32[]{:S(2)}, u32[]{:S(2)}) collective-permute-start(f32[256,256]{1,0:T(8,128)S(1)} %get-tuple-element.26.near_sent), channel_id=1, source_target_pairs={{0,16},{16,0},{32,48},{48,32},{64,80},{80,64},{96,112},{112,96},{1... | collective-permute-start | bytes 786440 | tf_op jit(solution)/shard_map/ppermute | solution.py:249
  26.7 8.5 %all_to_all.30 = f32[4,16,256]{2,1,0:T(8,128)S(1)} all-to-all(f32[4,16,256]{2,1,0:T(8,128)S(1)} %get-tuple-element.24), channel_id=1, replica_groups={{0,128,256,384},{16,144,272,400},{32,160,288,416},{48,176,304,432},{64,..., dimensions={0} | all-to-all | bytes 131072 | tf_op jit(solution)/shard_map/all_to_all | solution.py:247
  35.1 0.6 broadcast_in_dim.30
  35.8 3.4 %all-to-all-start.1 = ((f32[4,16,256]{2,1,0:T(8,128)}), f32[4,16,256]{2,1,0:T(8,128)S(1)}, u32[]{:S(2)}, u32[]{:S(2)}) async-start(f32[4,16,256]{2,1,0:T(8,128)} %broadcast_in_dim.30), calls=%async_computation.1 | async-start | bytes 131072 | tf_op jit(solution)/shard_map/all_to_all | solution.py:251
  39.2 0.0 copy-start.7
  39.2 0.6 copy-done.7
  39.9 0.1 copy.15.bands_ref
  39.9 0.7 copy-done.6
  40.6 0.1 copy.16.nu_ref
  40.8 3.0 %all-to-all-done.1.sums_ref = f32[4,16,256]{2,1,0:T(8,128)S(1)} async-done(((f32[4,16,256]{2,1,0:T(8,128)}), f32[4,16,256]{2,1,0:T(8,128)S(1)}, u32[]{:S(2)}, u32[]{:S(2)}) %all-to-all-start.1) | async-done | bytes 65568 | tf_op jit(solution)/shard_map/all_to_all | solution.py:251
  43.8 0.0 collective-permute-done.1.far_ref
  43.8 1.3 %shard_map.75 = (f32[256,256]{1,0:T(8,128)S(1)}, f32[256,256]{1,0:T(8,128)S(1)}, f32[4,16,256]{2,1,0:T(8,128)S(1)}) custom-call(s32[1]{0:T(128)} %bitcast.core_ref, s32[4,64]{1,0:T(4,128)S(1)} %copy-done.5, bf16[1,4,64,256]{3,2,1,0:T(8,128)(2,1)S(1)} %bitcast.7, bf16[256,256]{1,0:T(8,128)(2,1)S(1)} %copy-done.3, ...), custom_call_target="tpu_custom_call" | custom-call | flops 400000000 | bytes 2000000 | tf_op jit(solution)/shard_map/pallas_call | solution.py:183
  45.1 5.8 %collective-permute-start.3 = (f32[256,256]{1,0:T(8,128)S(1)}, f32[256,256]{1,0:T(8,128)S(1)}, u32[]{:S(2)}, u32[]{:S(2)}) collective-permute-start(f32[256,256]{1,0:T(8,128)S(1)} %get-tuple-element.28.far_sent), channel_id=1, source_target_pairs={{0,31},{1,16},{2,17},{3,18},{4,19},{5,20},{6,21},{7,22},{8,23},{9,... | collective-permute-start | bytes 786440 | tf_op jit(solution)/shard_map/ppermute | solution.py:248
  50.9 1.9 %collective-permute-start.4 = (f32[256,256]{1,0:T(8,128)S(1)}, f32[256,256]{1,0:T(8,128)S(1)}, u32[]{:S(2)}, u32[]{:S(2)}) collective-permute-start(f32[256,256]{1,0:T(8,128)S(1)} %get-tuple-element.29.near_sent), channel_id=1, source_target_pairs={{0,16},{16,0},{32,48},{48,32},{64,80},{80,64},{96,112},{112,96},{1... | collective-permute-start | bytes 786440 | tf_op jit(solution)/shard_map/ppermute | solution.py:249
  52.8 7.1 %all_to_all.31 = f32[4,16,256]{2,1,0:T(8,128)S(1)} all-to-all(f32[4,16,256]{2,1,0:T(8,128)S(1)} %get-tuple-element.27), channel_id=1, replica_groups={{0,128,256,384},{16,144,272,400},{32,160,288,416},{48,176,304,432},{64,..., dimensions={0} | all-to-all | bytes 131072 | tf_op jit(solution)/shard_map/all_to_all | solution.py:247
  60.0 7.0 %all_to_all.32.sums_ref = f32[4,16,256]{2,1,0:T(8,128)S(1)} all-to-all(f32[4,16,256]{2,1,0:T(8,128)S(1)} %broadcast_in_dim.31), channel_id=1, replica_groups={{0,32,64,96},{16,48,80,112},{128,160,192,224},{144,176,208,240},{256,28..., dimensions={0} | all-to-all | bytes 131072 | tf_op jit(solution)/shard_map/all_to_all | solution.py:251
  67.0 1.3 %shard_map.76 = (f32[256,256]{1,0:T(8,128)S(1)}, f32[256,256]{1,0:T(8,128)S(1)}, f32[4,16,256]{2,1,0:T(8,128)S(1)}) custom-call(s32[1]{0:T(128)} %bitcast.core_ref, s32[4,64]{1,0:T(4,128)S(1)} %copy-done.5, bf16[1,4,64,256]{3,2,1,0:T(8,128)(2,1)S(1)} %bitcast.8, bf16[256,256]{1,0:T(8,128)(2,1)S(1)} %copy-done.3, ...), custom_call_target="tpu_custom_call" | custom-call | flops 400000000 | bytes 2000000 | tf_op jit(solution)/shard_map/pallas_call | solution.py:183
  68.3 6.4 %collective-permute-start.5 = (f32[256,256]{1,0:T(8,128)S(1)}, f32[256,256]{1,0:T(8,128)S(1)}, u32[]{:S(2)}, u32[]{:S(2)}) collective-permute-start(f32[256,256]{1,0:T(8,128)S(1)} %get-tuple-element.31.far_sent), channel_id=1, source_target_pairs={{0,31},{1,16},{2,17},{3,18},{4,19},{5,20},{6,21},{7,22},{8,23},{9,... | collective-permute-start | bytes 786440 | tf_op jit(solution)/shard_map/ppermute | solution.py:248
  74.7 3.9 %collective-permute-start.6 = (f32[256,256]{1,0:T(8,128)S(1)}, f32[256,256]{1,0:T(8,128)S(1)}, u32[]{:S(2)}, u32[]{:S(2)}) collective-permute-start(f32[256,256]{1,0:T(8,128)S(1)} %get-tuple-element.32.near_sent), channel_id=1, source_target_pairs={{0,16},{16,0},{32,48},{48,32},{64,80},{80,64},{96,112},{112,96},{1... | collective-permute-start | bytes 786440 | tf_op jit(solution)/shard_map/ppermute | solution.py:249
  78.5 7.1 %all_to_all.33 = f32[4,16,256]{2,1,0:T(8,128)S(1)} all-to-all(f32[4,16,256]{2,1,0:T(8,128)S(1)} %get-tuple-element.30), channel_id=1, replica_groups={{0,128,256,384},{16,144,272,400},{32,160,288,416},{48,176,304,432},{64,..., dimensions={0} | all-to-all | bytes 131072 | tf_op jit(solution)/shard_map/all_to_all | solution.py:247
  85.7 7.0 %all_to_all.34.sums_ref = f32[4,16,256]{2,1,0:T(8,128)S(1)} all-to-all(f32[4,16,256]{2,1,0:T(8,128)S(1)} %broadcast_in_dim.32), channel_id=1, replica_groups={{0,32,64,96},{16,48,80,112},{128,160,192,224},{144,176,208,240},{256,28..., dimensions={0} | all-to-all | bytes 131072 | tf_op jit(solution)/shard_map/all_to_all | solution.py:251
  92.7 0.7 shard_map.77
  93.4 3.9 %collective-permute-start.7 = (f32[256,256]{1,0:T(8,128)S(1)}, f32[256,256]{1,0:T(8,128)S(1)}, u32[]{:S(2)}, u32[]{:S(2)}) collective-permute-start(f32[256,256]{1,0:T(8,128)S(1)} %get-tuple-element.34), channel_id=1, source_target_pairs={{0,16},{16,0},{32,48},{48,32},{64,80},{80,64},{96,112},{112,96},{1... | collective-permute-start | bytes 786440 | tf_op jit(solution)/shard_map/ppermute | solution.py:269
  97.3 1.1 %collective-permute-done.7.back_ref = f32[256,256]{1,0:T(8,128)S(1)} collective-permute-done((f32[256,256]{1,0:T(8,128)S(1)}, f32[256,256]{1,0:T(8,128)S(1)}, u32[]{:S(2)}, u32[]{:S(2)}) %collective-permute-start.7) | collective-permute-done | bytes 262176 | tf_op jit(solution)/shard_map/ppermute | solution.py:269
  98.5 1.1 %shard_map.78 = f32[1,256,4,128]{3,2,1,0:T(4,128)} custom-call(s32[1]{0:T(128)} %bitcast.core_ref, f32[256,256]{1,0:T(8,128)S(1)} %get-tuple-element.33.own_ref, f32[256,256]{1,0:T(8,128)S(1)} %collective-permute-done.7.back_ref), custom_call_target="tpu_custom_call" | custom-call | flops 400000000 | bytes 2000000 | tf_op jit(solution)/shard_map/pallas_call | solution.py:183
  (21 shorter events, 0.1 us)
Async XLA Ops:
  0.0 13.2 %copy-start = (f32[4,256,256]{2,1,0:T(8,128)S(1)}, f32[4,256,256]{2,1,0:T(8,128)}, u32[]{:S(2)}) copy-start(f32[4,256,256]{2,1,0:T(8,128)} %physics_ref.5) | copy-start | bytes 3145732
  0.0 13.2 %copy-start.1 = (bf16[1,4,256,64]{2,3,1,0:T(8,128)(2,1)S(1)}, bf16[1,4,256,64]{2,3,1,0:T(8,128)(2,1)}, u32[]{:S(2)}) copy-start(bf16[1,4,256,64]{2,3,1,0:T(8,128)(2,1)} %param.7) | copy-start | bytes 393220
  0.0 13.2 %copy-start.4 = (f32[256,16]{0,1:T(8,128)S(1)}, f32[256,16]{0,1:T(8,128)}, u32[]{:S(2)}) copy-start(f32[256,16]{0,1:T(8,128)} %param.12) | copy-start | bytes 49156
  2.7 10.5 %copy-start.5 = (s32[4,64]{1,0:T(4,128)S(1)}, s32[4,64]{1,0:T(4,128)}, u32[]{:S(2)}) copy-start(s32[4,64]{1,0:T(4,128)} %obs_ref.7) | copy-start | bytes 3076
  2.7 10.5 %collective-permute-start = (f32[512,256]{1,0:T(8,128)}, f32[512,256]{1,0:T(8,128)S(1)}, u32[]{:S(2)}, u32[]{:S(2)}) collective-permute-start(f32[512,256]{1,0:T(8,128)} %get-tuple-element.21), channel_id=1, source_target_pairs={{0,16},{16,0},{32,48},{48,32},{64,80},{80,64},{96,112},{112,96},{1... | collective-permute-start | bytes 1572872 | tf_op jit(solution)/shard_map/ppermute | solution.py:230
  13.2 0.9 copy-start.2
  15.0 28.7 %collective-permute-start.1 = (f32[256,256]{1,0:T(8,128)S(1)}, f32[256,256]{1,0:T(8,128)S(1)}, u32[]{:S(2)}, u32[]{:S(2)}) collective-permute-start(f32[256,256]{1,0:T(8,128)S(1)} %get-tuple-element.25.far_sent), channel_id=1, source_target_pairs={{0,31},{1,16},{2,17},{3,18},{4,19},{5,20},{6,21},{7,22},{8,23},{9,... | collective-permute-start | bytes 786440 | tf_op jit(solution)/shard_map/ppermute | solution.py:248
  18.8 25.0 %collective-permute-start.2 = (f32[256,256]{1,0:T(8,128)S(1)}, f32[256,256]{1,0:T(8,128)S(1)}, u32[]{:S(2)}, u32[]{:S(2)}) collective-permute-start(f32[256,256]{1,0:T(8,128)S(1)} %get-tuple-element.26.near_sent), channel_id=1, source_target_pairs={{0,16},{16,0},{32,48},{48,32},{64,80},{80,64},{96,112},{112,96},{1... | collective-permute-start | bytes 786440 | tf_op jit(solution)/shard_map/ppermute | solution.py:249
  35.8 8.0 %copy-start.3 = (bf16[256,256]{1,0:T(8,128)(2,1)S(1)}, bf16[256,256]{1,0:T(8,128)(2,1)}, u32[]{:S(2)}) copy-start(bf16[256,256]{1,0:T(8,128)(2,1)} %get-tuple-element.20.own_a_ref) | copy-start | bytes 393220
  35.8 8.0 %all-to-all-start.1 = ((f32[4,16,256]{2,1,0:T(8,128)}), f32[4,16,256]{2,1,0:T(8,128)S(1)}, u32[]{:S(2)}, u32[]{:S(2)}) async-start(f32[4,16,256]{2,1,0:T(8,128)} %broadcast_in_dim.30), calls=%async_computation.1 | async-start | bytes 131072 | tf_op jit(solution)/shard_map/all_to_all | solution.py:251
  39.2 0.7 copy-start.7
  39.9 0.7 copy-start.6
  45.1 21.9 %collective-permute-start.3 = (f32[256,256]{1,0:T(8,128)S(1)}, f32[256,256]{1,0:T(8,128)S(1)}, u32[]{:S(2)}, u32[]{:S(2)}) collective-permute-start(f32[256,256]{1,0:T(8,128)S(1)} %get-tuple-element.28.far_sent), channel_id=1, source_target_pairs={{0,31},{1,16},{2,17},{3,18},{4,19},{5,20},{6,21},{7,22},{8,23},{9,... | collective-permute-start | bytes 786440 | tf_op jit(solution)/shard_map/ppermute | solution.py:248
  50.9 16.1 %collective-permute-start.4 = (f32[256,256]{1,0:T(8,128)S(1)}, f32[256,256]{1,0:T(8,128)S(1)}, u32[]{:S(2)}, u32[]{:S(2)}) collective-permute-start(f32[256,256]{1,0:T(8,128)S(1)} %get-tuple-element.29.near_sent), channel_id=1, source_target_pairs={{0,16},{16,0},{32,48},{48,32},{64,80},{80,64},{96,112},{112,96},{1... | collective-permute-start | bytes 786440 | tf_op jit(solution)/shard_map/ppermute | solution.py:249
  68.3 24.4 %collective-permute-start.5 = (f32[256,256]{1,0:T(8,128)S(1)}, f32[256,256]{1,0:T(8,128)S(1)}, u32[]{:S(2)}, u32[]{:S(2)}) collective-permute-start(f32[256,256]{1,0:T(8,128)S(1)} %get-tuple-element.31.far_sent), channel_id=1, source_target_pairs={{0,31},{1,16},{2,17},{3,18},{4,19},{5,20},{6,21},{7,22},{8,23},{9,... | collective-permute-start | bytes 786440 | tf_op jit(solution)/shard_map/ppermute | solution.py:248
  74.7 18.0 %collective-permute-start.6 = (f32[256,256]{1,0:T(8,128)S(1)}, f32[256,256]{1,0:T(8,128)S(1)}, u32[]{:S(2)}, u32[]{:S(2)}) collective-permute-start(f32[256,256]{1,0:T(8,128)S(1)} %get-tuple-element.32.near_sent), channel_id=1, source_target_pairs={{0,16},{16,0},{32,48},{48,32},{64,80},{80,64},{96,112},{112,96},{1... | collective-permute-start | bytes 786440 | tf_op jit(solution)/shard_map/ppermute | solution.py:249
  93.4 5.1 %collective-permute-start.7 = (f32[256,256]{1,0:T(8,128)S(1)}, f32[256,256]{1,0:T(8,128)S(1)}, u32[]{:S(2)}, u32[]{:S(2)}) collective-permute-start(f32[256,256]{1,0:T(8,128)S(1)} %get-tuple-element.34), channel_id=1, source_target_pairs={{0,16},{16,0},{32,48},{48,32},{64,80},{80,64},{96,112},{112,96},{1... | collective-permute-start | bytes 786440 | tf_op jit(solution)/shard_map/ppermute | solution.py:269

commit v4 on v3

v4 whole, which is shorter than its diff:
```python
import functools

import jax
import jax.numpy as jnp
from jax import lax
from jax.experimental import pallas as pl
from jax.experimental.pallas import tpu as pltpu
from jax.sharding import PartitionSpec as P

STEPS = 4
REACH = 8
VMEM = 24 << 20
PLANES = 4


MM = (((1,), (0,)), ((), ()))
TM = (((0,), (0,)), ((), ()))


def halves(x):
    high = x.astype(jnp.bfloat16)
    return high, (x - high.astype(jnp.float32)).astype(jnp.bfloat16)


def dot(a, b, dims=MM):
    part = lambda p, q: lax.dot_general(p, q, dims, preferred_element_type=jnp.float32)
    a_high, a_low = halves(a)
    b_high, b_low = halves(b)
    return part(a_high, b_high) + (part(a_high, b_low) + part(a_low, b_high))


def hot_rows(core, obs_row, sides, width_y):
    count = obs_row.shape[1]
    y = lax.broadcasted_iota(jnp.int32, (width_y, count), 0)
    hot = []
    for side in sides:
        x = jnp.where(core == 0, side, 3 - side)
        hot.append((obs_row == x * width_y + y).astype(jnp.bfloat16))
    return jnp.concatenate(hot, axis=0) if len(hot) > 1 else hot[0]


def placed(values, hot):
    return lax.dot_general(values, hot, (((0,), (1,)), ((), ())), preferred_element_type=jnp.float32)


def send_parts(lam, spread, physics, modes_ref, far_ref, near_ref, sums_ref, width_y):
    product = spread[0] * lam[0] + spread[1] * lam[1]
    local = dot(modes_ref[...], product)
    for copy in range(PLANES):
        sums_ref[copy] = local
    w = width_y
    matrix = physics[...]
    for m in range(2):
        moved = dot(matrix, lam[m], TM)
        far_ref[:, m * w : (m + 1) * w] = moved[:, :w]
        near_ref[:, m * w : (m + 1) * w] = moved[:, w:]


def prepare_kernel(width_y, core_ref, obs_ref, mine_hbm, anomalies_hbm, modes_ref, late_ref, sums_ref,
                   mine_ref, anomalies_ref, sems):
    copies = (
        pltpu.make_async_copy(mine_hbm.at[0, STEPS - 1], mine_ref, sems.at[0]),
        pltpu.make_async_copy(anomalies_hbm, anomalies_ref, sems.at[1]),
    )
    for copy in copies:
        copy.start()
    w = width_y
    order = (0, 1, 3, 2)
    count = obs_ref.shape[1]
    obs_row = obs_ref[STEPS - 1 : STEPS, :]
    y = lax.broadcasted_iota(jnp.int32, (w, count), 0)
    hot = jnp.concatenate([(obs_row == x * w + y).astype(jnp.bfloat16) for x in order], axis=0)
    copies[0].wait()
    values = mine_ref[...]
    late_ref[...] = values.astype(jnp.float32)
    lam = placed(values, hot)
    copies[1].wait()
    spread = jnp.concatenate([anomalies_ref[0, :, x, :].astype(jnp.float32) for x in order], axis=1)
    local = dot(modes_ref[...], spread * lam)
    for copy in range(PLANES):
        sums_ref[copy] = local


def divide_kernel(width_y, core_ref, mine_ref, anomalies_ref, own_a_ref, rest_ref):
    low = core_ref[0] == 0
    w = width_y
    rows = [anomalies_ref[0, :, x, :].astype(jnp.float32) for x in range(4)]
    state = rows[0].shape[0]
    count = mine_ref.shape[2]
    for i in range(2):
        own_a_ref[:, i * w : (i + 1) * w] = jnp.where(low, rows[i], rows[3 - i]).astype(jnp.bfloat16)
        rest_ref[:state, i * w : (i + 1) * w] = jnp.where(low, rows[3 - i], rows[i])
    for t in range(STEPS - 1):
        rest_ref[state + t * count : state + (t + 1) * count, :] = mine_ref[0, t].astype(jnp.float32)


def pass_on_kernel(core_ref, obs_ref, late_ref, other_ref, far_ref):
    count = late_ref.shape[0]
    far_ref[:count, :] = late_ref[...]
    far_ref[count : 2 * count, :] = other_ref[...]
    far_ref[2 * count :, :] = jnp.zeros((far_ref.shape[0] - 2 * count, far_ref.shape[1]), jnp.float32)
    far_ref[2 * count : 2 * count + 1, :count] = obs_ref[STEPS - 1 : STEPS, :].astype(jnp.float32)


def regroup_kernel(core_ref, sums_ref, out_ref):
    total = sums_ref[0] + sums_ref[1] + sums_ref[2] + sums_ref[3]
    half = total.shape[1] // 2
    for j in range(2 * PLANES):
        out_ref[j] = total[:, (j % 2) * half : (j % 2 + 1) * half]


def both_spreads(own_a_ref, other_a_ref):
    return own_a_ref[...].astype(jnp.float32), other_a_ref[...].astype(jnp.float32)


def smooth_of(total, bands, width_y, members):
    lane = lax.broadcasted_iota(jnp.int32, (total.shape[0], width_y), 1)
    halves = []
    for i in range(2):
        here = total[:, i * width_y : (i + 1) * width_y]
        out = here
        for off in range(1, REACH + 1):
            up = jnp.where(lane >= off, pltpu.roll(here, off, 1), 0.0)
            down = jnp.where(lane < width_y - off, pltpu.roll(here, width_y - off, 1), 0.0)
            out = out + jnp.where(bands >= off, up + down, 0.0)
        halves.append(out)
    whole = jnp.concatenate(halves, axis=1)
    return whole / ((members - 1) * (2 * bands + 1)).astype(jnp.float32)


def beside(row, width_y):
    lane = lax.broadcasted_iota(jnp.int32, row.shape, 1)
    up = jnp.where(lane >= 1, pltpu.roll(row, 1, 1), 0.0)
    down = jnp.where(lane < width_y - 1, pltpu.roll(row, width_y - 1, 1), 0.0)
    return up + down


def advance(moved, spread, force, smooth, modes_ref, nu_ref, width_y):
    lifted = dot(modes_ref[...], smooth, TM)
    nu = nu_ref[...]
    lam = []
    for m in range(2):
        far, near, out_near, out_far = moved[m]
        v_far = far + nu * (out_far + near + beside(far, width_y) - 4.0 * far)
        v_near = near + nu * (far + out_near + beside(near, width_y) - 4.0 * near)
        lam.append(jnp.concatenate([v_far, v_near], axis=1) + spread[m] * lifted + force[m])
    return lam


def forcings(step, core, obs_ref, mine_ref, other, width_y):
    hot = hot_rows(core, obs_ref[step : step + 1, :], (0, 1), width_y)
    return placed(mine_ref[0, step], hot), placed(other, hot)


def next_lam(step, width_y, members, core_ref, obs_ref, mine_ref, own_a_ref, other_a_ref, other_ref, modes_ref,
             bands_ref, nu_ref, sums_ref, far_sent, near_sent, far_ref, near_ref):
    w = width_y
    total = sums_ref[0] + sums_ref[1] + sums_ref[2] + sums_ref[3]
    smooth = smooth_of(total, bands_ref[...], w, members)
    spread = both_spreads(own_a_ref, other_a_ref)
    count = obs_ref.shape[1]
    other = other_ref[step * count : (step + 1) * count, :]
    force = forcings(step, core_ref[0], obs_ref, mine_ref, other, w)
    cut = lambda ref, m: ref[:, m * w : (m + 1) * w]
    moved = [
        (cut(far_sent, m), cut(near_sent, m), cut(near_ref, 1 - m), cut(far_ref, 1 - m)) for m in range(2)
    ]
    return advance(moved, spread, force, smooth, modes_ref, nu_ref, w), spread


def second_kernel(width_y, members, core_ref, obs_ref, mine_ref, own_a_ref, rest_ref, late_ref, beyond_ref, first_matrix, matrix,
                  modes_ref, bands_ref, nu_ref, sums_ref,
                  far_out, near_out, sums_out, other_a_ref, other_ref):
    step = STEPS - 2
    core = core_ref[0]
    w = width_y
    state = own_a_ref.shape[0]
    count = obs_ref.shape[1]
    other_a_ref[...] = rest_ref[:state, :].astype(jnp.bfloat16)
    other_ref[...] = rest_ref[state:, :].astype(jnp.bfloat16)
    spread = both_spreads(own_a_ref, other_a_ref)
    hot = hot_rows(core, obs_ref[STEPS - 1 : STEPS, :], (0, 1, 2), w)
    far_hot = hot_rows(core, beyond_ref[2 * count : 2 * count + 1, :count].astype(jnp.int32), (3,), w)
    inside = (mine_ref[0, STEPS - 1], late_ref[...].astype(jnp.bfloat16))
    beyond = [beyond_ref[(1 - m) * count : (2 - m) * count, :].astype(jnp.bfloat16) for m in range(2)]
    turned = first_matrix[...]
    moved = []
    for m in range(2):
        lam = jnp.concatenate([placed(inside[m], hot), placed(beyond[m], far_hot)], axis=1)
        u = dot(turned, lam, TM)
        moved.append([u[:, i * w : (i + 1) * w] for i in range(4)])
    total = sums_ref[0]
    for j in range(1, 2 * PLANES):
        total = total + sums_ref[j]
    smooth = smooth_of(total, bands_ref[...], w, members)
    force = forcings(step, core, obs_ref, mine_ref, other_ref[step * count : (step + 1) * count, :], w)
    lam = advance(moved, spread, force, smooth, modes_ref, nu_ref, w)
    send_parts(lam, spread, matrix, modes_ref, far_out, near_out, sums_out, w)


def step_kernel(step, width_y, members, core_ref, obs_ref, mine_ref, own_a_ref, other_a_ref, other_ref, matrix,
                modes_ref, bands_ref, nu_ref, sums_ref, far_sent, near_sent, far_ref, near_ref,
                far_out, near_out, sums_out):
    lam, spread = next_lam(step, width_y, members, core_ref, obs_ref, mine_ref, own_a_ref, other_a_ref, other_ref,
                           modes_ref, bands_ref, nu_ref, sums_ref, far_sent, near_sent, far_ref, near_ref)
    send_parts(lam, spread, matrix, modes_ref, far_out, near_out, sums_out, width_y)


def last_kernel(step, width_y, members, core_ref, obs_ref, mine_ref, own_a_ref, other_a_ref, other_ref,
                modes_ref, bands_ref, nu_ref, sums_ref, far_sent, near_sent, far_ref, near_ref, own_out, other_out):
    lam, _ = next_lam(step, width_y, members, core_ref, obs_ref, mine_ref, own_a_ref, other_a_ref, other_ref,
                      modes_ref, bands_ref, nu_ref, sums_ref, far_sent, near_sent, far_ref, near_ref)
    own_out[...] = lam[0]
    other_out[...] = lam[1]


def finish_kernel(width_y, core_ref, own_ref, back_ref, out_ref):
    low = core_ref[0] == 0
    w = width_y
    mine = (own_ref[:, :w], own_ref[:, w:])
    got = (back_ref[:, :w], back_ref[:, w:])
    when_low = (mine[0], mine[1], got[1], got[0])
    when_high = (got[0], got[1], mine[1], mine[0])
    for x in range(4):
        out_ref[0, :, x, :] = jnp.where(low, when_low[x], when_high[x])


def call(kernel, name, args, outs, types=(), hbm=(), scratch=(), flops=400_000_000):
    spaces = [pltpu.SMEM] + [pltpu.HBM if i in hbm else pltpu.VMEM for i in range(1, len(args))]
    types = tuple(types) or (jnp.float32,) * len(outs)
    return pl.pallas_call(
        kernel,
        in_specs=[pl.BlockSpec(memory_space=space) for space in spaces],
        out_specs=[pl.BlockSpec(memory_space=pltpu.VMEM)] * len(outs),
        out_shape=[jax.ShapeDtypeStruct(o, t) for o, t in zip(outs, types)],
        scratch_shapes=list(scratch),
        cost_estimate=pl.CostEstimate(flops=flops, bytes_accessed=2_000_000, transcendentals=0),
        compiler_params=pltpu.CompilerParams(vmem_limit_bytes=None if name == "prepare" else VMEM),
    )(*args)


def per_device(innovations, obs_column, physics, diffusion, anomalies, modes, bands):
    members = lax.axis_size("member")
    tiles = lax.axis_size("tile")
    _, state, _, width_y = anomalies.shape
    core = (lax.axis_index("member") & 1).astype(jnp.int32)[None]
    mine = jnp.swapaxes(innovations, 2, 3)
    count = mine.shape[2]
    modes_t = modes.T
    n_modes = modes.shape[1]

    swap = [(i, i ^ 1) for i in range(members)]
    far_pairs = []
    for m in range(members):
        for t in range(tiles):
            target = (t + 1) % tiles if m % 2 else (t - 1) % tiles
            far_pairs.append((m * tiles + t, (m ^ 1) * tiles + target))
    side = 2 * PLANES
    y_groups = [[side * y + j for y in range(PLANES)] for j in range(side)]
    z_groups = [[side * y + 2 * z + c for z in range(PLANES)] for y in range(PLANES) for c in range(2)]
    chip_groups = [[side * y + j for j in range(side)] for y in range(PLANES)]

    half = (state, 2 * width_y)
    sums_shape = (PLANES, n_modes, 2 * width_y)
    bands_col = bands[:, None]
    nu_col = diffusion[:, None]
    late, sums = call(
        functools.partial(prepare_kernel, width_y),
        "prepare",
        (core, obs_column, mine, anomalies, modes_t),
        [(count, state), (PLANES, n_modes, 4 * width_y)],
        hbm=(2, 3),
        scratch=(
            pltpu.VMEM((count, state), mine.dtype),
            pltpu.VMEM(anomalies.shape, anomalies.dtype),
            pltpu.SemaphoreType.DMA((2,)),
        ),
    )
    sums = lax.all_to_all(sums, "member", 0, 0, tiled=True, axis_index_groups=y_groups)
    other_late = lax.ppermute(late, "member", swap)
    (beyond,) = call(pass_on_kernel, "pass_on", (core, obs_column, late, other_late), [(2 * count + 8, state)])
    beyond = lax.ppermute(beyond, ("member", "tile"), far_pairs)
    (sums,) = call(regroup_kernel, "regroup", (core, sums), [(side, n_modes, 2 * width_y)])
    sums = lax.all_to_all(sums, "member", 0, 0, tiled=True, axis_index_groups=chip_groups)
    mine_late, anomalies_late, _ = lax.optimization_barrier((mine, anomalies, other_late))
    own_a, rest = call(
        functools.partial(divide_kernel, width_y),
        "divide",
        (core, mine_late, anomalies_late),
        [half, (state + (STEPS - 1) * count, 2 * width_y)],
        types=(jnp.bfloat16, jnp.float32),
    )
    rest = lax.ppermute(rest, "member", swap)
    *sent, other_a, other_innov = call(
        functools.partial(second_kernel, width_y, members),
        "second",
        (core, obs_column, mine, own_a, rest, other_late, beyond, physics[STEPS - 2], physics[STEPS - 3], modes_t, bands_col, nu_col, sums),
        [half, half, sums_shape, half, ((STEPS - 1) * count, state)],
        types=(jnp.float32,) * 3 + (jnp.bfloat16,) * 2,
    )
    known = (core, obs_column, mine, own_a, other_a, other_innov)
    for step in range(STEPS - 3, -1, -1):
        far_sent, near_sent, sums = sent
        far = lax.ppermute(far_sent, ("member", "tile"), far_pairs)
        sums = lax.all_to_all(sums, "member", 0, 0, tiled=True, axis_index_groups=y_groups)
        near = lax.ppermute(near_sent, "member", swap)
        sums = jnp.broadcast_to(sums.sum(axis=0)[None], sums_shape)
        sums = lax.all_to_all(sums, "member", 0, 0, tiled=True, axis_index_groups=z_groups)
        tail = (modes_t, bands_col, nu_col, sums, far_sent, near_sent, far, near)
        if step > 0:
            sent = call(
                functools.partial(step_kernel, step, width_y, members),
                f"step{step}",
                known + (physics[step - 1],) + tail,
                [half, half, sums_shape],
            )
        else:
            own, other = call(
                functools.partial(last_kernel, step, width_y, members),
                "last",
                known + tail,
                [half, half],
            )
    back = lax.ppermute(other, "member", swap)
    return call(functools.partial(finish_kernel, width_y), "finish", (core, own, back), [(1, *anomalies.shape[1:])])[0]


def solution(mesh):
    in_specs = (
        P("member", None, None, "tile"),
        P(None, "tile"),
        P(),
        P(),
        P("member", None, "tile", None),
        P(),
        P(),
    )
    out_specs = P("member", None, "tile", None)
    return jax.shard_map(
        per_device, mesh=mesh, in_specs=in_specs, out_specs=out_specs, check_vma=False
    )
```

time: 100 us -> 104 us (1.040)
  blocking collectives: 36.7 us -> 28.2 us
  starting transfers between devices: 45.7 us -> 52.8 us
  waiting for transfers between devices: 5.89 us -> 9.47 us
  Pallas kernels: 7.98 us -> 9.27 us
    ppermute x1 -> x3, starting transfers between devices: 8.74 us -> 17.6 us  [the longest x1 8.75 us: per_device(): other_late = lax.ppermute(late, 'member', swap)]
    all_to_all x5 -> x4, blocking collectives: 36.7 us -> 28.2 us  [the longest x2 14.3 us: per_device(): lax.all_to_all(sums, 'member', 0, 0, tiled=True, axis_index_groups=y_groups)]
    ppermute x3 -> x2, starting transfers between devices: 15.9 us -> 8.1 us  [per_device(): far = lax.ppermute(far_sent, ('member', 'tile'), far_pairs)]
    all_to_all x1 -> x2, starting transfers between devices: 3.42 us -> 7.91 us  [the longest x1 4.44 us: per_device(): lax.all_to_all(sums, 'member', 0, 0, tiled=True, axis_index_groups=chip_g...]
    ppermute x1 -> x3, waiting for transfers between devices: 1.73 us -> 6.05 us  [the longest x1 6.04 us: per_device(): beyond = lax.ppermute(beyond, ('member', 'tile'), far_pairs)]
    ppermute x3 -> x2, starting transfers between devices: 13.7 us -> 15.3 us  [per_device(): near = lax.ppermute(near_sent, 'member', swap)]
    pallas_call x6 -> x8, Pallas kernels: 7.98 us -> 9.27 us  [call(): pl.pallas_call(kernel, in_specs=[pl.BlockSpec(memory_space=space) for spa...]
    squeeze x0 -> x1, local copies, waits for them, and re-layouts: none -> 1.16 us  [per_device(): physics[step - 1]]
  transfers between devices with their start and end apart: 9 -> 10, of which waited for: 3 -> 3; matrix products, arithmetic and copies ran while one was open for 1% -> 1% of each run, Pallas kernels for 0% -> 1%
where the time goes in v4:
time: 104 us; the launch traced here: 103 us
  starting transfers between devices  52.8 us (51%)
  blocking collectives  28.2 us (27%)
  waiting for transfers between devices  9.47 us (9%)
  Pallas kernels  9.27 us (9%)
  local copies, waits for them, and re-layouts  3.46 us (3%)
    ppermute x2, starting transfers between devices, per_device(): near = lax.ppermute(near_sent, 'member', swap)  15.3 us
    all_to_all x2, blocking collectives, per_device(): lax.all_to_all(sums, 'member', 0, 0, tiled=True, axis_index_groups=y_groups)  14.3 us
    all_to_all x2, blocking collectives, per_device(): lax.all_to_all(sums, 'member', 0, 0, tiled=True, axis_index_groups=z_groups)  13.9 us
    pallas_call x8, Pallas kernels, call(): pl.pallas_call(kernel, in_specs=[pl.BlockSpec(memory_space=space) for spa...  9.27 us
    ppermute x1, starting transfers between devices, per_device(): other_late = lax.ppermute(late, 'member', swap)  8.75 us
    ppermute x2, starting transfers between devices, per_device(): far = lax.ppermute(far_sent, ('member', 'tile'), far_pairs)  8.1 us
    ppermute x1, starting transfers between devices, per_device(): beyond = lax.ppermute(beyond, ('member', 'tile'), far_pairs)  6.93 us
    ppermute x1, waiting for transfers between devices, per_device(): beyond = lax.ppermute(beyond, ('member', 'tile'), far_pairs)  6.04 us
  transfers between devices with their start and end apart: 10, of which 3 were waited for; matrix products, arithmetic and copies ran while one was open for 1% of the time, Pallas kernels for 1%

profile of v4, /device:TPU:1, one launch (start us, length us, event | category | flops | bytes accessed | tf_op | source)
XLA Modules:
  0.0 103.4 jit_solution(1013236682902001397)
XLA Ops:
  0.0 3.1 %shard_map.73 = (f32[64,256]{1,0:T(8,128)}, f32[4,16,512]{2,1,0:T(8,128)}) custom-call(s32[1]{0:T(128)} %bitcast.core_ref, s32[4,64]{1,0:T(4,128)} %obs_ref.9, bf16[1,4,64,256]{3,2,1,0:T(8,128)(2,1)} %bitcast.11, bf16[1,256,4,128]{3,2,1,0:T(4,128)(2,1)} %anomalies_ref, f32[16,256]{1,0:T(8,128)} %bitcast.16), custom_call_target="tpu_custom_call" | custom-call | flops 400000000 | bytes 2000000 | tf_op jit(solution)/shard_map/pallas_call | solution.py:231
  3.1 8.7 %collective-permute-start = (f32[64,256]{1,0:T(8,128)}, f32[64,256]{1,0:T(8,128)S(1)}, u32[]{:S(2)}, u32[]{:S(2)}) collective-permute-start(f32[64,256]{1,0:T(8,128)} %get-tuple-element.21.late_ref), channel_id=1, source_target_pairs={{0,16},{16,0},{32,48},{48,32},{64,80},{80,64},{96,112},{112,96},{1... | collective-permute-start | bytes 196616 | tf_op jit(solution)/shard_map/ppermute | solution.py:280
  11.8 0.0 copy-start
  11.8 3.5 %all-to-all-start = ((f32[4,16,512]{2,1,0:T(8,128)}), f32[4,16,512]{2,1,0:T(8,128)S(1)}, u32[]{:S(2)}, u32[]{:S(2)}) async-start(f32[4,16,512]{2,1,0:T(8,128)} %get-tuple-element.26), calls=%async_computation | async-start | bytes 262144 | tf_op jit(solution)/shard_map/all_to_all | solution.py:279
  15.4 0.8 shard_map.74
  16.1 1.9 %collective-permute-start.1 = (f32[448,256]{1,0:T(8,128)S(1)}, f32[448,256]{1,0:T(8,128)S(1)}, u32[]{:S(2)}, u32[]{:S(2)}) collective-permute-start(f32[448,256]{1,0:T(8,128)S(1)} %get-tuple-element.25), channel_id=1, source_target_pairs={{0,16},{16,0},{32,48},{48,32},{64,80},{80,64},{96,112},{112,96},{1... | collective-permute-start | bytes 1376264 | tf_op jit(solution)/shard_map/ppermute | solution.py:293
  18.1 2.3 %all-to-all-done.sums_ref = f32[4,16,512]{2,1,0:T(8,128)S(1)} async-done(((f32[4,16,512]{2,1,0:T(8,128)}), f32[4,16,512]{2,1,0:T(8,128)S(1)}, u32[]{:S(2)}, u32[]{:S(2)}) %all-to-all-start) | async-done | bytes 131104 | tf_op jit(solution)/shard_map/all_to_all | solution.py:279
  20.3 0.7 shard_map.76
  21.0 4.4 %all-to-all-start.1 = ((f32[8,16,256]{2,1,0:T(8,128)}), f32[8,16,256]{2,1,0:T(8,128)S(1)}, u32[]{:S(2)}, u32[]{:S(2)}) async-start(f32[8,16,256]{2,1,0:T(8,128)} %shard_map.76), calls=%async_computation.1 | async-start | bytes 262144 | tf_op jit(solution)/shard_map/all_to_all | solution.py:284
  25.5 0.7 copy-done.6
  26.1 0.1 copy.11.bands_ref
  26.2 0.7 copy-done.5
  26.9 0.1 copy.12.nu_ref
  27.0 0.5 copy-done.2
  27.6 0.2 copy-done.4
  27.7 6.9 %collective-permute-start.2 = (f32[136,256]{1,0:T(8,128)S(1)}, f32[136,256]{1,0:T(8,128)S(1)}, u32[]{:S(2)}, u32[]{:S(2)}) collective-permute-start(f32[136,256]{1,0:T(8,128)S(1)} %shard_map.75), channel_id=1, source_target_pairs={{0,31},{1,16},{2,17},{3,18},{4,19},{5,20},{6,21},{7,22},{8,23},{9,... | collective-permute-start | bytes 417800 | tf_op jit(solution)/shard_map/ppermute | solution.py:282
  34.7 1.2 %slice_bitcast_fusion = (f32[256,256]{1,0:T(8,128)S(1)}, f32[256,256]{1,0:T(8,128)S(1)}, f32[256,256]{1,0:T(8,128)S(1)}) fusion(f32[4,256,256]{2,1,0:T(8,128)} %param.9), kind=kLoop, calls=%fused_computation | loop fusion | bytes 1572864 | tf_op jit(solution)/shard_map/squeeze | solution.py:314
  35.9 6.0 %collective-permute-done.2.beyond_ref = f32[136,256]{1,0:T(8,128)S(1)} collective-permute-done((f32[136,256]{1,0:T(8,128)S(1)}, f32[136,256]{1,0:T(8,128)S(1)}, u32[]{:S(2)}, u32[]{:S(2)}) %collective-permute-start.2) | collective-permute-done | bytes 139296 | tf_op jit(solution)/shard_map/ppermute | solution.py:282
  41.9 1.8 %shard_map.77 = (f32[256,256]{1,0:T(8,128)S(1)}, f32[256,256]{1,0:T(8,128)S(1)}, f32[4,16,256]{2,1,0:T(8,128)S(1)}, bf16[256,256]{1,0:T(8,128)(2,1)S(1)}, bf16[192,256]{1,0:T(8,128)(2,1)S(1)}) custom-call(s32[1]{0:T(128)} %bitcast.core_ref, s32[4,64]{1,0:T(4,128)S(1)} %copy-done.2, bf16[1,4,64,256]{3,2,1,0:T(8,128)(2,1)S(1)} %bitcast.13, ...), custom_call_target="tpu_custom_call" | custom-call | flops 400000000 | bytes 2000000 | tf_op jit(solution)/shard_map/pallas_call | solution.py:231
  43.7 3.4 %collective-permute-start.3 = (f32[256,256]{1,0:T(8,128)S(1)}, f32[256,256]{1,0:T(8,128)S(1)}, u32[]{:S(2)}, u32[]{:S(2)}) collective-permute-start(f32[256,256]{1,0:T(8,128)S(1)} %get-tuple-element.30.far_sent), channel_id=1, source_target_pairs={{0,31},{1,16},{2,17},{3,18},{4,19},{5,20},{6,21},{7,22},{8,23},{9,... | collective-permute-start | bytes 786440 | tf_op jit(solution)/shard_map/ppermute | solution.py:304
  47.0 12.0 %collective-permute-start.4 = (f32[256,256]{1,0:T(8,128)S(1)}, f32[256,256]{1,0:T(8,128)S(1)}, u32[]{:S(2)}, u32[]{:S(2)}) collective-permute-start(f32[256,256]{1,0:T(8,128)S(1)} %get-tuple-element.31.near_sent), channel_id=1, source_target_pairs={{0,16},{16,0},{32,48},{48,32},{64,80},{80,64},{96,112},{112,96},{1... | collective-permute-start | bytes 786440 | tf_op jit(solution)/shard_map/ppermute | solution.py:306
  59.0 7.1 %all_to_all.30 = f32[4,16,256]{2,1,0:T(8,128)S(1)} all-to-all(f32[4,16,256]{2,1,0:T(8,128)S(1)} %get-tuple-element.29), channel_id=1, replica_groups={{0,128,256,384},{16,144,272,400},{32,160,288,416},{48,176,304,432},{64,..., dimensions={0} | all-to-all | bytes 131072 | tf_op jit(solution)/shard_map/all_to_all | solution.py:305
  66.2 7.0 %all_to_all.31.sums_ref = f32[4,16,256]{2,1,0:T(8,128)S(1)} all-to-all(f32[4,16,256]{2,1,0:T(8,128)S(1)} %broadcast_in_dim.24), channel_id=1, replica_groups={{0,32,64,96},{16,48,80,112},{128,160,192,224},{144,176,208,240},{256,28..., dimensions={0} | all-to-all | bytes 131072 | tf_op jit(solution)/shard_map/all_to_all | solution.py:308
  73.2 1.2 %shard_map.78 = (f32[256,256]{1,0:T(8,128)S(1)}, f32[256,256]{1,0:T(8,128)S(1)}, f32[4,16,256]{2,1,0:T(8,128)S(1)}) custom-call(s32[1]{0:T(128)} %bitcast.core_ref, s32[4,64]{1,0:T(4,128)S(1)} %copy-done.2, bf16[1,4,64,256]{3,2,1,0:T(8,128)(2,1)S(1)} %bitcast.14, bf16[256,256]{1,0:T(8,128)(2,1)S(1)} %get-tuple-element.24.own_a_ref, ...), custom_call_target="tpu_custom_call" | custom-call | flops 400000000 | bytes 2000000 | tf_op jit(solution)/shard_map/pallas_call | solution.py:231
  74.3 4.8 %collective-permute-start.5 = (f32[256,256]{1,0:T(8,128)S(1)}, f32[256,256]{1,0:T(8,128)S(1)}, u32[]{:S(2)}, u32[]{:S(2)}) collective-permute-start(f32[256,256]{1,0:T(8,128)S(1)} %get-tuple-element.33.far_sent), channel_id=1, source_target_pairs={{0,31},{1,16},{2,17},{3,18},{4,19},{5,20},{6,21},{7,22},{8,23},{9,... | collective-permute-start | bytes 786440 | tf_op jit(solution)/shard_map/ppermute | solution.py:304
  79.1 3.3 %collective-permute-start.6 = (f32[256,256]{1,0:T(8,128)S(1)}, f32[256,256]{1,0:T(8,128)S(1)}, u32[]{:S(2)}, u32[]{:S(2)}) collective-permute-start(f32[256,256]{1,0:T(8,128)S(1)} %get-tuple-element.34.near_sent), channel_id=1, source_target_pairs={{0,16},{16,0},{32,48},{48,32},{64,80},{80,64},{96,112},{112,96},{1... | collective-permute-start | bytes 786440 | tf_op jit(solution)/shard_map/ppermute | solution.py:306
  82.4 7.1 %all_to_all.32 = f32[4,16,256]{2,1,0:T(8,128)S(1)} all-to-all(f32[4,16,256]{2,1,0:T(8,128)S(1)} %get-tuple-element.32), channel_id=1, replica_groups={{0,128,256,384},{16,144,272,400},{32,160,288,416},{48,176,304,432},{64,..., dimensions={0} | all-to-all | bytes 131072 | tf_op jit(solution)/shard_map/all_to_all | solution.py:305
  89.6 7.0 %all_to_all.33.sums_ref = f32[4,16,256]{2,1,0:T(8,128)S(1)} all-to-all(f32[4,16,256]{2,1,0:T(8,128)S(1)} %broadcast_in_dim.25), channel_id=1, replica_groups={{0,32,64,96},{16,48,80,112},{128,160,192,224},{144,176,208,240},{256,28..., dimensions={0} | all-to-all | bytes 131072 | tf_op jit(solution)/shard_map/all_to_all | solution.py:308
  96.5 0.7 shard_map.79
  97.3 3.9 %collective-permute-start.7 = (f32[256,256]{1,0:T(8,128)S(1)}, f32[256,256]{1,0:T(8,128)S(1)}, u32[]{:S(2)}, u32[]{:S(2)}) collective-permute-start(f32[256,256]{1,0:T(8,128)S(1)} %get-tuple-element.36), channel_id=1, source_target_pairs={{0,16},{16,0},{32,48},{48,32},{64,80},{80,64},{96,112},{112,96},{1... | collective-permute-start | bytes 786440 | tf_op jit(solution)/shard_map/ppermute | solution.py:324
  101.2 1.1 %collective-permute-done.7.back_ref = f32[256,256]{1,0:T(8,128)S(1)} collective-permute-done((f32[256,256]{1,0:T(8,128)S(1)}, f32[256,256]{1,0:T(8,128)S(1)}, u32[]{:S(2)}, u32[]{:S(2)}) %collective-permute-start.7) | collective-permute-done | bytes 262176 | tf_op jit(solution)/shard_map/ppermute | solution.py:324
  102.3 1.1 %shard_map.80 = f32[1,256,4,128]{3,2,1,0:T(4,128)} custom-call(s32[1]{0:T(128)} %bitcast.core_ref, f32[256,256]{1,0:T(8,128)S(1)} %get-tuple-element.35.own_ref, f32[256,256]{1,0:T(8,128)S(1)} %collective-permute-done.7.back_ref), custom_call_target="tpu_custom_call" | custom-call | flops 400000000 | bytes 2000000 | tf_op jit(solution)/shard_map/pallas_call | solution.py:231
  (21 shorter events, 0.1 us)
Async XLA Ops:
  0.0 15.3 %copy-start.3 = (bf16[1,256,4,128]{3,2,1,0:T(4,128)(2,1)S(1)}, bf16[1,256,4,128]{3,2,1,0:T(4,128)(2,1)}, u32[]{:S(2)}) copy-start(bf16[1,256,4,128]{3,2,1,0:T(4,128)(2,1)} %anomalies_ref) | copy-start | bytes 786436
  3.1 12.2 %collective-permute-start = (f32[64,256]{1,0:T(8,128)}, f32[64,256]{1,0:T(8,128)S(1)}, u32[]{:S(2)}, u32[]{:S(2)}) collective-permute-start(f32[64,256]{1,0:T(8,128)} %get-tuple-element.21.late_ref), channel_id=1, source_target_pairs={{0,16},{16,0},{32,48},{48,32},{64,80},{80,64},{96,112},{112,96},{1... | collective-permute-start | bytes 196616 | tf_op jit(solution)/shard_map/ppermute | solution.py:280
  11.8 3.5 %copy-start = (bf16[1,4,256,64]{2,3,1,0:T(8,128)(2,1)S(1)}, bf16[1,4,256,64]{2,3,1,0:T(8,128)(2,1)}, u32[]{:S(2)}) copy-start(bf16[1,4,256,64]{2,3,1,0:T(8,128)(2,1)} %param.7) | copy-start | bytes 393220
  11.8 8.5 %all-to-all-start = ((f32[4,16,512]{2,1,0:T(8,128)}), f32[4,16,512]{2,1,0:T(8,128)S(1)}, u32[]{:S(2)}, u32[]{:S(2)}) async-start(f32[4,16,512]{2,1,0:T(8,128)} %get-tuple-element.26), calls=%async_computation | async-start | bytes 262144 | tf_op jit(solution)/shard_map/all_to_all | solution.py:279
  16.1 25.8 %collective-permute-start.1 = (f32[448,256]{1,0:T(8,128)S(1)}, f32[448,256]{1,0:T(8,128)S(1)}, u32[]{:S(2)}, u32[]{:S(2)}) collective-permute-start(f32[448,256]{1,0:T(8,128)S(1)} %get-tuple-element.25), channel_id=1, source_target_pairs={{0,16},{16,0},{32,48},{48,32},{64,80},{80,64},{96,112},{112,96},{1... | collective-permute-start | bytes 1376264 | tf_op jit(solution)/shard_map/ppermute | solution.py:293
  21.0 20.9 %all-to-all-start.1 = ((f32[8,16,256]{2,1,0:T(8,128)}), f32[8,16,256]{2,1,0:T(8,128)S(1)}, u32[]{:S(2)}, u32[]{:S(2)}) async-start(f32[8,16,256]{2,1,0:T(8,128)} %shard_map.76), calls=%async_computation.1 | async-start | bytes 262144 | tf_op jit(solution)/shard_map/all_to_all | solution.py:284
  25.5 0.7 copy-start.6
  26.2 0.7 copy-start.5
  26.9 0.7 copy-start.2
  26.9 0.9 copy-start.4
  27.7 14.2 %collective-permute-start.2 = (f32[136,256]{1,0:T(8,128)S(1)}, f32[136,256]{1,0:T(8,128)S(1)}, u32[]{:S(2)}, u32[]{:S(2)}) collective-permute-start(f32[136,256]{1,0:T(8,128)S(1)} %shard_map.75), channel_id=1, source_target_pairs={{0,31},{1,16},{2,17},{3,18},{4,19},{5,20},{6,21},{7,22},{8,23},{9,... | collective-permute-start | bytes 417800 | tf_op jit(solution)/shard_map/ppermute | solution.py:282
  34.7 7.2 %copy-start.1 = (f32[256,16]{0,1:T(8,128)S(1)}, f32[256,16]{0,1:T(8,128)}, u32[]{:S(2)}) copy-start(f32[256,16]{0,1:T(8,128)} %param.12) | copy-start | bytes 49156
  43.7 29.5 %collective-permute-start.3 = (f32[256,256]{1,0:T(8,128)S(1)}, f32[256,256]{1,0:T(8,128)S(1)}, u32[]{:S(2)}, u32[]{:S(2)}) collective-permute-start(f32[256,256]{1,0:T(8,128)S(1)} %get-tuple-element.30.far_sent), channel_id=1, source_target_pairs={{0,31},{1,16},{2,17},{3,18},{4,19},{5,20},{6,21},{7,22},{8,23},{9,... | collective-permute-start | bytes 786440 | tf_op jit(solution)/shard_map/ppermute | solution.py:304
  47.0 26.1 %collective-permute-start.4 = (f32[256,256]{1,0:T(8,128)S(1)}, f32[256,256]{1,0:T(8,128)S(1)}, u32[]{:S(2)}, u32[]{:S(2)}) collective-permute-start(f32[256,256]{1,0:T(8,128)S(1)} %get-tuple-element.31.near_sent), channel_id=1, source_target_pairs={{0,16},{16,0},{32,48},{48,32},{64,80},{80,64},{96,112},{112,96},{1... | collective-permute-start | bytes 786440 | tf_op jit(solution)/shard_map/ppermute | solution.py:306
  74.3 22.2 %collective-permute-start.5 = (f32[256,256]{1,0:T(8,128)S(1)}, f32[256,256]{1,0:T(8,128)S(1)}, u32[]{:S(2)}, u32[]{:S(2)}) collective-permute-start(f32[256,256]{1,0:T(8,128)S(1)} %get-tuple-element.33.far_sent), channel_id=1, source_target_pairs={{0,31},{1,16},{2,17},{3,18},{4,19},{5,20},{6,21},{7,22},{8,23},{9,... | collective-permute-start | bytes 786440 | tf_op jit(solution)/shard_map/ppermute | solution.py:304
  79.1 17.4 %collective-permute-start.6 = (f32[256,256]{1,0:T(8,128)S(1)}, f32[256,256]{1,0:T(8,128)S(1)}, u32[]{:S(2)}, u32[]{:S(2)}) collective-permute-start(f32[256,256]{1,0:T(8,128)S(1)} %get-tuple-element.34.near_sent), channel_id=1, source_target_pairs={{0,16},{16,0},{32,48},{48,32},{64,80},{80,64},{96,112},{112,96},{1... | collective-permute-start | bytes 786440 | tf_op jit(solution)/shard_map/ppermute | solution.py:306
  97.3 5.1 %collective-permute-start.7 = (f32[256,256]{1,0:T(8,128)S(1)}, f32[256,256]{1,0:T(8,128)S(1)}, u32[]{:S(2)}, u32[]{:S(2)}) collective-permute-start(f32[256,256]{1,0:T(8,128)S(1)} %get-tuple-element.36), channel_id=1, source_target_pairs={{0,16},{16,0},{32,48},{48,32},{64,80},{80,64},{96,112},{112,96},{1... | collective-permute-start | bytes 786440 | tf_op jit(solution)/shard_map/ppermute | solution.py:324

commit v5 on v4

--- a/solution.py
+++ b/solution.py
@@ -22,11 +22,13 @@
     return high, (x - high.astype(jnp.float32)).astype(jnp.bfloat16)
 
 
+def product(a, b, dims=MM):
+    part = lambda p, q: lax.dot_general(p, q, dims, preferred_element_type=jnp.float32)
+    return part(a[0], b[0]) + (part(a[0], b[1]) + part(a[1], b[0]))
+
+
 def dot(a, b, dims=MM):
-    part = lambda p, q: lax.dot_general(p, q, dims, preferred_element_type=jnp.float32)
-    a_high, a_low = halves(a)
-    b_high, b_low = halves(b)
-    return part(a_high, b_high) + (part(a_high, b_low) + part(a_low, b_high))
+    return product(halves(a), halves(b), dims)
 
 
 def hot_rows(core, obs_row, sides, width_y):
@@ -43,17 +45,20 @@
     return lax.dot_general(values, hot, (((0,), (1,)), ((), ())), preferred_element_type=jnp.float32)
 
 
-def send_parts(lam, spread, physics, modes_ref, far_ref, near_ref, sums_ref, width_y):
-    product = spread[0] * lam[0] + spread[1] * lam[1]
-    local = dot(modes_ref[...], product)
+def send_parts(lam, spread, turned, modes_ref, far_ref, near_ref, sums_ref, width_y):
+    w = width_y
+    for m in range(2):
+        moved = product(turned, halves(lam[m]))
+        far_ref[:, m * w : (m + 1) * w] = moved[:, :w]
+        near_ref[:, m * w : (m + 1) * w] = moved[:, w:]
+    local = dot(modes_ref[...], spread[0] * lam[0] + spread[1] * lam[1])
     for copy in range(PLANES):
         sums_ref[copy] = local
-    w = width_y
-    matrix = physics[...]
-    for m in range(2):
-        moved = dot(matrix, lam[m], TM)
-        far_ref[:, m * w : (m + 1) * w] = moved[:, :w]
-        near_ref[:, m * w : (m + 1) * w] = moved[:, w:]
+
+
+def turn_kernel(core_ref, physics_ref, high_ref, low_ref):
+    for t in range(STEPS - 1):
+        high_ref[t], low_ref[t] = halves(jnp.transpose(physics_ref[t]))
 
 
 def prepare_kernel(width_y, core_ref, obs_ref, mine_hbm, anomalies_hbm, modes_ref, late_ref, sums_ref,
@@ -135,16 +140,10 @@
     return up + down
 
 
-def advance(moved, spread, force, smooth, modes_ref, nu_ref, width_y):
-    lifted = dot(modes_ref[...], smooth, TM)
-    nu = nu_ref[...]
-    lam = []
-    for m in range(2):
-        far, near, out_near, out_far = moved[m]
-        v_far = far + nu * (out_far + near + beside(far, width_y) - 4.0 * far)
-        v_near = near + nu * (far + out_near + beside(near, width_y) - 4.0 * near)
-        lam.append(jnp.concatenate([v_far, v_near], axis=1) + spread[m] * lifted + force[m])
-    return lam
+def diffused(far, near, out_near, nu, width_y):
+    v_far = far + nu * (near + beside(far, width_y) - 4.0 * far)
+    v_near = near + nu * (far + out_near + beside(near, width_y) - 4.0 * near)
+    return jnp.concatenate([v_far, v_near], axis=1)
 
 
 def forcings(step, core, obs_ref, mine_ref, other, width_y):
@@ -152,66 +151,78 @@
     return placed(mine_ref[0, step], hot), placed(other, hot)
 
 
-def next_lam(step, width_y, members, core_ref, obs_ref, mine_ref, own_a_ref, other_a_ref, other_ref, modes_ref,
-             bands_ref, nu_ref, sums_ref, far_sent, near_sent, far_ref, near_ref):
-    w = width_y
-    total = sums_ref[0] + sums_ref[1] + sums_ref[2] + sums_ref[3]
-    smooth = smooth_of(total, bands_ref[...], w, members)
-    spread = both_spreads(own_a_ref, other_a_ref)
+def ahead_kernel(width_y, core_ref, obs_ref, mine_ref, rest_ref, late_ref, beyond_ref, high_ref, low_ref, nu_ref,
+                 own_g_ref, other_g_ref, other_a_ref, other_ref):
+    step = STEPS - 2
+    core = core_ref[0]
+    w = width_y
+    nu = nu_ref[...]
+    state = other_a_ref.shape[0]
+    count = obs_ref.shape[1]
+    other_a_ref[...] = rest_ref[:state, :].astype(jnp.bfloat16)
+    other_ref[...] = rest_ref[state:, :].astype(jnp.bfloat16)
+    hot = hot_rows(core, obs_ref[STEPS - 1 : STEPS, :], (0, 1, 2), w)
+    far_hot = hot_rows(core, beyond_ref[2 * count : 2 * count + 1, :count].astype(jnp.int32), (3,), w)
+    inside = (mine_ref[0, STEPS - 1], late_ref[...].astype(jnp.bfloat16))
+    beyond = [beyond_ref[(1 - m) * count : (2 - m) * count, :].astype(jnp.bfloat16) for m in range(2)]
+    force = forcings(step, core, obs_ref, mine_ref, other_ref[step * count : (step + 1) * count, :], w)
+    for m, out_ref in enumerate((own_g_ref, other_g_ref)):
+        lam = jnp.concatenate([placed(inside[m], hot), placed(beyond[m], far_hot)], axis=1)
+        u = product((high_ref[step], low_ref[step]), halves(lam))
+        far, near, out_near, out_far = [u[:, i * w : (i + 1) * w] for i in range(4)]
+        g = diffused(far, near, out_near, nu, w) + force[m]
+        out_ref[:, :w] = g[:, :w] + nu * out_far
+        out_ref[:, w:] = g[:, w:]
+
+
+def between_kernel(step, width_y, core_ref, obs_ref, mine_ref, other_ref, nu_ref, far_sent, near_sent, near_ref,
+                   own_g_ref, other_g_ref):
+    w = width_y
     count = obs_ref.shape[1]
     other = other_ref[step * count : (step + 1) * count, :]
     force = forcings(step, core_ref[0], obs_ref, mine_ref, other, w)
     cut = lambda ref, m: ref[:, m * w : (m + 1) * w]
-    moved = [
-        (cut(far_sent, m), cut(near_sent, m), cut(near_ref, 1 - m), cut(far_ref, 1 - m)) for m in range(2)
-    ]
-    return advance(moved, spread, force, smooth, modes_ref, nu_ref, w), spread
-
-
-def second_kernel(width_y, members, core_ref, obs_ref, mine_ref, own_a_ref, rest_ref, late_ref, beyond_ref, first_matrix, matrix,
-                  modes_ref, bands_ref, nu_ref, sums_ref,
-                  far_out, near_out, sums_out, other_a_ref, other_ref):
-    step = STEPS - 2
-    core = core_ref[0]
-    w = width_y
-    state = own_a_ref.shape[0]
-    count = obs_ref.shape[1]
-    other_a_ref[...] = rest_ref[:state, :].astype(jnp.bfloat16)
-    other_ref[...] = rest_ref[state:, :].astype(jnp.bfloat16)
+    for m, out_ref in enumerate((own_g_ref, other_g_ref)):
+        g = diffused(cut(far_sent, m), cut(near_sent, m), cut(near_ref, 1 - m), nu_ref[...], w)
+        out_ref[...] = g + force[m]
+
+
+def lifted_of(sums_ref, bands_ref, modes_ref, width_y, members):
+    total = sums_ref[0]
+    for j in range(1, sums_ref.shape[0]):
+        total = total + sums_ref[j]
+    return dot(modes_ref[...], smooth_of(total, bands_ref[...], width_y, members), TM)
+
+
+def second_kernel(width_y, members, core_ref, own_a_ref, other_a_ref, high_ref, low_ref, modes_ref, bands_ref, sums_ref,
+                  own_g_ref, other_g_ref, far_out, near_out, sums_out):
+    lifted = lifted_of(sums_ref, bands_ref, modes_ref, width_y, members)
     spread = both_spreads(own_a_ref, other_a_ref)
-    hot = hot_rows(core, obs_ref[STEPS - 1 : STEPS, :], (0, 1, 2), w)
-    far_hot = hot_rows(core, beyond_ref[2 * count : 2 * count + 1, :count].astype(jnp.int32), (3,), w)
-    inside = (mine_ref[0, STEPS - 1], late_ref[...].astype(jnp.bfloat16))
-    beyond = [beyond_ref[(1 - m) * count : (2 - m) * count, :].astype(jnp.bfloat16) for m in range(2)]
-    turned = first_matrix[...]
-    moved = []
-    for m in range(2):
-        lam = jnp.concatenate([placed(inside[m], hot), placed(beyond[m], far_hot)], axis=1)
-        u = dot(turned, lam, TM)
-        moved.append([u[:, i * w : (i + 1) * w] for i in range(4)])
-    total = sums_ref[0]
-    for j in range(1, 2 * PLANES):
-        total = total + sums_ref[j]
-    smooth = smooth_of(total, bands_ref[...], w, members)
-    force = forcings(step, core, obs_ref, mine_ref, other_ref[step * count : (step + 1) * count, :], w)
-    lam = advance(moved, spread, force, smooth, modes_ref, nu_ref, w)
-    send_parts(lam, spread, matrix, modes_ref, far_out, near_out, sums_out, w)
-
-
-def step_kernel(step, width_y, members, core_ref, obs_ref, mine_ref, own_a_ref, other_a_ref, other_ref, matrix,
-                modes_ref, bands_ref, nu_ref, sums_ref, far_sent, near_sent, far_ref, near_ref,
-                far_out, near_out, sums_out):
-    lam, spread = next_lam(step, width_y, members, core_ref, obs_ref, mine_ref, own_a_ref, other_a_ref, other_ref,
-                           modes_ref, bands_ref, nu_ref, sums_ref, far_sent, near_sent, far_ref, near_ref)
-    send_parts(lam, spread, matrix, modes_ref, far_out, near_out, sums_out, width_y)
-
-
-def last_kernel(step, width_y, members, core_ref, obs_ref, mine_ref, own_a_ref, other_a_ref, other_ref,
-                modes_ref, bands_ref, nu_ref, sums_ref, far_sent, near_sent, far_ref, near_ref, own_out, other_out):
-    lam, _ = next_lam(step, width_y, members, core_ref, obs_ref, mine_ref, own_a_ref, other_a_ref, other_ref,
-                      modes_ref, bands_ref, nu_ref, sums_ref, far_sent, near_sent, far_ref, near_ref)
-    own_out[...] = lam[0]
-    other_out[...] = lam[1]
+    lam = [g_ref[...] + a * lifted for g_ref, a in zip((own_g_ref, other_g_ref), spread)]
+    turned = (high_ref[STEPS - 3], low_ref[STEPS - 3])
+    send_parts(lam, spread, turned, modes_ref, far_out, near_out, sums_out, width_y)
+
+
+def joined(g_ref, far_ref, nu, m, width_y):
+    w = width_y
+    far = g_ref[:, :w] + nu * far_ref[:, (1 - m) * w : (2 - m) * w]
+    return jnp.concatenate([far, g_ref[:, w:]], axis=1)
+
+
+def step_kernel(step, width_y, members, core_ref, own_a_ref, other_a_ref, high_ref, low_ref, modes_ref, bands_ref,
+                nu_ref, sums_ref, own_g_ref, other_g_ref, far_ref, far_out, near_out, sums_out):
+    lifted = lifted_of(sums_ref, bands_ref, modes_ref, width_y, members)
+    spread = both_spreads(own_a_ref, other_a_ref)
+    nu = nu_ref[...]
+    g = (joined(own_g_ref, far_ref, nu, 0, width_y), joined(other_g_ref, far_ref, nu, 1, width_y))
+    lam = [g[m] + spread[m] * lifted for m in range(2)]
+    turned = (high_ref[step - 1], low_ref[step - 1])
+    send_parts(lam, spread, turned, modes_ref, far_out, near_out, sums_out, width_y)
+
+
+def last_kernel(member, width_y, members, core_ref, a_ref, modes_ref, bands_ref, nu_ref, sums_ref, g_ref, far_ref, out_ref):
+    lifted = lifted_of(sums_ref, bands_ref, modes_ref, width_y, members)
+    out_ref[...] = joined(g_ref, far_ref, nu_ref[...], member, width_y) + a_ref[...].astype(jnp.float32) * lifted
 
 
 def finish_kernel(width_y, core_ref, own_ref, back_ref, out_ref):
@@ -291,36 +302,51 @@
         types=(jnp.bfloat16, jnp.float32),
     )
     rest = lax.ppermute(rest, "member", swap)
-    *sent, other_a, other_innov = call(
+    physics_late, _ = lax.optimization_barrier((physics, other_late))
+    turned = call(turn_kernel, "turn", (core, physics_late), [(STEPS - 1, state, state)] * 2, types=(jnp.bfloat16,) * 2)
+    own_g, other_g, other_a, other_innov = call(
+        functools.partial(ahead_kernel, width_y),
+        "ahead",
+        (core, obs_column, mine, rest, other_late, beyond, *turned, nu_col),
+        [half, half, half, ((STEPS - 1) * count, state)],
+        types=(jnp.float32,) * 2 + (jnp.bfloat16,) * 2,
+    )
+    spreads = (own_a, other_a)
+    far_sent, near_sent, sums = call(
         functools.partial(second_kernel, width_y, members),
         "second",
-        (core, obs_column, mine, own_a, rest, other_late, beyond, physics[STEPS - 2], physics[STEPS - 3], modes_t, bands_col, nu_col, sums),
-        [half, half, sums_shape, half, ((STEPS - 1) * count, state)],
-        types=(jnp.float32,) * 3 + (jnp.bfloat16,) * 2,
-    )
-    known = (core, obs_column, mine, own_a, other_a, other_innov)
+        (core, *spreads, *turned, modes_t, bands_col, sums, own_g, other_g),
+        [half, half, sums_shape],
+    )
     for step in range(STEPS - 3, -1, -1):
-        far_sent, near_sent, sums = sent
         far = lax.ppermute(far_sent, ("member", "tile"), far_pairs)
         sums = lax.all_to_all(sums, "member", 0, 0, tiled=True, axis_index_groups=y_groups)
         near = lax.ppermute(near_sent, "member", swap)
         sums = jnp.broadcast_to(sums.sum(axis=0)[None], sums_shape)
         sums = lax.all_to_all(sums, "member", 0, 0, tiled=True, axis_index_groups=z_groups)
-        tail = (modes_t, bands_col, nu_col, sums, far_sent, near_sent, far, near)
+        own_g, other_g = call(
+            functools.partial(between_kernel, step, width_y),
+            f"between{step}",
+            (core, obs_column, mine, other_innov, nu_col, far_sent, near_sent, near),
+            [half, half],
+        )
         if step > 0:
-            sent = call(
+            far_sent, near_sent, sums = call(
                 functools.partial(step_kernel, step, width_y, members),
                 f"step{step}",
-                known + (physics[step - 1],) + tail,
+                (core, *spreads, *turned, modes_t, bands_col, nu_col, sums, own_g, other_g, far),
                 [half, half, sums_shape],
             )
-        else:
-            own, other = call(
-                functools.partial(last_kernel, step, width_y, members),
-                "last",
-                known + tail,
-                [half, half],
-            )
+    ends = []
+    for member, g in ((1, other_g), (0, own_g)):
+        (end,) = call(
+            functools.partial(last_kernel, member, width_y, members),
+            f"last{member}",
+            (core, spreads[member], modes_t, bands_col, nu_col, sums, g, far),
+            [half],
+        )
+        ends.append(end)
+    other, own = ends
     back = lax.ppermute(other, "member", swap)
     return call(functools.partial(finish_kernel, width_y), "finish", (core, own, back), [(1, *anomalies.shape[1:])])[0]
 

time: 104 us -> 106 us (1.019)
  blocking collectives: 28.2 us -> 13.7 us
  starting transfers between devices: 52.8 us -> 61.6 us
  waiting for transfers between devices: 9.47 us -> 15.1 us
  Pallas kernels: 9.27 us -> 10.8 us
    all_to_all x2 -> x0, blocking collectives: 13.9 us -> none  [per_device(): lax.all_to_all(sums, 'member', 0, 0, tiled=True, axis_index_groups=z_groups)]
    all_to_all x0 -> x2, waiting for transfers between devices: none -> 11.1 us  [per_device(): lax.all_to_all(sums, 'member', 0, 0, tiled=True, axis_index_groups=z_groups)]
    all_to_all x0 -> x2, starting transfers between devices: none -> 8.85 us  [per_device(): lax.all_to_all(sums, 'member', 0, 0, tiled=True, axis_index_groups=z_groups)]
    ppermute x1, waiting for transfers between devices: 6.04 us -> 1 us  [per_device(): beyond = lax.ppermute(beyond, ('member', 'tile'), far_pairs)]
    ppermute x2, starting transfers between devices: 8.1 us -> 4.81 us  [per_device(): far = lax.ppermute(far_sent, ('member', 'tile'), far_pairs)]
    ppermute x2, starting transfers between devices: 15.3 us -> 18.1 us  [per_device(): near = lax.ppermute(near_sent, 'member', swap)]
    pallas_call x8 -> x13, Pallas kernels: 9.27 us -> 10.8 us  [call(): pl.pallas_call(kernel, in_specs=[pl.BlockSpec(memory_space=space) for spa...]
    broadcast_in_dim x2, local copies, waits for them, and re-layouts: 0.01 us -> 1.27 us  [per_device(): sums = jnp.broadcast_to(sums.sum(axis=0)[None], sums_shape)]
  transfers between devices with their start and end apart: 10 -> 12, of which waited for: 3 -> 5; matrix products, arithmetic and copies ran while one was open for 1% -> 1% of each run, Pallas kernels for 1% -> 4%
where the time goes in v5:
time: 106 us; the launch traced here: 105 us
  starting transfers between devices  61.6 us (58%)
  waiting for transfers between devices  15.1 us (14%)
  blocking collectives  13.7 us (13%)
  Pallas kernels  10.8 us (10%)
  local copies, waits for them, and re-layouts  3.39 us (3%)
    ppermute x2, starting transfers between devices, per_device(): near = lax.ppermute(near_sent, 'member', swap)  18.1 us
    all_to_all x2, blocking collectives, per_device(): lax.all_to_all(sums, 'member', 0, 0, tiled=True, axis_index_groups=y_groups)  13.7 us
    all_to_all x2, waiting for transfers between devices, per_device(): lax.all_to_all(sums, 'member', 0, 0, tiled=True, axis_index_groups=z_groups)  11.1 us
    pallas_call x13, Pallas kernels, call(): pl.pallas_call(kernel, in_specs=[pl.BlockSpec(memory_space=space) for spa...  10.8 us
    all_to_all x2, starting transfers between devices, per_device(): lax.all_to_all(sums, 'member', 0, 0, tiled=True, axis_index_groups=z_groups)  8.85 us
    ppermute x1, starting transfers between devices, per_device(): other_late = lax.ppermute(late, 'member', swap)  8.75 us
    ppermute x1, starting transfers between devices, per_device(): beyond = lax.ppermute(beyond, ('member', 'tile'), far_pairs)  6.93 us
    ppermute x2, starting transfers between devices, per_device(): far = lax.ppermute(far_sent, ('member', 'tile'), far_pairs)  4.81 us
  transfers between devices with their start and end apart: 12, of which 5 were waited for; matrix products, arithmetic and copies ran while one was open for 1% of the time, Pallas kernels for 4%

profile of v5, /device:TPU:1, one launch (start us, length us, event | category | flops | bytes accessed | tf_op | source)
XLA Modules:
  0.0 104.8 jit_solution(8483974277456053733)
XLA Ops:
  0.0 3.1 %shard_map.73 = (f32[64,256]{1,0:T(8,128)}, f32[4,16,512]{2,1,0:T(8,128)}) custom-call(s32[1]{0:T(128)} %bitcast.core_ref, s32[4,64]{1,0:T(4,128)} %obs_ref.9, bf16[1,4,64,256]{3,2,1,0:T(8,128)(2,1)} %bitcast.5, bf16[1,256,4,128]{3,2,1,0:T(4,128)(2,1)} %anomalies_ref, f32[16,256]{1,0:T(8,128)} %bitcast.10), custom_call_target="tpu_custom_call" | custom-call | flops 400000000 | bytes 2000000 | tf_op jit(solution)/shard_map/pallas_call | solution.py:242
  3.1 8.7 %collective-permute-start = (f32[64,256]{1,0:T(8,128)}, f32[64,256]{1,0:T(8,128)S(1)}, u32[]{:S(2)}, u32[]{:S(2)}) collective-permute-start(f32[64,256]{1,0:T(8,128)} %get-tuple-element.28.late_ref), channel_id=1, source_target_pairs={{0,16},{16,0},{32,48},{48,32},{64,80},{80,64},{96,112},{112,96},{1... | collective-permute-start | bytes 196616 | tf_op jit(solution)/shard_map/ppermute | solution.py:291
  11.8 3.5 %all-to-all-start = ((f32[4,16,512]{2,1,0:T(8,128)}), f32[4,16,512]{2,1,0:T(8,128)S(1)}, u32[]{:S(2)}, u32[]{:S(2)}) async-start(f32[4,16,512]{2,1,0:T(8,128)} %get-tuple-element.37), calls=%async_computation | async-start | bytes 262144 | tf_op jit(solution)/shard_map/all_to_all | solution.py:290
  15.4 0.8 shard_map.74
  16.1 1.9 %collective-permute-start.1 = (f32[448,256]{1,0:T(8,128)S(1)}, f32[448,256]{1,0:T(8,128)S(1)}, u32[]{:S(2)}, u32[]{:S(2)}) collective-permute-start(f32[448,256]{1,0:T(8,128)S(1)} %get-tuple-element.32), channel_id=1, source_target_pairs={{0,16},{16,0},{32,48},{48,32},{64,80},{80,64},{96,112},{112,96},{1... | collective-permute-start | bytes 1376264 | tf_op jit(solution)/shard_map/ppermute | solution.py:304
  18.1 2.3 %all-to-all-done.sums_ref = f32[4,16,512]{2,1,0:T(8,128)S(1)} async-done(((f32[4,16,512]{2,1,0:T(8,128)}), f32[4,16,512]{2,1,0:T(8,128)S(1)}, u32[]{:S(2)}, u32[]{:S(2)}) %all-to-all-start) | async-done | bytes 131104 | tf_op jit(solution)/shard_map/all_to_all | solution.py:290
  20.3 0.7 shard_map.78
  21.0 4.6 %all-to-all-start.1 = ((f32[8,16,256]{2,1,0:T(8,128)}), f32[8,16,256]{2,1,0:T(8,128)S(1)}, u32[]{:S(2)}, u32[]{:S(2)}) async-start(f32[8,16,256]{2,1,0:T(8,128)} %shard_map.78), calls=%async_computation.1 | async-start | bytes 262144 | tf_op jit(solution)/shard_map/all_to_all | solution.py:295
  25.6 6.9 %collective-permute-start.2 = (f32[136,256]{1,0:T(8,128)S(1)}, f32[136,256]{1,0:T(8,128)S(1)}, u32[]{:S(2)}, u32[]{:S(2)}) collective-permute-start(f32[136,256]{1,0:T(8,128)S(1)} %shard_map.75), channel_id=1, source_target_pairs={{0,31},{1,16},{2,17},{3,18},{4,19},{5,20},{6,21},{7,22},{8,23},{9,... | collective-permute-start | bytes 417800 | tf_op jit(solution)/shard_map/ppermute | solution.py:293
  32.7 0.7 copy-done.7
  33.5 1.2 %copy-done.3 = f32[4,256,256]{2,1,0:T(8,128)S(1)} copy-done((f32[4,256,256]{2,1,0:T(8,128)S(1)}, f32[4,256,256]{2,1,0:T(8,128)}, u32[]{:S(2)}) %copy-start.3) | copy-done | bytes 1048600
  35.0 1.0 collective-permute-done.2.beyond_ref
  36.0 1.3 %shard_map.77 = (f32[256,256]{1,0:T(8,128)S(1)}, f32[256,256]{1,0:T(8,128)S(1)}, bf16[256,256]{1,0:T(8,128)(2,1)S(1)}, bf16[192,256]{1,0:T(8,128)(2,1)S(1)}) custom-call(s32[1]{0:T(128)} %bitcast.core_ref, s32[4,64]{1,0:T(4,128)S(1)} %copy-done.2, bf16[1,4,64,256]{3,2,1,0:T(8,128)(2,1)S(1)} %bitcast.7, f32[448,256]{1,0:T(8,128)S(1)} %collective-permute-done.1.rest_ref, ...), custom_call_target="tpu_custom_call" | custom-call | flops 400000000 | bytes 2000000 | tf_op jit(solution)/shard_map/pallas_call | solution.py:242
  37.3 0.9 shard_map.79
  38.2 9.4 %collective-permute-start.3 = (f32[256,256]{1,0:T(8,128)S(1)}, f32[256,256]{1,0:T(8,128)S(1)}, u32[]{:S(2)}, u32[]{:S(2)}) collective-permute-start(f32[256,256]{1,0:T(8,128)S(1)} %get-tuple-element.43.near_sent), channel_id=1, source_target_pairs={{0,16},{16,0},{32,48},{48,32},{64,80},{80,64},{96,112},{112,96},{1... | collective-permute-start | bytes 786440 | tf_op jit(solution)/shard_map/ppermute | solution.py:324
  47.5 2.9 %collective-permute-start.4 = (f32[256,256]{1,0:T(8,128)S(1)}, f32[256,256]{1,0:T(8,128)S(1)}, u32[]{:S(2)}, u32[]{:S(2)}) collective-permute-start(f32[256,256]{1,0:T(8,128)S(1)} %get-tuple-element.42.far_sent), channel_id=1, source_target_pairs={{0,31},{1,16},{2,17},{3,18},{4,19},{5,20},{6,21},{7,22},{8,23},{9,... | collective-permute-start | bytes 786440 | tf_op jit(solution)/shard_map/ppermute | solution.py:322
  50.4 6.8 %all_to_all.30 = f32[4,16,256]{2,1,0:T(8,128)S(1)} all-to-all(f32[4,16,256]{2,1,0:T(8,128)S(1)} %get-tuple-element.40), channel_id=1, replica_groups={{0,128,256,384},{16,144,272,400},{32,160,288,416},{48,176,304,432},{64,..., dimensions={0} | all-to-all | bytes 131072 | tf_op jit(solution)/shard_map/all_to_all | solution.py:323
  57.3 0.6 broadcast_in_dim.24
  57.9 5.6 %all-to-all-start.3 = ((f32[4,16,256]{2,1,0:T(8,128)}), f32[4,16,256]{2,1,0:T(8,128)S(1)}, u32[]{:S(2)}, u32[]{:S(2)}) async-start(f32[4,16,256]{2,1,0:T(8,128)} %broadcast_in_dim.24), calls=%async_computation.3 | async-start | bytes 131072 | tf_op jit(solution)/shard_map/all_to_all | solution.py:326
  63.5 0.5 shard_map.80
  64.0 4.2 %all-to-all-done.3.sums_ref = f32[4,16,256]{2,1,0:T(8,128)S(1)} async-done(((f32[4,16,256]{2,1,0:T(8,128)}), f32[4,16,256]{2,1,0:T(8,128)S(1)}, u32[]{:S(2)}, u32[]{:S(2)}) %all-to-all-start.3) | async-done | bytes 65568 | tf_op jit(solution)/shard_map/all_to_all | solution.py:326
  68.2 0.9 shard_map.81
  69.1 8.7 %collective-permute-start.5 = (f32[256,256]{1,0:T(8,128)S(1)}, f32[256,256]{1,0:T(8,128)S(1)}, u32[]{:S(2)}, u32[]{:S(2)}) collective-permute-start(f32[256,256]{1,0:T(8,128)S(1)} %get-tuple-element.48.near_sent), channel_id=1, source_target_pairs={{0,16},{16,0},{32,48},{48,32},{64,80},{80,64},{96,112},{112,96},{1... | collective-permute-start | bytes 786440 | tf_op jit(solution)/shard_map/ppermute | solution.py:324
  77.8 1.9 %collective-permute-start.6 = (f32[256,256]{1,0:T(8,128)S(1)}, f32[256,256]{1,0:T(8,128)S(1)}, u32[]{:S(2)}, u32[]{:S(2)}) collective-permute-start(f32[256,256]{1,0:T(8,128)S(1)} %get-tuple-element.47.far_sent), channel_id=1, source_target_pairs={{0,31},{1,16},{2,17},{3,18},{4,19},{5,20},{6,21},{7,22},{8,23},{9,... | collective-permute-start | bytes 786440 | tf_op jit(solution)/shard_map/ppermute | solution.py:322
  79.8 6.8 %all_to_all.31 = f32[4,16,256]{2,1,0:T(8,128)S(1)} all-to-all(f32[4,16,256]{2,1,0:T(8,128)S(1)} %get-tuple-element.46), channel_id=1, replica_groups={{0,128,256,384},{16,144,272,400},{32,160,288,416},{48,176,304,432},{64,..., dimensions={0} | all-to-all | bytes 131072 | tf_op jit(solution)/shard_map/all_to_all | solution.py:323
  86.6 0.6 broadcast_in_dim.25
  87.3 3.3 %all-to-all-start.5 = ((f32[4,16,256]{2,1,0:T(8,128)}), f32[4,16,256]{2,1,0:T(8,128)S(1)}, u32[]{:S(2)}, u32[]{:S(2)}) async-start(f32[4,16,256]{2,1,0:T(8,128)} %broadcast_in_dim.25), calls=%async_computation.5 | async-start | bytes 131072 | tf_op jit(solution)/shard_map/all_to_all | solution.py:326
  90.6 0.5 shard_map.82
  91.1 6.9 %all-to-all-done.5.sums_ref = f32[4,16,256]{2,1,0:T(8,128)S(1)} async-done(((f32[4,16,256]{2,1,0:T(8,128)}), f32[4,16,256]{2,1,0:T(8,128)S(1)}, u32[]{:S(2)}, u32[]{:S(2)}) %all-to-all-start.5) | async-done | bytes 65568 | tf_op jit(solution)/shard_map/all_to_all | solution.py:326
  98.3 4.2 %collective-permute-start.7 = (f32[256,256]{1,0:T(8,128)S(1)}, f32[256,256]{1,0:T(8,128)S(1)}, u32[]{:S(2)}, u32[]{:S(2)}) collective-permute-start(f32[256,256]{1,0:T(8,128)S(1)} %shard_map.84), channel_id=1, source_target_pairs={{0,16},{16,0},{32,48},{48,32},{64,80},{80,64},{96,112},{112,96},{1... | collective-permute-start | bytes 786440 | tf_op jit(solution)/shard_map/ppermute | solution.py:350
  103.0 0.7 collective-permute-done.7.back_ref
  103.7 1.1 %shard_map.85 = f32[1,256,4,128]{3,2,1,0:T(4,128)} custom-call(s32[1]{0:T(128)} %bitcast.core_ref, f32[256,256]{1,0:T(8,128)S(1)} %shard_map.83.own_ref, f32[256,256]{1,0:T(8,128)S(1)} %collective-permute-done.7.back_ref), custom_call_target="tpu_custom_call" | custom-call | flops 400000000 | bytes 2000000 | tf_op jit(solution)/shard_map/pallas_call | solution.py:242
  (29 shorter events, 1.4 us)
Async XLA Ops:
  0.0 15.3 %copy-start.4 = (bf16[1,256,4,128]{3,2,1,0:T(4,128)(2,1)S(1)}, bf16[1,256,4,128]{3,2,1,0:T(4,128)(2,1)}, u32[]{:S(2)}) copy-start(bf16[1,256,4,128]{3,2,1,0:T(4,128)(2,1)} %anomalies_ref) | copy-start | bytes 786436
  3.1 12.2 %collective-permute-start = (f32[64,256]{1,0:T(8,128)}, f32[64,256]{1,0:T(8,128)S(1)}, u32[]{:S(2)}, u32[]{:S(2)}) collective-permute-start(f32[64,256]{1,0:T(8,128)} %get-tuple-element.28.late_ref), channel_id=1, source_target_pairs={{0,16},{16,0},{32,48},{48,32},{64,80},{80,64},{96,112},{112,96},{1... | collective-permute-start | bytes 196616 | tf_op jit(solution)/shard_map/ppermute | solution.py:291
  11.8 3.5 %copy-start = (bf16[1,4,256,64]{2,3,1,0:T(8,128)(2,1)S(1)}, bf16[1,4,256,64]{2,3,1,0:T(8,128)(2,1)}, u32[]{:S(2)}) copy-start(bf16[1,4,256,64]{2,3,1,0:T(8,128)(2,1)} %param.7) | copy-start | bytes 393220
  11.8 8.5 %all-to-all-start = ((f32[4,16,512]{2,1,0:T(8,128)}), f32[4,16,512]{2,1,0:T(8,128)S(1)}, u32[]{:S(2)}, u32[]{:S(2)}) async-start(f32[4,16,512]{2,1,0:T(8,128)} %get-tuple-element.37), calls=%async_computation | async-start | bytes 262144 | tf_op jit(solution)/shard_map/all_to_all | solution.py:290
  16.1 19.8 %collective-permute-start.1 = (f32[448,256]{1,0:T(8,128)S(1)}, f32[448,256]{1,0:T(8,128)S(1)}, u32[]{:S(2)}, u32[]{:S(2)}) collective-permute-start(f32[448,256]{1,0:T(8,128)S(1)} %get-tuple-element.32), channel_id=1, source_target_pairs={{0,16},{16,0},{32,48},{48,32},{64,80},{80,64},{96,112},{112,96},{1... | collective-permute-start | bytes 1376264 | tf_op jit(solution)/shard_map/ppermute | solution.py:304
  21.0 4.6 %copy-start.2 = (s32[4,64]{1,0:T(4,128)S(1)}, s32[4,64]{1,0:T(4,128)}, u32[]{:S(2)}) copy-start(s32[4,64]{1,0:T(4,128)} %obs_ref.9) | copy-start | bytes 3076
  21.0 4.6 %copy-start.5 = (f32[64,256]{1,0:T(8,128)S(1)}, f32[64,256]{1,0:T(8,128)}, u32[]{:S(2)}) copy-start(f32[64,256]{1,0:T(8,128)} %get-tuple-element.28.late_ref) | copy-start | bytes 196612
  21.0 16.2 %all-to-all-start.1 = ((f32[8,16,256]{2,1,0:T(8,128)}), f32[8,16,256]{2,1,0:T(8,128)S(1)}, u32[]{:S(2)}, u32[]{:S(2)}) async-start(f32[8,16,256]{2,1,0:T(8,128)} %shard_map.78), calls=%async_computation.1 | async-start | bytes 262144 | tf_op jit(solution)/shard_map/all_to_all | solution.py:295
  25.6 7.0 %copy-start.6 = (f32[256]{0:T(256)S(1)}, f32[256]{0:T(256)}, u32[]{:S(2)}) copy-start(f32[256]{0:T(256)} %param.10) | copy-start | bytes 3076
  25.6 10.3 %collective-permute-start.2 = (f32[136,256]{1,0:T(8,128)S(1)}, f32[136,256]{1,0:T(8,128)S(1)}, u32[]{:S(2)}, u32[]{:S(2)}) collective-permute-start(f32[136,256]{1,0:T(8,128)S(1)} %shard_map.75), channel_id=1, source_target_pairs={{0,31},{1,16},{2,17},{3,18},{4,19},{5,20},{6,21},{7,22},{8,23},{9,... | collective-permute-start | bytes 417800 | tf_op jit(solution)/shard_map/ppermute | solution.py:293
  32.7 0.7 copy-start.7
  33.5 1.2 %copy-start.3 = (f32[4,256,256]{2,1,0:T(8,128)S(1)}, f32[4,256,256]{2,1,0:T(8,128)}, u32[]{:S(2)}) copy-start(f32[4,256,256]{2,1,0:T(8,128)} %physics_ref) | copy-start | bytes 3145732
  36.0 1.3 %copy-start.1 = (f32[256,16]{0,1:T(8,128)S(1)}, f32[256,16]{0,1:T(8,128)}, u32[]{:S(2)}) copy-start(f32[256,16]{0,1:T(8,128)} %param.12) | copy-start | bytes 49156
  38.2 25.3 %collective-permute-start.3 = (f32[256,256]{1,0:T(8,128)S(1)}, f32[256,256]{1,0:T(8,128)S(1)}, u32[]{:S(2)}, u32[]{:S(2)}) collective-permute-start(f32[256,256]{1,0:T(8,128)S(1)} %get-tuple-element.43.near_sent), channel_id=1, source_target_pairs={{0,16},{16,0},{32,48},{48,32},{64,80},{80,64},{96,112},{112,96},{1... | collective-permute-start | bytes 786440 | tf_op jit(solution)/shard_map/ppermute | solution.py:324
  47.5 20.6 %collective-permute-start.4 = (f32[256,256]{1,0:T(8,128)S(1)}, f32[256,256]{1,0:T(8,128)S(1)}, u32[]{:S(2)}, u32[]{:S(2)}) collective-permute-start(f32[256,256]{1,0:T(8,128)S(1)} %get-tuple-element.42.far_sent), channel_id=1, source_target_pairs={{0,31},{1,16},{2,17},{3,18},{4,19},{5,20},{6,21},{7,22},{8,23},{9,... | collective-permute-start | bytes 786440 | tf_op jit(solution)/shard_map/ppermute | solution.py:322
  57.9 10.3 %all-to-all-start.3 = ((f32[4,16,256]{2,1,0:T(8,128)}), f32[4,16,256]{2,1,0:T(8,128)S(1)}, u32[]{:S(2)}, u32[]{:S(2)}) async-start(f32[4,16,256]{2,1,0:T(8,128)} %broadcast_in_dim.24), calls=%async_computation.3 | async-start | bytes 131072 | tf_op jit(solution)/shard_map/all_to_all | solution.py:326
  69.1 21.4 %collective-permute-start.5 = (f32[256,256]{1,0:T(8,128)S(1)}, f32[256,256]{1,0:T(8,128)S(1)}, u32[]{:S(2)}, u32[]{:S(2)}) collective-permute-start(f32[256,256]{1,0:T(8,128)S(1)} %get-tuple-element.48.near_sent), channel_id=1, source_target_pairs={{0,16},{16,0},{32,48},{48,32},{64,80},{80,64},{96,112},{112,96},{1... | collective-permute-start | bytes 786440 | tf_op jit(solution)/shard_map/ppermute | solution.py:324
  77.8 20.1 %collective-permute-start.6 = (f32[256,256]{1,0:T(8,128)S(1)}, f32[256,256]{1,0:T(8,128)S(1)}, u32[]{:S(2)}, u32[]{:S(2)}) collective-permute-start(f32[256,256]{1,0:T(8,128)S(1)} %get-tuple-element.47.far_sent), channel_id=1, source_target_pairs={{0,31},{1,16},{2,17},{3,18},{4,19},{5,20},{6,21},{7,22},{8,23},{9,... | collective-permute-start | bytes 786440 | tf_op jit(solution)/shard_map/ppermute | solution.py:322
  87.3 10.7 %all-to-all-start.5 = ((f32[4,16,256]{2,1,0:T(8,128)}), f32[4,16,256]{2,1,0:T(8,128)S(1)}, u32[]{:S(2)}, u32[]{:S(2)}) async-start(f32[4,16,256]{2,1,0:T(8,128)} %broadcast_in_dim.25), calls=%async_computation.5 | async-start | bytes 131072 | tf_op jit(solution)/shard_map/all_to_all | solution.py:326
  98.3 5.4 %collective-permute-start.7 = (f32[256,256]{1,0:T(8,128)S(1)}, f32[256,256]{1,0:T(8,128)S(1)}, u32[]{:S(2)}, u32[]{:S(2)}) collective-permute-start(f32[256,256]{1,0:T(8,128)S(1)} %shard_map.84), channel_id=1, source_target_pairs={{0,16},{16,0},{32,48},{48,32},{64,80},{80,64},{96,112},{112,96},{1... | collective-permute-start | bytes 786440 | tf_op jit(solution)/shard_map/ppermute | solution.py:350

commit v6 on v4

--- a/solution.py
+++ b/solution.py
@@ -72,7 +72,9 @@
     hot = jnp.concatenate([(obs_row == x * w + y).astype(jnp.bfloat16) for x in order], axis=0)
     copies[0].wait()
     values = mine_ref[...]
-    late_ref[...] = values.astype(jnp.float32)
+    late_ref[:count, :] = values.astype(jnp.float32)
+    late_ref[count:, :] = jnp.zeros((late_ref.shape[0] - count, late_ref.shape[1]), jnp.float32)
+    late_ref[count : count + 1, :count] = obs_row.astype(jnp.float32)
     lam = placed(values, hot)
     copies[1].wait()
     spread = jnp.concatenate([anomalies_ref[0, :, x, :].astype(jnp.float32) for x in order], axis=1)
@@ -90,16 +92,8 @@
     for i in range(2):
         own_a_ref[:, i * w : (i + 1) * w] = jnp.where(low, rows[i], rows[3 - i]).astype(jnp.bfloat16)
         rest_ref[:state, i * w : (i + 1) * w] = jnp.where(low, rows[3 - i], rows[i])
-    for t in range(STEPS - 1):
+    for t in range(STEPS):
         rest_ref[state + t * count : state + (t + 1) * count, :] = mine_ref[0, t].astype(jnp.float32)
-
-
-def pass_on_kernel(core_ref, obs_ref, late_ref, other_ref, far_ref):
-    count = late_ref.shape[0]
-    far_ref[:count, :] = late_ref[...]
-    far_ref[count : 2 * count, :] = other_ref[...]
-    far_ref[2 * count :, :] = jnp.zeros((far_ref.shape[0] - 2 * count, far_ref.shape[1]), jnp.float32)
-    far_ref[2 * count : 2 * count + 1, :count] = obs_ref[STEPS - 1 : STEPS, :].astype(jnp.float32)
 
 
 def regroup_kernel(core_ref, sums_ref, out_ref):
@@ -168,7 +162,7 @@
     return advance(moved, spread, force, smooth, modes_ref, nu_ref, w), spread
 
 
-def second_kernel(width_y, members, core_ref, obs_ref, mine_ref, own_a_ref, rest_ref, late_ref, beyond_ref, first_matrix, matrix,
+def second_kernel(width_y, members, core_ref, obs_ref, mine_ref, own_a_ref, rest_ref, own_beyond_ref, other_beyond_ref, first_matrix, matrix,
                   modes_ref, bands_ref, nu_ref, sums_ref,
                   far_out, near_out, sums_out, other_a_ref, other_ref):
     step = STEPS - 2
@@ -177,12 +171,13 @@
     state = own_a_ref.shape[0]
     count = obs_ref.shape[1]
     other_a_ref[...] = rest_ref[:state, :].astype(jnp.bfloat16)
-    other_ref[...] = rest_ref[state:, :].astype(jnp.bfloat16)
+    other = rest_ref[state:, :].astype(jnp.bfloat16)
+    other_ref[...] = other[: (STEPS - 1) * count]
     spread = both_spreads(own_a_ref, other_a_ref)
     hot = hot_rows(core, obs_ref[STEPS - 1 : STEPS, :], (0, 1, 2), w)
-    far_hot = hot_rows(core, beyond_ref[2 * count : 2 * count + 1, :count].astype(jnp.int32), (3,), w)
-    inside = (mine_ref[0, STEPS - 1], late_ref[...].astype(jnp.bfloat16))
-    beyond = [beyond_ref[(1 - m) * count : (2 - m) * count, :].astype(jnp.bfloat16) for m in range(2)]
+    far_hot = hot_rows(core, own_beyond_ref[count : count + 1, :count].astype(jnp.int32), (3,), w)
+    inside = (mine_ref[0, STEPS - 1], other[(STEPS - 1) * count :])
+    beyond = [ref[:count, :].astype(jnp.bfloat16) for ref in (own_beyond_ref, other_beyond_ref)]
     turned = first_matrix[...]
     moved = []
     for m in range(2):
@@ -206,12 +201,20 @@
     send_parts(lam, spread, matrix, modes_ref, far_out, near_out, sums_out, width_y)
 
 
-def last_kernel(step, width_y, members, core_ref, obs_ref, mine_ref, own_a_ref, other_a_ref, other_ref,
-                modes_ref, bands_ref, nu_ref, sums_ref, far_sent, near_sent, far_ref, near_ref, own_out, other_out):
-    lam, _ = next_lam(step, width_y, members, core_ref, obs_ref, mine_ref, own_a_ref, other_a_ref, other_ref,
-                      modes_ref, bands_ref, nu_ref, sums_ref, far_sent, near_sent, far_ref, near_ref)
-    own_out[...] = lam[0]
-    other_out[...] = lam[1]
+def last_kernel(member, step, width_y, members, core_ref, obs_ref, values_ref, a_ref, modes_ref, bands_ref, nu_ref, sums_ref,
+                far_sent, near_sent, far_ref, near_ref, out_ref):
+    w = width_y
+    total = sums_ref[0] + sums_ref[1] + sums_ref[2] + sums_ref[3]
+    lifted = dot(modes_ref[...], smooth_of(total, bands_ref[...], w, members), TM)
+    count = obs_ref.shape[1]
+    values = values_ref[step * count : (step + 1) * count, :] if member else values_ref[0, step]
+    force = placed(values, hot_rows(core_ref[0], obs_ref[step : step + 1, :], (0, 1), w))
+    nu = nu_ref[...]
+    cut = lambda ref, m: ref[:, m * w : (m + 1) * w]
+    far, near, out_near, out_far = cut(far_sent, member), cut(near_sent, member), cut(near_ref, 1 - member), cut(far_ref, 1 - member)
+    v_far = far + nu * (out_far + near + beside(far, w) - 4.0 * far)
+    v_near = near + nu * (far + out_near + beside(near, w) - 4.0 * near)
+    out_ref[...] = jnp.concatenate([v_far, v_near], axis=1) + a_ref[...].astype(jnp.float32) * lifted + force
 
 
 def finish_kernel(width_y, core_ref, own_ref, back_ref, out_ref):
@@ -251,10 +254,12 @@
 
     swap = [(i, i ^ 1) for i in range(members)]
     far_pairs = []
+    along_pairs = []
     for m in range(members):
         for t in range(tiles):
-            target = (t + 1) % tiles if m % 2 else (t - 1) % tiles
-            far_pairs.append((m * tiles + t, (m ^ 1) * tiles + target))
+            after, before = (t + 1) % tiles, (t - 1) % tiles
+            far_pairs.append((m * tiles + t, (m ^ 1) * tiles + (after if m % 2 else before)))
+            along_pairs.append((m * tiles + t, m * tiles + (before if m % 2 else after)))
     side = 2 * PLANES
     y_groups = [[side * y + j for y in range(PLANES)] for j in range(side)]
     z_groups = [[side * y + 2 * z + c for z in range(PLANES)] for y in range(PLANES) for c in range(2)]
@@ -268,7 +273,7 @@
         functools.partial(prepare_kernel, width_y),
         "prepare",
         (core, obs_column, mine, anomalies, modes_t),
-        [(count, state), (PLANES, n_modes, 4 * width_y)],
+        [(count + 8, state), (PLANES, n_modes, 4 * width_y)],
         hbm=(2, 3),
         scratch=(
             pltpu.VMEM((count, state), mine.dtype),
@@ -277,24 +282,23 @@
         ),
     )
     sums = lax.all_to_all(sums, "member", 0, 0, tiled=True, axis_index_groups=y_groups)
-    other_late = lax.ppermute(late, "member", swap)
-    (beyond,) = call(pass_on_kernel, "pass_on", (core, obs_column, late, other_late), [(2 * count + 8, state)])
-    beyond = lax.ppermute(beyond, ("member", "tile"), far_pairs)
+    own_beyond = lax.ppermute(late, ("member", "tile"), along_pairs)
+    other_beyond = lax.ppermute(late, ("member", "tile"), far_pairs)
     (sums,) = call(regroup_kernel, "regroup", (core, sums), [(side, n_modes, 2 * width_y)])
     sums = lax.all_to_all(sums, "member", 0, 0, tiled=True, axis_index_groups=chip_groups)
-    mine_late, anomalies_late, _ = lax.optimization_barrier((mine, anomalies, other_late))
+    mine_late, anomalies_late, _ = lax.optimization_barrier((mine, anomalies, late))
     own_a, rest = call(
         functools.partial(divide_kernel, width_y),
         "divide",
         (core, mine_late, anomalies_late),
-        [half, (state + (STEPS - 1) * count, 2 * width_y)],
+        [half, (state + STEPS * count, 2 * width_y)],
         types=(jnp.bfloat16, jnp.float32),
     )
     rest = lax.ppermute(rest, "member", swap)
     *sent, other_a, other_innov = call(
         functools.partial(second_kernel, width_y, members),
         "second",
-        (core, obs_column, mine, own_a, rest, other_late, beyond, physics[STEPS - 2], physics[STEPS - 3], modes_t, bands_col, nu_col, sums),
+        (core, obs_column, mine, own_a, rest, own_beyond, other_beyond, physics[STEPS - 2], physics[STEPS - 3], modes_t, bands_col, nu_col, sums),
         [half, half, sums_shape, half, ((STEPS - 1) * count, state)],
         types=(jnp.float32,) * 3 + (jnp.bfloat16,) * 2,
     )
@@ -314,13 +318,16 @@
                 known + (physics[step - 1],) + tail,
                 [half, half, sums_shape],
             )
-        else:
-            own, other = call(
-                functools.partial(last_kernel, step, width_y, members),
-                "last",
-                known + tail,
-                [half, half],
-            )
+    ends = []
+    for member, values, a in ((1, other_innov, other_a), (0, mine, own_a)):
+        (end,) = call(
+            functools.partial(last_kernel, member, 0, width_y, members),
+            f"last{member}",
+            (core, obs_column, values, a) + tail,
+            [half],
+        )
+        ends.append(end)
+    other, own = ends
     back = lax.ppermute(other, "member", swap)
     return call(functools.partial(finish_kernel, width_y), "finish", (core, own, back), [(1, *anomalies.shape[1:])])[0]
 

time: 104 us -> 105 us (level)
  waiting for transfers between devices: 9.47 us -> 1.87 us
  starting transfers between devices: 52.8 us -> 58.3 us
  blocking collectives: 28.2 us -> 31.3 us
    ppermute x1, starting transfers between devices: 1.92 us -> 7.1 us  [per_device(): rest = lax.ppermute(rest, 'member', swap)]
    ppermute x2, waiting for transfers between devices: 6.05 us -> 1.21 us  [the longest x1 1.21 us: per_device(): own_beyond = lax.ppermute(late, ('member', 'tile'), along_pairs)]
    all_to_all x2, blocking collectives: 13.9 us -> 17.3 us  [per_device(): lax.all_to_all(sums, 'member', 0, 0, tiled=True, axis_index_groups=z_groups)]
    ppermute x2, starting transfers between devices: 15.3 us -> 11.9 us  [per_device(): near = lax.ppermute(near_sent, 'member', swap)]
    ppermute x2, starting transfers between devices: 15.7 us -> 12.4 us  [the longest x1 7.16 us: per_device(): other_beyond = lax.ppermute(late, ('member', 'tile'), far_pairs)]
    ppermute x2, starting transfers between devices: 8.1 us -> 10.9 us  [per_device(): far = lax.ppermute(far_sent, ('member', 'tile'), far_pairs)]
    all_to_all x1, waiting for transfers between devices: 2.27 us -> 0.01 us  [per_device(): lax.all_to_all(sums, 'member', 0, 0, tiled=True, axis_index_groups=y_groups)]
    all_to_all x1, starting transfers between devices: 4.44 us -> 6.61 us  [per_device(): lax.all_to_all(sums, 'member', 0, 0, tiled=True, axis_index_groups=chip_g...]
  transfers between devices with their start and end apart: 10 -> 10, of which waited for: 3 -> 2; matrix products, arithmetic and copies ran while one was open for 1% -> 1% of each run, Pallas kernels for 1% -> 2%
where the time goes in v6:
time: 105 us
  starting transfers between devices  58.3 us (56%)
  blocking collectives  31.3 us (30%)
  Pallas kernels  9.52 us (9%)
  local copies, waits for them, and re-layouts  3.41 us (3%)
  waiting for transfers between devices  1.87 us (2%)
    all_to_all x2, blocking collectives, per_device(): lax.all_to_all(sums, 'member', 0, 0, tiled=True, axis_index_groups=z_groups)  17.3 us
    all_to_all x2, blocking collectives, per_device(): lax.all_to_all(sums, 'member', 0, 0, tiled=True, axis_index_groups=y_groups)  14 us
    ppermute x2, starting transfers between devices, per_device(): near = lax.ppermute(near_sent, 'member', swap)  11.9 us
    ppermute x2, starting transfers between devices, per_device(): far = lax.ppermute(far_sent, ('member', 'tile'), far_pairs)  10.9 us
    pallas_call x8, Pallas kernels, call(): pl.pallas_call(kernel, in_specs=[pl.BlockSpec(memory_space=space) for spa...  9.52 us
    ppermute x1, starting transfers between devices, per_device(): other_beyond = lax.ppermute(late, ('member', 'tile'), far_pairs)  7.16 us
    ppermute x1, starting transfers between devices, per_device(): rest = lax.ppermute(rest, 'member', swap)  7.1 us
    all_to_all x1, starting transfers between devices, per_device(): lax.all_to_all(sums, 'member', 0, 0, tiled=True, axis_index_groups=chip_g...  6.61 us
  transfers between devices with their start and end apart: 10, of which 2 were waited for; matrix products, arithmetic and copies ran while one was open for 1% of the time, Pallas kernels for 2%

profile of v6, /device:TPU:1, one launch (start us, length us, event | category | flops | bytes accessed | tf_op | source)
XLA Modules:
  0.0 104.6 jit_solution(177275076106797308)
XLA Ops:
  0.0 3.1 %shard_map.73 = (f32[72,256]{1,0:T(8,128)}, f32[4,16,512]{2,1,0:T(8,128)}) custom-call(s32[1]{0:T(128)} %bitcast.core_ref, s32[4,64]{1,0:T(4,128)} %obs_ref.9, bf16[1,4,64,256]{3,2,1,0:T(8,128)(2,1)} %bitcast.11, bf16[1,256,4,128]{3,2,1,0:T(4,128)(2,1)} %anomalies_ref, f32[16,256]{1,0:T(8,128)} %bitcast.16), custom_call_target="tpu_custom_call" | custom-call | flops 400000000 | bytes 2000000 | tf_op jit(solution)/shard_map/pallas_call | solution.py:234
  3.1 0.0 copy-start
  3.1 5.1 %all-to-all-start = ((f32[4,16,512]{2,1,0:T(8,128)}), f32[4,16,512]{2,1,0:T(8,128)S(1)}, u32[]{:S(2)}, u32[]{:S(2)}) async-start(f32[4,16,512]{2,1,0:T(8,128)} %get-tuple-element.24), calls=%async_computation | async-start | bytes 262144 | tf_op jit(solution)/shard_map/all_to_all | solution.py:284
  8.2 0.8 shard_map.74
  9.0 7.1 %collective-permute-start = (f32[512,256]{1,0:T(8,128)S(1)}, f32[512,256]{1,0:T(8,128)S(1)}, u32[]{:S(2)}, u32[]{:S(2)}) collective-permute-start(f32[512,256]{1,0:T(8,128)S(1)} %get-tuple-element.23), channel_id=1, source_target_pairs={{0,16},{16,0},{32,48},{48,32},{64,80},{80,64},{96,112},{112,96},{1... | collective-permute-start | bytes 1572872 | tf_op jit(solution)/shard_map/ppermute | solution.py:297
  16.1 0.7 shard_map.75
  16.8 6.6 %all-to-all-start.1 = ((f32[8,16,256]{2,1,0:T(8,128)}), f32[8,16,256]{2,1,0:T(8,128)S(1)}, u32[]{:S(2)}, u32[]{:S(2)}) async-start(f32[8,16,256]{2,1,0:T(8,128)} %shard_map.75), calls=%async_computation.1 | async-start | bytes 262144 | tf_op jit(solution)/shard_map/all_to_all | solution.py:288
  23.4 7.2 %collective-permute-start.2 = (f32[72,256]{1,0:T(8,128)S(1)}, f32[72,256]{1,0:T(8,128)S(1)}, u32[]{:S(2)}, u32[]{:S(2)}) collective-permute-start(f32[72,256]{1,0:T(8,128)S(1)} %copy-done.6), channel_id=1, source_target_pairs={{0,31},{1,16},{2,17},{3,18},{4,19},{5,20},{6,21},{7,22},{8,23},{9,... | collective-permute-start | bytes 221192 | tf_op jit(solution)/shard_map/ppermute | solution.py:286
  30.6 5.2 %collective-permute-start.1 = (f32[72,256]{1,0:T(8,128)S(1)}, f32[72,256]{1,0:T(8,128)S(1)}, u32[]{:S(2)}, u32[]{:S(2)}) collective-permute-start(f32[72,256]{1,0:T(8,128)S(1)} %copy-done.6), channel_id=1, source_target_pairs={{0,1},{1,2},{2,3},{3,4},{4,5},{5,6},{6,7},{7,8},{8,9},{9,10},{10,1... | collective-permute-start | bytes 221192 | tf_op jit(solution)/shard_map/ppermute | solution.py:285
  35.8 1.2 %slice_bitcast_fusion = (f32[256,256]{1,0:T(8,128)S(1)}, f32[256,256]{1,0:T(8,128)S(1)}, f32[256,256]{1,0:T(8,128)S(1)}) fusion(f32[4,256,256]{2,1,0:T(8,128)} %param.9), kind=kLoop, calls=%fused_computation | loop fusion | bytes 1572864 | tf_op jit(solution)/shard_map/squeeze | solution.py:318
  37.0 0.0 copy-start.5
  37.0 0.6 copy-done.5
  37.7 0.1 copy.16.bands_ref
  37.7 0.7 copy-done.4
  38.4 0.1 copy.17.nu_ref
  38.6 1.2 %collective-permute-done.1.own_beyond_ref = f32[72,256]{1,0:T(8,128)S(1)} collective-permute-done((f32[72,256]{1,0:T(8,128)S(1)}, f32[72,256]{1,0:T(8,128)S(1)}, u32[]{:S(2)}, u32[]{:S(2)}) %collective-permute-start.1) | collective-permute-done | bytes 73760 | tf_op jit(solution)/shard_map/ppermute | solution.py:285
  39.8 0.7 copy-done.2
  40.5 1.7 %shard_map.76 = (f32[256,256]{1,0:T(8,128)S(1)}, f32[256,256]{1,0:T(8,128)S(1)}, f32[4,16,256]{2,1,0:T(8,128)S(1)}, bf16[256,256]{1,0:T(8,128)(2,1)S(1)}, bf16[192,256]{1,0:T(8,128)(2,1)S(1)}) custom-call(s32[1]{0:T(128)} %bitcast.core_ref, s32[4,64]{1,0:T(4,128)S(1)} %copy-done.2, bf16[1,4,64,256]{3,2,1,0:T(8,128)(2,1)S(1)} %bitcast.13, ...), custom_call_target="tpu_custom_call" | custom-call | flops 400000000 | bytes 2000000 | tf_op jit(solution)/shard_map/pallas_call | solution.py:234
  42.2 6.4 %collective-permute-start.3 = (f32[256,256]{1,0:T(8,128)S(1)}, f32[256,256]{1,0:T(8,128)S(1)}, u32[]{:S(2)}, u32[]{:S(2)}) collective-permute-start(f32[256,256]{1,0:T(8,128)S(1)} %get-tuple-element.28.far_sent), channel_id=1, source_target_pairs={{0,31},{1,16},{2,17},{3,18},{4,19},{5,20},{6,21},{7,22},{8,23},{9,... | collective-permute-start | bytes 786440 | tf_op jit(solution)/shard_map/ppermute | solution.py:308
  48.6 4.9 %collective-permute-start.4 = (f32[256,256]{1,0:T(8,128)S(1)}, f32[256,256]{1,0:T(8,128)S(1)}, u32[]{:S(2)}, u32[]{:S(2)}) collective-permute-start(f32[256,256]{1,0:T(8,128)S(1)} %get-tuple-element.29.near_sent), channel_id=1, source_target_pairs={{0,16},{16,0},{32,48},{48,32},{64,80},{80,64},{96,112},{112,96},{1... | collective-permute-start | bytes 786440 | tf_op jit(solution)/shard_map/ppermute | solution.py:310
  53.5 7.1 %all_to_all.30 = f32[4,16,256]{2,1,0:T(8,128)S(1)} all-to-all(f32[4,16,256]{2,1,0:T(8,128)S(1)} %get-tuple-element.27), channel_id=1, replica_groups={{0,128,256,384},{16,144,272,400},{32,160,288,416},{48,176,304,432},{64,..., dimensions={0} | all-to-all | bytes 131072 | tf_op jit(solution)/shard_map/all_to_all | solution.py:309
  60.7 10.4 %all_to_all.31.sums_ref = f32[4,16,256]{2,1,0:T(8,128)S(1)} all-to-all(f32[4,16,256]{2,1,0:T(8,128)S(1)} %broadcast_in_dim.24), channel_id=1, replica_groups={{0,32,64,96},{16,48,80,112},{128,160,192,224},{144,176,208,240},{256,28..., dimensions={0} | all-to-all | bytes 131072 | tf_op jit(solution)/shard_map/all_to_all | solution.py:312
  71.0 1.2 %shard_map.77 = (f32[256,256]{1,0:T(8,128)S(1)}, f32[256,256]{1,0:T(8,128)S(1)}, f32[4,16,256]{2,1,0:T(8,128)S(1)}) custom-call(s32[1]{0:T(128)} %bitcast.core_ref, s32[4,64]{1,0:T(4,128)S(1)} %copy-done.2, bf16[1,4,64,256]{3,2,1,0:T(8,128)(2,1)S(1)} %bitcast.14, bf16[256,256]{1,0:T(8,128)(2,1)S(1)} %get-tuple-element.22.own_a_ref.a_ref, ...), custom_call_target="tpu_custom_call" | custom-call | flops 400000000 | bytes 2000000 | tf_op jit(solution)/shard_map/pallas_call | solution.py:234
  72.2 4.5 %collective-permute-start.5 = (f32[256,256]{1,0:T(8,128)S(1)}, f32[256,256]{1,0:T(8,128)S(1)}, u32[]{:S(2)}, u32[]{:S(2)}) collective-permute-start(f32[256,256]{1,0:T(8,128)S(1)} %get-tuple-element.31.far_sent), channel_id=1, source_target_pairs={{0,31},{1,16},{2,17},{3,18},{4,19},{5,20},{6,21},{7,22},{8,23},{9,... | collective-permute-start | bytes 786440 | tf_op jit(solution)/shard_map/ppermute | solution.py:308
  76.7 7.0 %collective-permute-start.6 = (f32[256,256]{1,0:T(8,128)S(1)}, f32[256,256]{1,0:T(8,128)S(1)}, u32[]{:S(2)}, u32[]{:S(2)}) collective-permute-start(f32[256,256]{1,0:T(8,128)S(1)} %get-tuple-element.32.near_sent), channel_id=1, source_target_pairs={{0,16},{16,0},{32,48},{48,32},{64,80},{80,64},{96,112},{112,96},{1... | collective-permute-start | bytes 786440 | tf_op jit(solution)/shard_map/ppermute | solution.py:310
  83.8 6.9 %all_to_all.32 = f32[4,16,256]{2,1,0:T(8,128)S(1)} all-to-all(f32[4,16,256]{2,1,0:T(8,128)S(1)} %get-tuple-element.30), channel_id=1, replica_groups={{0,128,256,384},{16,144,272,400},{32,160,288,416},{48,176,304,432},{64,..., dimensions={0} | all-to-all | bytes 131072 | tf_op jit(solution)/shard_map/all_to_all | solution.py:309
  90.7 7.0 %all_to_all.33.sums_ref = f32[4,16,256]{2,1,0:T(8,128)S(1)} all-to-all(f32[4,16,256]{2,1,0:T(8,128)S(1)} %broadcast_in_dim.25), channel_id=1, replica_groups={{0,32,64,96},{16,48,80,112},{128,160,192,224},{144,176,208,240},{256,28..., dimensions={0} | all-to-all | bytes 131072 | tf_op jit(solution)/shard_map/all_to_all | solution.py:312
  97.7 0.5 shard_map.79
  98.2 4.2 %collective-permute-start.7 = (f32[256,256]{1,0:T(8,128)S(1)}, f32[256,256]{1,0:T(8,128)S(1)}, u32[]{:S(2)}, u32[]{:S(2)}) collective-permute-start(f32[256,256]{1,0:T(8,128)S(1)} %shard_map.79), channel_id=1, source_target_pairs={{0,16},{16,0},{32,48},{48,32},{64,80},{80,64},{96,112},{112,96},{1... | collective-permute-start | bytes 786440 | tf_op jit(solution)/shard_map/ppermute | solution.py:331
  102.4 0.5 shard_map.78.own_ref
  102.9 0.6 collective-permute-done.7.back_ref
  103.5 1.1 %shard_map.80 = f32[1,256,4,128]{3,2,1,0:T(4,128)} custom-call(s32[1]{0:T(128)} %bitcast.core_ref, f32[256,256]{1,0:T(8,128)S(1)} %shard_map.78.own_ref, f32[256,256]{1,0:T(8,128)S(1)} %collective-permute-done.7.back_ref), custom_call_target="tpu_custom_call" | custom-call | flops 400000000 | bytes 2000000 | tf_op jit(solution)/shard_map/pallas_call | solution.py:234
  (21 shorter events, 0.1 us)
Async XLA Ops:
  0.0 8.2 %copy-start.3 = (bf16[1,256,4,128]{3,2,1,0:T(4,128)(2,1)S(1)}, bf16[1,256,4,128]{3,2,1,0:T(4,128)(2,1)}, u32[]{:S(2)}) copy-start(bf16[1,256,4,128]{3,2,1,0:T(4,128)(2,1)} %anomalies_ref) | copy-start | bytes 786436
  3.1 5.2 %copy-start = (bf16[1,4,256,64]{2,3,1,0:T(8,128)(2,1)S(1)}, bf16[1,4,256,64]{2,3,1,0:T(8,128)(2,1)}, u32[]{:S(2)}) copy-start(bf16[1,4,256,64]{2,3,1,0:T(8,128)(2,1)} %param.7) | copy-start | bytes 393220
  3.1 13.0 %all-to-all-start = ((f32[4,16,512]{2,1,0:T(8,128)}), f32[4,16,512]{2,1,0:T(8,128)S(1)}, u32[]{:S(2)}, u32[]{:S(2)}) async-start(f32[4,16,512]{2,1,0:T(8,128)} %get-tuple-element.24), calls=%async_computation | async-start | bytes 262144 | tf_op jit(solution)/shard_map/all_to_all | solution.py:284
  9.0 30.7 %collective-permute-start = (f32[512,256]{1,0:T(8,128)S(1)}, f32[512,256]{1,0:T(8,128)S(1)}, u32[]{:S(2)}, u32[]{:S(2)}) collective-permute-start(f32[512,256]{1,0:T(8,128)S(1)} %get-tuple-element.23), channel_id=1, source_target_pairs={{0,16},{16,0},{32,48},{48,32},{64,80},{80,64},{96,112},{112,96},{1... | collective-permute-start | bytes 1572872 | tf_op jit(solution)/shard_map/ppermute | solution.py:297
  16.8 6.6 %copy-start.6 = (f32[72,256]{1,0:T(8,128)S(1)}, f32[72,256]{1,0:T(8,128)}, u32[]{:S(2)}) copy-start(f32[72,256]{1,0:T(8,128)} %get-tuple-element.19) | copy-start | bytes 221188
  16.8 23.0 %all-to-all-start.1 = ((f32[8,16,256]{2,1,0:T(8,128)}), f32[8,16,256]{2,1,0:T(8,128)S(1)}, u32[]{:S(2)}, u32[]{:S(2)}) async-start(f32[8,16,256]{2,1,0:T(8,128)} %shard_map.75), calls=%async_computation.1 | async-start | bytes 262144 | tf_op jit(solution)/shard_map/all_to_all | solution.py:288
  23.4 15.1 %collective-permute-start.2 = (f32[72,256]{1,0:T(8,128)S(1)}, f32[72,256]{1,0:T(8,128)S(1)}, u32[]{:S(2)}, u32[]{:S(2)}) collective-permute-start(f32[72,256]{1,0:T(8,128)S(1)} %copy-done.6), channel_id=1, source_target_pairs={{0,31},{1,16},{2,17},{3,18},{4,19},{5,20},{6,21},{7,22},{8,23},{9,... | collective-permute-start | bytes 221192 | tf_op jit(solution)/shard_map/ppermute | solution.py:286
  30.6 9.2 %collective-permute-start.1 = (f32[72,256]{1,0:T(8,128)S(1)}, f32[72,256]{1,0:T(8,128)S(1)}, u32[]{:S(2)}, u32[]{:S(2)}) collective-permute-start(f32[72,256]{1,0:T(8,128)S(1)} %copy-done.6), channel_id=1, source_target_pairs={{0,1},{1,2},{2,3},{3,4},{4,5},{5,6},{6,7},{7,8},{8,9},{9,10},{10,1... | collective-permute-start | bytes 221192 | tf_op jit(solution)/shard_map/ppermute | solution.py:285
  37.0 0.7 copy-start.5
  37.7 0.7 copy-start.4
  38.4 1.4 %copy-start.1 = (f32[256,16]{0,1:T(8,128)S(1)}, f32[256,16]{0,1:T(8,128)}, u32[]{:S(2)}) copy-start(f32[256,16]{0,1:T(8,128)} %param.12) | copy-start | bytes 49156
  39.8 0.7 copy-start.2
  42.2 28.8 %collective-permute-start.3 = (f32[256,256]{1,0:T(8,128)S(1)}, f32[256,256]{1,0:T(8,128)S(1)}, u32[]{:S(2)}, u32[]{:S(2)}) collective-permute-start(f32[256,256]{1,0:T(8,128)S(1)} %get-tuple-element.28.far_sent), channel_id=1, source_target_pairs={{0,31},{1,16},{2,17},{3,18},{4,19},{5,20},{6,21},{7,22},{8,23},{9,... | collective-permute-start | bytes 786440 | tf_op jit(solution)/shard_map/ppermute | solution.py:308
  48.6 22.4 %collective-permute-start.4 = (f32[256,256]{1,0:T(8,128)S(1)}, f32[256,256]{1,0:T(8,128)S(1)}, u32[]{:S(2)}, u32[]{:S(2)}) collective-permute-start(f32[256,256]{1,0:T(8,128)S(1)} %get-tuple-element.29.near_sent), channel_id=1, source_target_pairs={{0,16},{16,0},{32,48},{48,32},{64,80},{80,64},{96,112},{112,96},{1... | collective-permute-start | bytes 786440 | tf_op jit(solution)/shard_map/ppermute | solution.py:310
  72.2 25.4 %collective-permute-start.5 = (f32[256,256]{1,0:T(8,128)S(1)}, f32[256,256]{1,0:T(8,128)S(1)}, u32[]{:S(2)}, u32[]{:S(2)}) collective-permute-start(f32[256,256]{1,0:T(8,128)S(1)} %get-tuple-element.31.far_sent), channel_id=1, source_target_pairs={{0,31},{1,16},{2,17},{3,18},{4,19},{5,20},{6,21},{7,22},{8,23},{9,... | collective-permute-start | bytes 786440 | tf_op jit(solution)/shard_map/ppermute | solution.py:308
  76.7 20.9 %collective-permute-start.6 = (f32[256,256]{1,0:T(8,128)S(1)}, f32[256,256]{1,0:T(8,128)S(1)}, u32[]{:S(2)}, u32[]{:S(2)}) collective-permute-start(f32[256,256]{1,0:T(8,128)S(1)} %get-tuple-element.32.near_sent), channel_id=1, source_target_pairs={{0,16},{16,0},{32,48},{48,32},{64,80},{80,64},{96,112},{112,96},{1... | collective-permute-start | bytes 786440 | tf_op jit(solution)/shard_map/ppermute | solution.py:310
  98.2 5.4 %collective-permute-start.7 = (f32[256,256]{1,0:T(8,128)S(1)}, f32[256,256]{1,0:T(8,128)S(1)}, u32[]{:S(2)}, u32[]{:S(2)}) collective-permute-start(f32[256,256]{1,0:T(8,128)S(1)} %shard_map.79), channel_id=1, source_target_pairs={{0,16},{16,0},{32,48},{48,32},{64,80},{80,64},{96,112},{112,96},{1... | collective-permute-start | bytes 786440 | tf_op jit(solution)/shard_map/ppermute | solution.py:331

commit v7 on v6

--- a/solution.py
+++ b/solution.py
@@ -83,7 +83,15 @@
         sums_ref[copy] = local
 
 
-def divide_kernel(width_y, core_ref, mine_ref, anomalies_ref, own_a_ref, rest_ref):
+def column(row):
+    n = row.shape[1]
+    same = lax.broadcasted_iota(jnp.int32, (n, n), 0) == lax.broadcasted_iota(jnp.int32, (n, n), 1)
+    return jnp.sum(jnp.where(same, row, 0.0), axis=1, keepdims=True)
+
+
+def divide_kernel(width_y, core_ref, mine_ref, anomalies_ref, bands_ref, nu_ref, own_a_ref, rest_ref, bands_col_ref, nu_col_ref):
+    bands_col_ref[...] = column(bands_ref[...].astype(jnp.float32)).astype(jnp.int32)
+    nu_col_ref[...] = column(nu_ref[...])
     low = core_ref[0] == 0
     w = width_y
     rows = [anomalies_ref[0, :, x, :].astype(jnp.float32) for x in range(4)]
@@ -162,10 +170,13 @@
     return advance(moved, spread, force, smooth, modes_ref, nu_ref, w), spread
 
 
-def second_kernel(width_y, members, core_ref, obs_ref, mine_ref, own_a_ref, rest_ref, own_beyond_ref, other_beyond_ref, first_matrix, matrix,
+def second_kernel(width_y, members, core_ref, obs_ref, mine_ref, own_a_ref, rest_ref, own_beyond_ref, other_beyond_ref, physics_ref,
                   modes_ref, bands_ref, nu_ref, sums_ref,
-                  far_out, near_out, sums_out, other_a_ref, other_ref):
+                  far_out, near_out, sums_out, other_a_ref, other_ref, first_matrix, matrix, sems):
     step = STEPS - 2
+    copies = [pltpu.make_async_copy(physics_ref.at[step - i], (first_matrix, matrix)[i], sems.at[i]) for i in range(2)]
+    for copy in copies:
+        copy.start()
     core = core_ref[0]
     w = width_y
     state = own_a_ref.shape[0]
@@ -178,6 +189,7 @@
     far_hot = hot_rows(core, own_beyond_ref[count : count + 1, :count].astype(jnp.int32), (3,), w)
     inside = (mine_ref[0, STEPS - 1], other[(STEPS - 1) * count :])
     beyond = [ref[:count, :].astype(jnp.bfloat16) for ref in (own_beyond_ref, other_beyond_ref)]
+    copies[0].wait()
     turned = first_matrix[...]
     moved = []
     for m in range(2):
@@ -190,14 +202,18 @@
     smooth = smooth_of(total, bands_ref[...], w, members)
     force = forcings(step, core, obs_ref, mine_ref, other_ref[step * count : (step + 1) * count, :], w)
     lam = advance(moved, spread, force, smooth, modes_ref, nu_ref, w)
+    copies[1].wait()
     send_parts(lam, spread, matrix, modes_ref, far_out, near_out, sums_out, w)
 
 
-def step_kernel(step, width_y, members, core_ref, obs_ref, mine_ref, own_a_ref, other_a_ref, other_ref, matrix,
+def step_kernel(step, width_y, members, core_ref, obs_ref, mine_ref, own_a_ref, other_a_ref, other_ref, physics_ref,
                 modes_ref, bands_ref, nu_ref, sums_ref, far_sent, near_sent, far_ref, near_ref,
-                far_out, near_out, sums_out):
+                far_out, near_out, sums_out, matrix, sem):
+    copy = pltpu.make_async_copy(physics_ref.at[step - 1], matrix, sem)
+    copy.start()
     lam, spread = next_lam(step, width_y, members, core_ref, obs_ref, mine_ref, own_a_ref, other_a_ref, other_ref,
                            modes_ref, bands_ref, nu_ref, sums_ref, far_sent, near_sent, far_ref, near_ref)
+    copy.wait()
     send_parts(lam, spread, matrix, modes_ref, far_out, near_out, sums_out, width_y)
 
 
@@ -266,9 +282,8 @@
     chip_groups = [[side * y + j for j in range(side)] for y in range(PLANES)]
 
     half = (state, 2 * width_y)
+    matrix = pltpu.VMEM((state, state), jnp.float32)
     sums_shape = (PLANES, n_modes, 2 * width_y)
-    bands_col = bands[:, None]
-    nu_col = diffusion[:, None]
     late, sums = call(
         functools.partial(prepare_kernel, width_y),
         "prepare",
@@ -287,20 +302,22 @@
     (sums,) = call(regroup_kernel, "regroup", (core, sums), [(side, n_modes, 2 * width_y)])
     sums = lax.all_to_all(sums, "member", 0, 0, tiled=True, axis_index_groups=chip_groups)
     mine_late, anomalies_late, _ = lax.optimization_barrier((mine, anomalies, late))
-    own_a, rest = call(
+    own_a, rest, bands_col, nu_col = call(
         functools.partial(divide_kernel, width_y),
         "divide",
-        (core, mine_late, anomalies_late),
-        [half, (state + STEPS * count, 2 * width_y)],
-        types=(jnp.bfloat16, jnp.float32),
+        (core, mine_late, anomalies_late, bands[None], diffusion[None]),
+        [half, (state + STEPS * count, 2 * width_y), (n_modes, 1), (state, 1)],
+        types=(jnp.bfloat16, jnp.float32, jnp.int32, jnp.float32),
     )
     rest = lax.ppermute(rest, "member", swap)
     *sent, other_a, other_innov = call(
         functools.partial(second_kernel, width_y, members),
         "second",
-        (core, obs_column, mine, own_a, rest, own_beyond, other_beyond, physics[STEPS - 2], physics[STEPS - 3], modes_t, bands_col, nu_col, sums),
+        (core, obs_column, mine, own_a, rest, own_beyond, other_beyond, physics, modes_t, bands_col, nu_col, sums),
         [half, half, sums_shape, half, ((STEPS - 1) * count, state)],
         types=(jnp.float32,) * 3 + (jnp.bfloat16,) * 2,
+        hbm=(7,),
+        scratch=(matrix, matrix, pltpu.SemaphoreType.DMA((2,))),
     )
     known = (core, obs_column, mine, own_a, other_a, other_innov)
     for step in range(STEPS - 3, -1, -1):
@@ -315,8 +332,10 @@
             sent = call(
                 functools.partial(step_kernel, step, width_y, members),
                 f"step{step}",
-                known + (physics[step - 1],) + tail,
+                known + (physics,) + tail,
                 [half, half, sums_shape],
+                hbm=(6,),
+                scratch=(matrix, pltpu.SemaphoreType.DMA),
             )
     ends = []
     for member, values, a in ((1, other_innov, other_a), (0, mine, own_a)):

time: 105 us -> 106 us (level)
  waiting for transfers between devices: 1.87 us -> 4.59 us
  local copies, waits for them, and re-layouts: 3.41 us -> 1.36 us
  starting transfers between devices: 58.3 us -> 57.2 us
    ppermute x1, waiting for transfers between devices: 1.21 us -> 3.94 us  [per_device(): own_beyond = lax.ppermute(late, ('member', 'tile'), along_pairs)]
    all_to_all x1, starting transfers between devices: 6.61 us -> 5.43 us  [per_device(): lax.all_to_all(sums, 'member', 0, 0, tiled=True, axis_index_groups=chip_g...]
    squeeze x1 -> x0, local copies, waits for them, and re-layouts: 1.16 us -> none  [per_device(): physics[step - 1]]
  transfers between devices with their start and end apart: 10 -> 10, of which waited for: 2 -> 2; matrix products, arithmetic and copies ran while one was open for 1% -> 0% of each run, Pallas kernels for 2% -> 2%
where the time goes in v7:
time: 106 us; the launch traced here: 105 us
  starting transfers between devices  57.2 us (54%)
  blocking collectives  31.3 us (30%)
  Pallas kernels  10.1 us (10%)
  waiting for transfers between devices  4.59 us (4%)
  local copies, waits for them, and re-layouts  1.36 us (1%)
    all_to_all x2, blocking collectives, per_device(): lax.all_to_all(sums, 'member', 0, 0, tiled=True, axis_index_groups=z_groups)  17.3 us
    all_to_all x2, blocking collectives, per_device(): lax.all_to_all(sums, 'member', 0, 0, tiled=True, axis_index_groups=y_groups)  14 us
    ppermute x2, starting transfers between devices, per_device(): near = lax.ppermute(near_sent, 'member', swap)  11.6 us
    ppermute x2, starting transfers between devices, per_device(): far = lax.ppermute(far_sent, ('member', 'tile'), far_pairs)  11.2 us
    pallas_call x8, Pallas kernels, call(): pl.pallas_call(kernel, in_specs=[pl.BlockSpec(memory_space=space) for spa...  10.1 us
    ppermute x1, starting transfers between devices, per_device(): rest = lax.ppermute(rest, 'member', swap)  7.21 us
    ppermute x1, starting transfers between devices, per_device(): other_beyond = lax.ppermute(late, ('member', 'tile'), far_pairs)  7.16 us
    all_to_all x1, starting transfers between devices, per_device(): lax.all_to_all(sums, 'member', 0, 0, tiled=True, axis_index_groups=chip_g...  5.43 us
  transfers between devices with their start and end apart: 10, of which 2 were waited for; matrix products, arithmetic and copies ran while one was open for 0% of the time, Pallas kernels for 2%

profile of v7, /device:TPU:1, one launch (start us, length us, event | category | flops | bytes accessed | tf_op | source)
XLA Modules:
  0.0 104.8 jit_solution(2736087817794195467)
XLA Ops:
  0.0 3.1 %shard_map.73 = (f32[72,256]{1,0:T(8,128)}, f32[4,16,512]{2,1,0:T(8,128)}) custom-call(s32[1]{0:T(128)} %bitcast.core_ref, s32[4,64]{1,0:T(4,128)} %obs_ref.9, bf16[1,4,64,256]{3,2,1,0:T(8,128)(2,1)} %bitcast.5, bf16[1,256,4,128]{3,2,1,0:T(4,128)(2,1)} %anomalies_ref, f32[16,256]{1,0:T(8,128)} %bitcast.10), custom_call_target="tpu_custom_call" | custom-call | flops 400000000 | bytes 2000000 | tf_op jit(solution)/shard_map/pallas_call | solution.py:250
  3.1 0.0 copy-start.1
  3.1 5.1 %all-to-all-start = ((f32[4,16,512]{2,1,0:T(8,128)}), f32[4,16,512]{2,1,0:T(8,128)S(1)}, u32[]{:S(2)}, u32[]{:S(2)}) async-start(f32[4,16,512]{2,1,0:T(8,128)} %get-tuple-element.28), calls=%async_computation | async-start | bytes 262144 | tf_op jit(solution)/shard_map/all_to_all | solution.py:299
  8.3 0.7 copy-done.5
  8.9 1.2 %shard_map.74 = (bf16[256,256]{1,0:T(8,128)(2,1)S(1)}, f32[512,256]{1,0:T(8,128)S(1)}, s32[16,1]{1,0:T(8,128)S(1)}, f32[256,1]{1,0:T(8,128)S(1)}) custom-call(s32[1]{0:T(128)} %bitcast.core_ref, bf16[1,4,64,256]{3,2,1,0:T(8,128)(2,1)S(1)} %bitcast.6, bf16[1,256,4,128]{3,2,1,0:T(4,128)(2,1)S(1)} %copy-done.4, s32[1,16]{1,0:T(1,128)S(1)} %bitcast.16, ...), custom_call_target="tpu_custom_call" | custom-call | flops 400000000 | bytes 2000000 | tf_op jit(solution)/shard_map/pallas_call | solution.py:250
  10.1 0.0 copy-start
  10.1 7.2 %collective-permute-start = (f32[512,256]{1,0:T(8,128)S(1)}, f32[512,256]{1,0:T(8,128)S(1)}, u32[]{:S(2)}, u32[]{:S(2)}) collective-permute-start(f32[512,256]{1,0:T(8,128)S(1)} %get-tuple-element.27), channel_id=1, source_target_pairs={{0,16},{16,0},{32,48},{48,32},{64,80},{80,64},{96,112},{112,96},{1... | collective-permute-start | bytes 1572872 | tf_op jit(solution)/shard_map/ppermute | solution.py:312
  17.3 0.0 all-to-all-done.sums_ref
  17.3 0.7 shard_map.75
  18.0 5.4 %all-to-all-start.1 = ((f32[8,16,256]{2,1,0:T(8,128)}), f32[8,16,256]{2,1,0:T(8,128)S(1)}, u32[]{:S(2)}, u32[]{:S(2)}) async-start(f32[8,16,256]{2,1,0:T(8,128)} %shard_map.75), calls=%async_computation.1 | async-start | bytes 262144 | tf_op jit(solution)/shard_map/all_to_all | solution.py:303
  23.4 7.2 %collective-permute-start.2 = (f32[72,256]{1,0:T(8,128)S(1)}, f32[72,256]{1,0:T(8,128)S(1)}, u32[]{:S(2)}, u32[]{:S(2)}) collective-permute-start(f32[72,256]{1,0:T(8,128)S(1)} %copy-done.7), channel_id=1, source_target_pairs={{0,31},{1,16},{2,17},{3,18},{4,19},{5,20},{6,21},{7,22},{8,23},{9,... | collective-permute-start | bytes 221192 | tf_op jit(solution)/shard_map/ppermute | solution.py:301
  30.6 5.2 %collective-permute-start.1 = (f32[72,256]{1,0:T(8,128)S(1)}, f32[72,256]{1,0:T(8,128)S(1)}, u32[]{:S(2)}, u32[]{:S(2)}) collective-permute-start(f32[72,256]{1,0:T(8,128)S(1)} %copy-done.7), channel_id=1, source_target_pairs={{0,1},{1,2},{2,3},{3,4},{4,5},{5,6},{6,7},{7,8},{8,9},{9,10},{10,1... | collective-permute-start | bytes 221192 | tf_op jit(solution)/shard_map/ppermute | solution.py:300
  35.8 3.9 %collective-permute-done.1.own_beyond_ref = f32[72,256]{1,0:T(8,128)S(1)} collective-permute-done((f32[72,256]{1,0:T(8,128)S(1)}, f32[72,256]{1,0:T(8,128)S(1)}, u32[]{:S(2)}, u32[]{:S(2)}) %collective-permute-start.1) | collective-permute-done | bytes 73760 | tf_op jit(solution)/shard_map/ppermute | solution.py:300
  39.8 0.0 collective-permute-done.rest_ref
  39.8 0.0 all-to-all-done.1.sums_ref
  39.8 0.7 copy-done.3
  40.5 1.9 %shard_map.76 = (f32[256,256]{1,0:T(8,128)S(1)}, f32[256,256]{1,0:T(8,128)S(1)}, f32[4,16,256]{2,1,0:T(8,128)S(1)}, bf16[256,256]{1,0:T(8,128)(2,1)S(1)}, bf16[192,256]{1,0:T(8,128)(2,1)S(1)}) custom-call(s32[1]{0:T(128)} %bitcast.core_ref, s32[4,64]{1,0:T(4,128)S(1)} %copy-done.3, bf16[1,4,64,256]{3,2,1,0:T(8,128)(2,1)S(1)} %bitcast.7, ...), custom_call_target="tpu_custom_call" | custom-call | flops 400000000 | bytes 2000000 | tf_op jit(solution)/shard_map/pallas_call | solution.py:250
  42.4 6.4 %collective-permute-start.3 = (f32[256,256]{1,0:T(8,128)S(1)}, f32[256,256]{1,0:T(8,128)S(1)}, u32[]{:S(2)}, u32[]{:S(2)}) collective-permute-start(f32[256,256]{1,0:T(8,128)S(1)} %get-tuple-element.32.far_sent), channel_id=1, source_target_pairs={{0,31},{1,16},{2,17},{3,18},{4,19},{5,20},{6,21},{7,22},{8,23},{9,... | collective-permute-start | bytes 786440 | tf_op jit(solution)/shard_map/ppermute | solution.py:325
  48.8 4.9 %collective-permute-start.4 = (f32[256,256]{1,0:T(8,128)S(1)}, f32[256,256]{1,0:T(8,128)S(1)}, u32[]{:S(2)}, u32[]{:S(2)}) collective-permute-start(f32[256,256]{1,0:T(8,128)S(1)} %get-tuple-element.33.near_sent), channel_id=1, source_target_pairs={{0,16},{16,0},{32,48},{48,32},{64,80},{80,64},{96,112},{112,96},{1... | collective-permute-start | bytes 786440 | tf_op jit(solution)/shard_map/ppermute | solution.py:327
  53.7 7.2 %all_to_all.30 = f32[4,16,256]{2,1,0:T(8,128)S(1)} all-to-all(f32[4,16,256]{2,1,0:T(8,128)S(1)} %get-tuple-element.31), channel_id=1, replica_groups={{0,128,256,384},{16,144,272,400},{32,160,288,416},{48,176,304,432},{64,..., dimensions={0} | all-to-all | bytes 131072 | tf_op jit(solution)/shard_map/all_to_all | solution.py:326
  60.8 10.3 %all_to_all.31.sums_ref = f32[4,16,256]{2,1,0:T(8,128)S(1)} all-to-all(f32[4,16,256]{2,1,0:T(8,128)S(1)} %broadcast_in_dim.24), channel_id=1, replica_groups={{0,32,64,96},{16,48,80,112},{128,160,192,224},{144,176,208,240},{256,28..., dimensions={0} | all-to-all | bytes 131072 | tf_op jit(solution)/shard_map/all_to_all | solution.py:329
  71.2 0.0 collective-permute-done.3.far_ref
  71.2 1.3 %shard_map.77 = (f32[256,256]{1,0:T(8,128)S(1)}, f32[256,256]{1,0:T(8,128)S(1)}, f32[4,16,256]{2,1,0:T(8,128)S(1)}) custom-call(s32[1]{0:T(128)} %bitcast.core_ref, s32[4,64]{1,0:T(4,128)S(1)} %copy-done.3, bf16[1,4,64,256]{3,2,1,0:T(8,128)(2,1)S(1)} %bitcast.8, bf16[256,256]{1,0:T(8,128)(2,1)S(1)} %get-tuple-element.24.own_a_ref.a_ref, ...), custom_call_target="tpu_custom_call" | custom-call | flops 400000000 | bytes 2000000 | tf_op jit(solution)/shard_map/pallas_call | solution.py:250
  72.5 4.8 %collective-permute-start.5 = (f32[256,256]{1,0:T(8,128)S(1)}, f32[256,256]{1,0:T(8,128)S(1)}, u32[]{:S(2)}, u32[]{:S(2)}) collective-permute-start(f32[256,256]{1,0:T(8,128)S(1)} %get-tuple-element.35.far_sent), channel_id=1, source_target_pairs={{0,31},{1,16},{2,17},{3,18},{4,19},{5,20},{6,21},{7,22},{8,23},{9,... | collective-permute-start | bytes 786440 | tf_op jit(solution)/shard_map/ppermute | solution.py:325
  77.3 6.8 %collective-permute-start.6 = (f32[256,256]{1,0:T(8,128)S(1)}, f32[256,256]{1,0:T(8,128)S(1)}, u32[]{:S(2)}, u32[]{:S(2)}) collective-permute-start(f32[256,256]{1,0:T(8,128)S(1)} %get-tuple-element.36.near_sent), channel_id=1, source_target_pairs={{0,16},{16,0},{32,48},{48,32},{64,80},{80,64},{96,112},{112,96},{1... | collective-permute-start | bytes 786440 | tf_op jit(solution)/shard_map/ppermute | solution.py:327
  84.0 6.9 %all_to_all.32 = f32[4,16,256]{2,1,0:T(8,128)S(1)} all-to-all(f32[4,16,256]{2,1,0:T(8,128)S(1)} %get-tuple-element.34), channel_id=1, replica_groups={{0,128,256,384},{16,144,272,400},{32,160,288,416},{48,176,304,432},{64,..., dimensions={0} | all-to-all | bytes 131072 | tf_op jit(solution)/shard_map/all_to_all | solution.py:326
  90.9 7.0 %all_to_all.33.sums_ref = f32[4,16,256]{2,1,0:T(8,128)S(1)} all-to-all(f32[4,16,256]{2,1,0:T(8,128)S(1)} %broadcast_in_dim.25), channel_id=1, replica_groups={{0,32,64,96},{16,48,80,112},{128,160,192,224},{144,176,208,240},{256,28..., dimensions={0} | all-to-all | bytes 131072 | tf_op jit(solution)/shard_map/all_to_all | solution.py:329
  97.9 0.5 shard_map.79
  98.4 4.2 %collective-permute-start.7 = (f32[256,256]{1,0:T(8,128)S(1)}, f32[256,256]{1,0:T(8,128)S(1)}, u32[]{:S(2)}, u32[]{:S(2)}) collective-permute-start(f32[256,256]{1,0:T(8,128)S(1)} %shard_map.79), channel_id=1, source_target_pairs={{0,16},{16,0},{32,48},{48,32},{64,80},{80,64},{96,112},{112,96},{1... | collective-permute-start | bytes 786440 | tf_op jit(solution)/shard_map/ppermute | solution.py:350
  102.6 0.5 shard_map.78.own_ref
  103.1 0.6 collective-permute-done.7.back_ref
  103.7 1.1 %shard_map.80 = f32[1,256,4,128]{3,2,1,0:T(4,128)} custom-call(s32[1]{0:T(128)} %bitcast.core_ref, f32[256,256]{1,0:T(8,128)S(1)} %shard_map.78.own_ref, f32[256,256]{1,0:T(8,128)S(1)} %collective-permute-done.7.back_ref), custom_call_target="tpu_custom_call" | custom-call | flops 400000000 | bytes 2000000 | tf_op jit(solution)/shard_map/pallas_call | solution.py:250
  (20 shorter events, 0.1 us)
Async XLA Ops:
  0.0 8.2 %copy-start.4 = (bf16[1,256,4,128]{3,2,1,0:T(4,128)(2,1)S(1)}, bf16[1,256,4,128]{3,2,1,0:T(4,128)(2,1)}, u32[]{:S(2)}) copy-start(bf16[1,256,4,128]{3,2,1,0:T(4,128)(2,1)} %anomalies_ref) | copy-start | bytes 786436
  3.1 5.2 %copy-start.1 = (bf16[1,4,256,64]{2,3,1,0:T(8,128)(2,1)S(1)}, bf16[1,4,256,64]{2,3,1,0:T(8,128)(2,1)}, u32[]{:S(2)}) copy-start(bf16[1,4,256,64]{2,3,1,0:T(8,128)(2,1)} %param.7) | copy-start | bytes 393220
  3.1 14.2 %all-to-all-start = ((f32[4,16,512]{2,1,0:T(8,128)}), f32[4,16,512]{2,1,0:T(8,128)S(1)}, u32[]{:S(2)}, u32[]{:S(2)}) async-start(f32[4,16,512]{2,1,0:T(8,128)} %get-tuple-element.28), calls=%async_computation | async-start | bytes 262144 | tf_op jit(solution)/shard_map/all_to_all | solution.py:299
  8.2 0.7 copy-start.5
  8.2 0.7 copy-start.6
  10.1 29.7 %copy-start = (f32[4,256,256]{2,1,0:T(8,128)S(1)}, f32[4,256,256]{2,1,0:T(8,128)}, u32[]{:S(2)}) copy-start(f32[4,256,256]{2,1,0:T(8,128)} %physics_ref.3) | copy-start | bytes 3145732
  10.1 29.7 %collective-permute-start = (f32[512,256]{1,0:T(8,128)S(1)}, f32[512,256]{1,0:T(8,128)S(1)}, u32[]{:S(2)}, u32[]{:S(2)}) collective-permute-start(f32[512,256]{1,0:T(8,128)S(1)} %get-tuple-element.27), channel_id=1, source_target_pairs={{0,16},{16,0},{32,48},{48,32},{64,80},{80,64},{96,112},{112,96},{1... | collective-permute-start | bytes 1572872 | tf_op jit(solution)/shard_map/ppermute | solution.py:312
  18.0 5.4 %copy-start.7 = (f32[72,256]{1,0:T(8,128)S(1)}, f32[72,256]{1,0:T(8,128)}, u32[]{:S(2)}) copy-start(f32[72,256]{1,0:T(8,128)} %get-tuple-element.21) | copy-start | bytes 221188
  18.0 21.8 %copy-start.2 = (f32[256,16]{0,1:T(8,128)S(1)}, f32[256,16]{0,1:T(8,128)}, u32[]{:S(2)}) copy-start(f32[256,16]{0,1:T(8,128)} %param.12) | copy-start | bytes 49156
  18.0 21.8 %all-to-all-start.1 = ((f32[8,16,256]{2,1,0:T(8,128)}), f32[8,16,256]{2,1,0:T(8,128)S(1)}, u32[]{:S(2)}, u32[]{:S(2)}) async-start(f32[8,16,256]{2,1,0:T(8,128)} %shard_map.75), calls=%async_computation.1 | async-start | bytes 262144 | tf_op jit(solution)/shard_map/all_to_all | solution.py:303
  23.4 12.4 %collective-permute-start.2 = (f32[72,256]{1,0:T(8,128)S(1)}, f32[72,256]{1,0:T(8,128)S(1)}, u32[]{:S(2)}, u32[]{:S(2)}) collective-permute-start(f32[72,256]{1,0:T(8,128)S(1)} %copy-done.7), channel_id=1, source_target_pairs={{0,31},{1,16},{2,17},{3,18},{4,19},{5,20},{6,21},{7,22},{8,23},{9,... | collective-permute-start | bytes 221192 | tf_op jit(solution)/shard_map/ppermute | solution.py:301
  30.6 9.2 %collective-permute-start.1 = (f32[72,256]{1,0:T(8,128)S(1)}, f32[72,256]{1,0:T(8,128)S(1)}, u32[]{:S(2)}, u32[]{:S(2)}) collective-permute-start(f32[72,256]{1,0:T(8,128)S(1)} %copy-done.7), channel_id=1, source_target_pairs={{0,1},{1,2},{2,3},{3,4},{4,5},{5,6},{6,7},{7,8},{8,9},{9,10},{10,1... | collective-permute-start | bytes 221192 | tf_op jit(solution)/shard_map/ppermute | solution.py:300
  39.8 0.7 copy-start.3
  42.4 28.8 %collective-permute-start.3 = (f32[256,256]{1,0:T(8,128)S(1)}, f32[256,256]{1,0:T(8,128)S(1)}, u32[]{:S(2)}, u32[]{:S(2)}) collective-permute-start(f32[256,256]{1,0:T(8,128)S(1)} %get-tuple-element.32.far_sent), channel_id=1, source_target_pairs={{0,31},{1,16},{2,17},{3,18},{4,19},{5,20},{6,21},{7,22},{8,23},{9,... | collective-permute-start | bytes 786440 | tf_op jit(solution)/shard_map/ppermute | solution.py:325
  48.8 22.4 %collective-permute-start.4 = (f32[256,256]{1,0:T(8,128)S(1)}, f32[256,256]{1,0:T(8,128)S(1)}, u32[]{:S(2)}, u32[]{:S(2)}) collective-permute-start(f32[256,256]{1,0:T(8,128)S(1)} %get-tuple-element.33.near_sent), channel_id=1, source_target_pairs={{0,16},{16,0},{32,48},{48,32},{64,80},{80,64},{96,112},{112,96},{1... | collective-permute-start | bytes 786440 | tf_op jit(solution)/shard_map/ppermute | solution.py:327
  72.5 25.4 %collective-permute-start.5 = (f32[256,256]{1,0:T(8,128)S(1)}, f32[256,256]{1,0:T(8,128)S(1)}, u32[]{:S(2)}, u32[]{:S(2)}) collective-permute-start(f32[256,256]{1,0:T(8,128)S(1)} %get-tuple-element.35.far_sent), channel_id=1, source_target_pairs={{0,31},{1,16},{2,17},{3,18},{4,19},{5,20},{6,21},{7,22},{8,23},{9,... | collective-permute-start | bytes 786440 | tf_op jit(solution)/shard_map/ppermute | solution.py:325
  77.3 20.6 %collective-permute-start.6 = (f32[256,256]{1,0:T(8,128)S(1)}, f32[256,256]{1,0:T(8,128)S(1)}, u32[]{:S(2)}, u32[]{:S(2)}) collective-permute-start(f32[256,256]{1,0:T(8,128)S(1)} %get-tuple-element.36.near_sent), channel_id=1, source_target_pairs={{0,16},{16,0},{32,48},{48,32},{64,80},{80,64},{96,112},{112,96},{1... | collective-permute-start | bytes 786440 | tf_op jit(solution)/shard_map/ppermute | solution.py:327
  98.4 5.4 %collective-permute-start.7 = (f32[256,256]{1,0:T(8,128)S(1)}, f32[256,256]{1,0:T(8,128)S(1)}, u32[]{:S(2)}, u32[]{:S(2)}) collective-permute-start(f32[256,256]{1,0:T(8,128)S(1)} %shard_map.79), channel_id=1, source_target_pairs={{0,16},{16,0},{32,48},{48,32},{64,80},{80,64},{96,112},{112,96},{1... | collective-permute-start | bytes 786440 | tf_op jit(solution)/shard_map/ppermute | solution.py:350

commit v8 on v7

--- a/solution.py
+++ b/solution.py
@@ -72,9 +72,7 @@
     hot = jnp.concatenate([(obs_row == x * w + y).astype(jnp.bfloat16) for x in order], axis=0)
     copies[0].wait()
     values = mine_ref[...]
-    late_ref[:count, :] = values.astype(jnp.float32)
-    late_ref[count:, :] = jnp.zeros((late_ref.shape[0] - count, late_ref.shape[1]), jnp.float32)
-    late_ref[count : count + 1, :count] = obs_row.astype(jnp.float32)
+    late_ref[...] = values.astype(jnp.float32)
     lam = placed(values, hot)
     copies[1].wait()
     spread = jnp.concatenate([anomalies_ref[0, :, x, :].astype(jnp.float32) for x in order], axis=1)
@@ -100,8 +98,16 @@
     for i in range(2):
         own_a_ref[:, i * w : (i + 1) * w] = jnp.where(low, rows[i], rows[3 - i]).astype(jnp.bfloat16)
         rest_ref[:state, i * w : (i + 1) * w] = jnp.where(low, rows[3 - i], rows[i])
-    for t in range(STEPS):
+    for t in range(STEPS - 1):
         rest_ref[state + t * count : state + (t + 1) * count, :] = mine_ref[0, t].astype(jnp.float32)
+
+
+def pass_on_kernel(core_ref, obs_ref, late_ref, other_ref, far_ref):
+    count = late_ref.shape[0]
+    far_ref[:count, :] = late_ref[...]
+    far_ref[count : 2 * count, :] = other_ref[...]
+    far_ref[2 * count :, :] = jnp.zeros((far_ref.shape[0] - 2 * count, far_ref.shape[1]), jnp.float32)
+    far_ref[2 * count : 2 * count + 1, :count] = obs_ref[STEPS - 1 : STEPS, :].astype(jnp.float32)
 
 
 def regroup_kernel(core_ref, sums_ref, out_ref):
@@ -170,7 +176,7 @@
     return advance(moved, spread, force, smooth, modes_ref, nu_ref, w), spread
 
 
-def second_kernel(width_y, members, core_ref, obs_ref, mine_ref, own_a_ref, rest_ref, own_beyond_ref, other_beyond_ref, physics_ref,
+def second_kernel(width_y, members, core_ref, obs_ref, mine_ref, own_a_ref, rest_ref, late_ref, beyond_ref, physics_ref,
                   modes_ref, bands_ref, nu_ref, sums_ref,
                   far_out, near_out, sums_out, other_a_ref, other_ref, first_matrix, matrix, sems):
     step = STEPS - 2
@@ -182,13 +188,12 @@
     state = own_a_ref.shape[0]
     count = obs_ref.shape[1]
     other_a_ref[...] = rest_ref[:state, :].astype(jnp.bfloat16)
-    other = rest_ref[state:, :].astype(jnp.bfloat16)
-    other_ref[...] = other[: (STEPS - 1) * count]
+    other_ref[...] = rest_ref[state:, :].astype(jnp.bfloat16)
     spread = both_spreads(own_a_ref, other_a_ref)
     hot = hot_rows(core, obs_ref[STEPS - 1 : STEPS, :], (0, 1, 2), w)
-    far_hot = hot_rows(core, own_beyond_ref[count : count + 1, :count].astype(jnp.int32), (3,), w)
-    inside = (mine_ref[0, STEPS - 1], other[(STEPS - 1) * count :])
-    beyond = [ref[:count, :].astype(jnp.bfloat16) for ref in (own_beyond_ref, other_beyond_ref)]
+    far_hot = hot_rows(core, beyond_ref[2 * count : 2 * count + 1, :count].astype(jnp.int32), (3,), w)
+    inside = (mine_ref[0, STEPS - 1], late_ref[...].astype(jnp.bfloat16))
+    beyond = [beyond_ref[(1 - m) * count : (2 - m) * count, :].astype(jnp.bfloat16) for m in range(2)]
     copies[0].wait()
     turned = first_matrix[...]
     moved = []
@@ -270,12 +275,10 @@
 
     swap = [(i, i ^ 1) for i in range(members)]
     far_pairs = []
-    along_pairs = []
     for m in range(members):
         for t in range(tiles):
-            after, before = (t + 1) % tiles, (t - 1) % tiles
-            far_pairs.append((m * tiles + t, (m ^ 1) * tiles + (after if m % 2 else before)))
-            along_pairs.append((m * tiles + t, m * tiles + (before if m % 2 else after)))
+            target = (t + 1) % tiles if m % 2 else (t - 1) % tiles
+            far_pairs.append((m * tiles + t, (m ^ 1) * tiles + target))
     side = 2 * PLANES
     y_groups = [[side * y + j for y in range(PLANES)] for j in range(side)]
     z_groups = [[side * y + 2 * z + c for z in range(PLANES)] for y in range(PLANES) for c in range(2)]
@@ -288,7 +291,7 @@
         functools.partial(prepare_kernel, width_y),
         "prepare",
         (core, obs_column, mine, anomalies, modes_t),
-        [(count + 8, state), (PLANES, n_modes, 4 * width_y)],
+        [(count, state), (PLANES, n_modes, 4 * width_y)],
         hbm=(2, 3),
         scratch=(
             pltpu.VMEM((count, state), mine.dtype),
@@ -297,23 +300,24 @@
         ),
     )
     sums = lax.all_to_all(sums, "member", 0, 0, tiled=True, axis_index_groups=y_groups)
-    own_beyond = lax.ppermute(late, ("member", "tile"), along_pairs)
-    other_beyond = lax.ppermute(late, ("member", "tile"), far_pairs)
+    other_late = lax.ppermute(late, "member", swap)
+    (beyond,) = call(pass_on_kernel, "pass_on", (core, obs_column, late, other_late), [(2 * count + 8, state)])
+    beyond = lax.ppermute(beyond, ("member", "tile"), far_pairs)
     (sums,) = call(regroup_kernel, "regroup", (core, sums), [(side, n_modes, 2 * width_y)])
     sums = lax.all_to_all(sums, "member", 0, 0, tiled=True, axis_index_groups=chip_groups)
-    mine_late, anomalies_late, _ = lax.optimization_barrier((mine, anomalies, late))
+    mine_late, anomalies_late, _ = lax.optimization_barrier((mine, anomalies, other_late))
     own_a, rest, bands_col, nu_col = call(
         functools.partial(divide_kernel, width_y),
         "divide",
         (core, mine_late, anomalies_late, bands[None], diffusion[None]),
-        [half, (state + STEPS * count, 2 * width_y), (n_modes, 1), (state, 1)],
+        [half, (state + (STEPS - 1) * count, 2 * width_y), (n_modes, 1), (state, 1)],
         types=(jnp.bfloat16, jnp.float32, jnp.int32, jnp.float32),
     )
     rest = lax.ppermute(rest, "member", swap)
     *sent, other_a, other_innov = call(
         functools.partial(second_kernel, width_y, members),
         "second",
-        (core, obs_column, mine, own_a, rest, own_beyond, other_beyond, physics, modes_t, bands_col, nu_col, sums),
+        (core, obs_column, mine, own_a, rest, other_late, beyond, physics, modes_t, bands_col, nu_col, sums),
         [half, half, sums_shape, half, ((STEPS - 1) * count, state)],
         types=(jnp.float32,) * 3 + (jnp.bfloat16,) * 2,
         hbm=(7,),

time: 106 us -> 101 us (0.953)
  blocking collectives: 31.3 us -> 28.2 us
  starting transfers between devices: 57.2 us -> 55.9 us
    ppermute x1, starting transfers between devices: 7.21 us -> 1.92 us  [per_device(): rest = lax.ppermute(rest, 'member', swap)]
    all_to_all x2, blocking collectives: 17.3 us -> 13.9 us  [per_device(): lax.all_to_all(sums, 'member', 0, 0, tiled=True, axis_index_groups=z_groups)]
    ppermute x2, starting transfers between devices: 12.4 us -> 15.7 us  [the longest x1 8.75 us: per_device(): other_late = lax.ppermute(late, 'member', swap)]
    ppermute x2, starting transfers between devices: 11.6 us -> 13.7 us  [per_device(): near = lax.ppermute(near_sent, 'member', swap)]
    all_to_all x1, starting transfers between devices: 5.15 us -> 3.47 us  [per_device(): lax.all_to_all(sums, 'member', 0, 0, tiled=True, axis_index_groups=y_groups)]
    all_to_all x1, waiting for transfers between devices: 0.01 us -> 1.24 us  [per_device(): lax.all_to_all(sums, 'member', 0, 0, tiled=True, axis_index_groups=y_groups)]
    pallas_call x8 -> x9, Pallas kernels: 10.1 us -> 10.1 us  [call(): pl.pallas_call(kernel, in_specs=[pl.BlockSpec(memory_space=space) for spa...]
  transfers between devices with their start and end apart: 10 -> 10, of which waited for: 2 -> 3; matrix products, arithmetic and copies ran while one was open for 0% -> 0% of each run, Pallas kernels for 2% -> 2%
where the time goes in v8:
time: 101 us
  starting transfers between devices  55.9 us (55%)
  blocking collectives  28.2 us (28%)
  Pallas kernels  10.1 us (10%)
  waiting for transfers between devices  5.29 us (5%)
    all_to_all x2, blocking collectives, per_device(): lax.all_to_all(sums, 'member', 0, 0, tiled=True, axis_index_groups=y_groups)  14.3 us
    all_to_all x2, blocking collectives, per_device(): lax.all_to_all(sums, 'member', 0, 0, tiled=True, axis_index_groups=z_groups)  13.9 us
    ppermute x2, starting transfers between devices, per_device(): near = lax.ppermute(near_sent, 'member', swap)  13.7 us
    ppermute x2, starting transfers between devices, per_device(): far = lax.ppermute(far_sent, ('member', 'tile'), far_pairs)  12.2 us
    pallas_call x9, Pallas kernels, call(): pl.pallas_call(kernel, in_specs=[pl.BlockSpec(memory_space=space) for spa...  10.1 us
    ppermute x1, starting transfers between devices, per_device(): other_late = lax.ppermute(late, 'member', swap)  8.75 us
    ppermute x1, starting transfers between devices, per_device(): beyond = lax.ppermute(beyond, ('member', 'tile'), far_pairs)  6.93 us
    all_to_all x1, starting transfers between devices, per_device(): lax.all_to_all(sums, 'member', 0, 0, tiled=True, axis_index_groups=chip_g...  4.57 us
  transfers between devices with their start and end apart: 10, of which 3 were waited for; matrix products, arithmetic and copies ran while one was open for 0% of the time, Pallas kernels for 2%

profile of v8, /device:TPU:1, one launch (start us, length us, event | category | flops | bytes accessed | tf_op | source)
XLA Modules:
  0.0 100.5 jit_solution(11489126857727815770)
XLA Ops:
  0.0 3.1 %shard_map.73 = (f32[64,256]{1,0:T(8,128)}, f32[4,16,512]{2,1,0:T(8,128)}) custom-call(s32[1]{0:T(128)} %bitcast.core_ref, s32[4,64]{1,0:T(4,128)} %obs_ref.11, bf16[1,4,64,256]{3,2,1,0:T(8,128)(2,1)} %bitcast.5, bf16[1,256,4,128]{3,2,1,0:T(4,128)(2,1)} %anomalies_ref, f32[16,256]{1,0:T(8,128)} %bitcast.10), custom_call_target="tpu_custom_call" | custom-call | flops 400000000 | bytes 2000000 | tf_op jit(solution)/shard_map/pallas_call | solution.py:255
  3.1 8.7 %collective-permute-start = (f32[64,256]{1,0:T(8,128)}, f32[64,256]{1,0:T(8,128)S(1)}, u32[]{:S(2)}, u32[]{:S(2)}) collective-permute-start(f32[64,256]{1,0:T(8,128)} %get-tuple-element.21.late_ref), channel_id=1, source_target_pairs={{0,16},{16,0},{32,48},{48,32},{64,80},{80,64},{96,112},{112,96},{1... | collective-permute-start | bytes 196616 | tf_op jit(solution)/shard_map/ppermute | solution.py:303
  11.8 0.0 copy-start.1
  11.8 3.5 %all-to-all-start = ((f32[4,16,512]{2,1,0:T(8,128)}), f32[4,16,512]{2,1,0:T(8,128)S(1)}, u32[]{:S(2)}, u32[]{:S(2)}) async-start(f32[4,16,512]{2,1,0:T(8,128)} %get-tuple-element.28), calls=%async_computation | async-start | bytes 262144 | tf_op jit(solution)/shard_map/all_to_all | solution.py:302
  15.3 0.0 copy-start.6
  15.3 0.0 copy-start.7
  15.4 0.6 copy-done.6
  16.0 1.1 %shard_map.74 = (bf16[256,256]{1,0:T(8,128)(2,1)S(1)}, f32[448,256]{1,0:T(8,128)S(1)}, s32[16,1]{1,0:T(8,128)S(1)}, f32[256,1]{1,0:T(8,128)S(1)}) custom-call(s32[1]{0:T(128)} %bitcast.core_ref, bf16[1,4,64,256]{3,2,1,0:T(8,128)(2,1)S(1)} %bitcast.6, bf16[1,256,4,128]{3,2,1,0:T(4,128)(2,1)S(1)} %copy-done.4, s32[1,16]{1,0:T(1,128)S(1)} %bitcast.16, ...), custom_call_target="tpu_custom_call" | custom-call | flops 400000000 | bytes 2000000 | tf_op jit(solution)/shard_map/pallas_call | solution.py:255
  17.2 1.9 %collective-permute-start.1 = (f32[448,256]{1,0:T(8,128)S(1)}, f32[448,256]{1,0:T(8,128)S(1)}, u32[]{:S(2)}, u32[]{:S(2)}) collective-permute-start(f32[448,256]{1,0:T(8,128)S(1)} %get-tuple-element.27), channel_id=1, source_target_pairs={{0,16},{16,0},{32,48},{48,32},{64,80},{80,64},{96,112},{112,96},{1... | collective-permute-start | bytes 1376264 | tf_op jit(solution)/shard_map/ppermute | solution.py:316
  19.1 1.2 %all-to-all-done.sums_ref = f32[4,16,512]{2,1,0:T(8,128)S(1)} async-done(((f32[4,16,512]{2,1,0:T(8,128)}), f32[4,16,512]{2,1,0:T(8,128)S(1)}, u32[]{:S(2)}, u32[]{:S(2)}) %all-to-all-start) | async-done | bytes 131104 | tf_op jit(solution)/shard_map/all_to_all | solution.py:302
  20.3 0.7 shard_map.76
  21.0 4.6 %all-to-all-start.1 = ((f32[8,16,256]{2,1,0:T(8,128)}), f32[8,16,256]{2,1,0:T(8,128)S(1)}, u32[]{:S(2)}, u32[]{:S(2)}) async-start(f32[8,16,256]{2,1,0:T(8,128)} %shard_map.76), calls=%async_computation.1 | async-start | bytes 262144 | tf_op jit(solution)/shard_map/all_to_all | solution.py:307
  25.6 0.0 copy-start.2
  25.6 6.9 %collective-permute-start.2 = (f32[136,256]{1,0:T(8,128)S(1)}, f32[136,256]{1,0:T(8,128)S(1)}, u32[]{:S(2)}, u32[]{:S(2)}) collective-permute-start(f32[136,256]{1,0:T(8,128)S(1)} %shard_map.75), channel_id=1, source_target_pairs={{0,31},{1,16},{2,17},{3,18},{4,19},{5,20},{6,21},{7,22},{8,23},{9,... | collective-permute-start | bytes 417800 | tf_op jit(solution)/shard_map/ppermute | solution.py:305
  32.6 3.4 %collective-permute-done.2.beyond_ref = f32[136,256]{1,0:T(8,128)S(1)} collective-permute-done((f32[136,256]{1,0:T(8,128)S(1)}, f32[136,256]{1,0:T(8,128)S(1)}, u32[]{:S(2)}, u32[]{:S(2)}) %collective-permute-start.2) | collective-permute-done | bytes 139296 | tf_op jit(solution)/shard_map/ppermute | solution.py:305
  36.0 0.0 collective-permute-done.1.rest_ref
  36.0 0.0 all-to-all-done.1.sums_ref
  36.0 1.9 %shard_map.77 = (f32[256,256]{1,0:T(8,128)S(1)}, f32[256,256]{1,0:T(8,128)S(1)}, f32[4,16,256]{2,1,0:T(8,128)S(1)}, bf16[256,256]{1,0:T(8,128)(2,1)S(1)}, bf16[192,256]{1,0:T(8,128)(2,1)S(1)}) custom-call(s32[1]{0:T(128)} %bitcast.core_ref, s32[4,64]{1,0:T(4,128)S(1)} %copy-done.3, bf16[1,4,64,256]{3,2,1,0:T(8,128)(2,1)S(1)} %bitcast.7, ...), custom_call_target="tpu_custom_call" | custom-call | flops 400000000 | bytes 2000000 | tf_op jit(solution)/shard_map/pallas_call | solution.py:255
  37.9 7.4 %collective-permute-start.3 = (f32[256,256]{1,0:T(8,128)S(1)}, f32[256,256]{1,0:T(8,128)S(1)}, u32[]{:S(2)}, u32[]{:S(2)}) collective-permute-start(f32[256,256]{1,0:T(8,128)S(1)} %get-tuple-element.32.far_sent), channel_id=1, source_target_pairs={{0,31},{1,16},{2,17},{3,18},{4,19},{5,20},{6,21},{7,22},{8,23},{9,... | collective-permute-start | bytes 786440 | tf_op jit(solution)/shard_map/ppermute | solution.py:329
  45.3 11.8 %collective-permute-start.4 = (f32[256,256]{1,0:T(8,128)S(1)}, f32[256,256]{1,0:T(8,128)S(1)}, u32[]{:S(2)}, u32[]{:S(2)}) collective-permute-start(f32[256,256]{1,0:T(8,128)S(1)} %get-tuple-element.33.near_sent), channel_id=1, source_target_pairs={{0,16},{16,0},{32,48},{48,32},{64,80},{80,64},{96,112},{112,96},{1... | collective-permute-start | bytes 786440 | tf_op jit(solution)/shard_map/ppermute | solution.py:331
  57.1 7.1 %all_to_all.30 = f32[4,16,256]{2,1,0:T(8,128)S(1)} all-to-all(f32[4,16,256]{2,1,0:T(8,128)S(1)} %get-tuple-element.31), channel_id=1, replica_groups={{0,128,256,384},{16,144,272,400},{32,160,288,416},{48,176,304,432},{64,..., dimensions={0} | all-to-all | bytes 131072 | tf_op jit(solution)/shard_map/all_to_all | solution.py:330
  64.2 7.0 %all_to_all.31.sums_ref = f32[4,16,256]{2,1,0:T(8,128)S(1)} all-to-all(f32[4,16,256]{2,1,0:T(8,128)S(1)} %broadcast_in_dim.24), channel_id=1, replica_groups={{0,32,64,96},{16,48,80,112},{128,160,192,224},{144,176,208,240},{256,28..., dimensions={0} | all-to-all | bytes 131072 | tf_op jit(solution)/shard_map/all_to_all | solution.py:333
  71.2 1.3 %shard_map.78 = (f32[256,256]{1,0:T(8,128)S(1)}, f32[256,256]{1,0:T(8,128)S(1)}, f32[4,16,256]{2,1,0:T(8,128)S(1)}) custom-call(s32[1]{0:T(128)} %bitcast.core_ref, s32[4,64]{1,0:T(4,128)S(1)} %copy-done.3, bf16[1,4,64,256]{3,2,1,0:T(8,128)(2,1)S(1)} %bitcast.8, bf16[256,256]{1,0:T(8,128)(2,1)S(1)} %get-tuple-element.24.own_a_ref.a_ref, ...), custom_call_target="tpu_custom_call" | custom-call | flops 400000000 | bytes 2000000 | tf_op jit(solution)/shard_map/pallas_call | solution.py:255
  72.5 4.8 %collective-permute-start.5 = (f32[256,256]{1,0:T(8,128)S(1)}, f32[256,256]{1,0:T(8,128)S(1)}, u32[]{:S(2)}, u32[]{:S(2)}) collective-permute-start(f32[256,256]{1,0:T(8,128)S(1)} %get-tuple-element.35.far_sent), channel_id=1, source_target_pairs={{0,31},{1,16},{2,17},{3,18},{4,19},{5,20},{6,21},{7,22},{8,23},{9,... | collective-permute-start | bytes 786440 | tf_op jit(solution)/shard_map/ppermute | solution.py:329
  77.3 1.9 %collective-permute-start.6 = (f32[256,256]{1,0:T(8,128)S(1)}, f32[256,256]{1,0:T(8,128)S(1)}, u32[]{:S(2)}, u32[]{:S(2)}) collective-permute-start(f32[256,256]{1,0:T(8,128)S(1)} %get-tuple-element.36.near_sent), channel_id=1, source_target_pairs={{0,16},{16,0},{32,48},{48,32},{64,80},{80,64},{96,112},{112,96},{1... | collective-permute-start | bytes 786440 | tf_op jit(solution)/shard_map/ppermute | solution.py:331
  79.2 7.1 %all_to_all.32 = f32[4,16,256]{2,1,0:T(8,128)S(1)} all-to-all(f32[4,16,256]{2,1,0:T(8,128)S(1)} %get-tuple-element.34), channel_id=1, replica_groups={{0,128,256,384},{16,144,272,400},{32,160,288,416},{48,176,304,432},{64,..., dimensions={0} | all-to-all | bytes 131072 | tf_op jit(solution)/shard_map/all_to_all | solution.py:330
  86.4 7.0 %all_to_all.33.sums_ref = f32[4,16,256]{2,1,0:T(8,128)S(1)} all-to-all(f32[4,16,256]{2,1,0:T(8,128)S(1)} %broadcast_in_dim.25), channel_id=1, replica_groups={{0,32,64,96},{16,48,80,112},{128,160,192,224},{144,176,208,240},{256,28..., dimensions={0} | all-to-all | bytes 131072 | tf_op jit(solution)/shard_map/all_to_all | solution.py:333
  93.4 0.5 shard_map.80
  93.9 4.4 %collective-permute-start.7 = (f32[256,256]{1,0:T(8,128)S(1)}, f32[256,256]{1,0:T(8,128)S(1)}, u32[]{:S(2)}, u32[]{:S(2)}) collective-permute-start(f32[256,256]{1,0:T(8,128)S(1)} %shard_map.80), channel_id=1, source_target_pairs={{0,16},{16,0},{32,48},{48,32},{64,80},{80,64},{96,112},{112,96},{1... | collective-permute-start | bytes 786440 | tf_op jit(solution)/shard_map/ppermute | solution.py:354
  98.3 0.5 shard_map.79.own_ref
  98.8 0.6 collective-permute-done.7.back_ref
  99.4 1.1 %shard_map.81 = f32[1,256,4,128]{3,2,1,0:T(4,128)} custom-call(s32[1]{0:T(128)} %bitcast.core_ref, f32[256,256]{1,0:T(8,128)S(1)} %shard_map.79.own_ref, f32[256,256]{1,0:T(8,128)S(1)} %collective-permute-done.7.back_ref), custom_call_target="tpu_custom_call" | custom-call | flops 400000000 | bytes 2000000 | tf_op jit(solution)/shard_map/pallas_call | solution.py:255
  (21 shorter events, 0.1 us)
Async XLA Ops:
  0.0 15.4 %copy-start.4 = (bf16[1,256,4,128]{3,2,1,0:T(4,128)(2,1)S(1)}, bf16[1,256,4,128]{3,2,1,0:T(4,128)(2,1)}, u32[]{:S(2)}) copy-start(bf16[1,256,4,128]{3,2,1,0:T(4,128)(2,1)} %anomalies_ref) | copy-start | bytes 786436
  3.1 12.2 %collective-permute-start = (f32[64,256]{1,0:T(8,128)}, f32[64,256]{1,0:T(8,128)S(1)}, u32[]{:S(2)}, u32[]{:S(2)}) collective-permute-start(f32[64,256]{1,0:T(8,128)} %get-tuple-element.21.late_ref), channel_id=1, source_target_pairs={{0,16},{16,0},{32,48},{48,32},{64,80},{80,64},{96,112},{112,96},{1... | collective-permute-start | bytes 196616 | tf_op jit(solution)/shard_map/ppermute | solution.py:303
  11.8 3.5 %copy-start.1 = (bf16[1,4,256,64]{2,3,1,0:T(8,128)(2,1)S(1)}, bf16[1,4,256,64]{2,3,1,0:T(8,128)(2,1)}, u32[]{:S(2)}) copy-start(bf16[1,4,256,64]{2,3,1,0:T(8,128)(2,1)} %param.7) | copy-start | bytes 393220
  11.8 8.5 %all-to-all-start = ((f32[4,16,512]{2,1,0:T(8,128)}), f32[4,16,512]{2,1,0:T(8,128)S(1)}, u32[]{:S(2)}, u32[]{:S(2)}) async-start(f32[4,16,512]{2,1,0:T(8,128)} %get-tuple-element.28), calls=%async_computation | async-start | bytes 262144 | tf_op jit(solution)/shard_map/all_to_all | solution.py:302
  15.3 0.7 copy-start.6
  15.3 0.7 copy-start.7
  17.2 18.8 %collective-permute-start.1 = (f32[448,256]{1,0:T(8,128)S(1)}, f32[448,256]{1,0:T(8,128)S(1)}, u32[]{:S(2)}, u32[]{:S(2)}) collective-permute-start(f32[448,256]{1,0:T(8,128)S(1)} %get-tuple-element.27), channel_id=1, source_target_pairs={{0,16},{16,0},{32,48},{48,32},{64,80},{80,64},{96,112},{112,96},{1... | collective-permute-start | bytes 1376264 | tf_op jit(solution)/shard_map/ppermute | solution.py:316
  20.3 5.2 %copy-start.3 = (s32[4,64]{1,0:T(4,128)S(1)}, s32[4,64]{1,0:T(4,128)}, u32[]{:S(2)}) copy-start(s32[4,64]{1,0:T(4,128)} %obs_ref.11) | copy-start | bytes 3076
  20.3 5.2 %copy-start.5 = (f32[64,256]{1,0:T(8,128)S(1)}, f32[64,256]{1,0:T(8,128)}, u32[]{:S(2)}) copy-start(f32[64,256]{1,0:T(8,128)} %get-tuple-element.21.late_ref) | copy-start | bytes 196612
  21.0 15.0 %copy-start = (f32[4,256,256]{2,1,0:T(8,128)S(1)}, f32[4,256,256]{2,1,0:T(8,128)}, u32[]{:S(2)}) copy-start(f32[4,256,256]{2,1,0:T(8,128)} %physics_ref.3) | copy-start | bytes 3145732
  21.0 15.0 %all-to-all-start.1 = ((f32[8,16,256]{2,1,0:T(8,128)}), f32[8,16,256]{2,1,0:T(8,128)S(1)}, u32[]{:S(2)}, u32[]{:S(2)}) async-start(f32[8,16,256]{2,1,0:T(8,128)} %shard_map.76), calls=%async_computation.1 | async-start | bytes 262144 | tf_op jit(solution)/shard_map/all_to_all | solution.py:307
  25.6 10.4 %copy-start.2 = (f32[256,16]{0,1:T(8,128)S(1)}, f32[256,16]{0,1:T(8,128)}, u32[]{:S(2)}) copy-start(f32[256,16]{0,1:T(8,128)} %param.12) | copy-start | bytes 49156
  25.6 10.3 %collective-permute-start.2 = (f32[136,256]{1,0:T(8,128)S(1)}, f32[136,256]{1,0:T(8,128)S(1)}, u32[]{:S(2)}, u32[]{:S(2)}) collective-permute-start(f32[136,256]{1,0:T(8,128)S(1)} %shard_map.75), channel_id=1, source_target_pairs={{0,31},{1,16},{2,17},{3,18},{4,19},{5,20},{6,21},{7,22},{8,23},{9,... | collective-permute-start | bytes 417800 | tf_op jit(solution)/shard_map/ppermute | solution.py:305
  37.9 33.3 %collective-permute-start.3 = (f32[256,256]{1,0:T(8,128)S(1)}, f32[256,256]{1,0:T(8,128)S(1)}, u32[]{:S(2)}, u32[]{:S(2)}) collective-permute-start(f32[256,256]{1,0:T(8,128)S(1)} %get-tuple-element.32.far_sent), channel_id=1, source_target_pairs={{0,31},{1,16},{2,17},{3,18},{4,19},{5,20},{6,21},{7,22},{8,23},{9,... | collective-permute-start | bytes 786440 | tf_op jit(solution)/shard_map/ppermute | solution.py:329
  45.3 25.9 %collective-permute-start.4 = (f32[256,256]{1,0:T(8,128)S(1)}, f32[256,256]{1,0:T(8,128)S(1)}, u32[]{:S(2)}, u32[]{:S(2)}) collective-permute-start(f32[256,256]{1,0:T(8,128)S(1)} %get-tuple-element.33.near_sent), channel_id=1, source_target_pairs={{0,16},{16,0},{32,48},{48,32},{64,80},{80,64},{96,112},{112,96},{1... | collective-permute-start | bytes 786440 | tf_op jit(solution)/shard_map/ppermute | solution.py:331
  72.5 20.9 %collective-permute-start.5 = (f32[256,256]{1,0:T(8,128)S(1)}, f32[256,256]{1,0:T(8,128)S(1)}, u32[]{:S(2)}, u32[]{:S(2)}) collective-permute-start(f32[256,256]{1,0:T(8,128)S(1)} %get-tuple-element.35.far_sent), channel_id=1, source_target_pairs={{0,31},{1,16},{2,17},{3,18},{4,19},{5,20},{6,21},{7,22},{8,23},{9,... | collective-permute-start | bytes 786440 | tf_op jit(solution)/shard_map/ppermute | solution.py:329
  77.3 16.1 %collective-permute-start.6 = (f32[256,256]{1,0:T(8,128)S(1)}, f32[256,256]{1,0:T(8,128)S(1)}, u32[]{:S(2)}, u32[]{:S(2)}) collective-permute-start(f32[256,256]{1,0:T(8,128)S(1)} %get-tuple-element.36.near_sent), channel_id=1, source_target_pairs={{0,16},{16,0},{32,48},{48,32},{64,80},{80,64},{96,112},{112,96},{1... | collective-permute-start | bytes 786440 | tf_op jit(solution)/shard_map/ppermute | solution.py:331
  93.9 5.5 %collective-permute-start.7 = (f32[256,256]{1,0:T(8,128)S(1)}, f32[256,256]{1,0:T(8,128)S(1)}, u32[]{:S(2)}, u32[]{:S(2)}) collective-permute-start(f32[256,256]{1,0:T(8,128)S(1)} %shard_map.80), channel_id=1, source_target_pairs={{0,16},{16,0},{32,48},{48,32},{64,80},{80,64},{96,112},{112,96},{1... | collective-permute-start | bytes 786440 | tf_op jit(solution)/shard_map/ppermute | solution.py:354

commit v9 on v4

--- a/solution.py
+++ b/solution.py
@@ -206,12 +206,20 @@
     send_parts(lam, spread, matrix, modes_ref, far_out, near_out, sums_out, width_y)
 
 
-def last_kernel(step, width_y, members, core_ref, obs_ref, mine_ref, own_a_ref, other_a_ref, other_ref,
-                modes_ref, bands_ref, nu_ref, sums_ref, far_sent, near_sent, far_ref, near_ref, own_out, other_out):
-    lam, _ = next_lam(step, width_y, members, core_ref, obs_ref, mine_ref, own_a_ref, other_a_ref, other_ref,
-                      modes_ref, bands_ref, nu_ref, sums_ref, far_sent, near_sent, far_ref, near_ref)
-    own_out[...] = lam[0]
-    other_out[...] = lam[1]
+def last_kernel(member, step, width_y, members, core_ref, obs_ref, values_ref, a_ref, modes_ref, bands_ref, nu_ref, sums_ref,
+                far_sent, near_sent, far_ref, near_ref, out_ref):
+    w = width_y
+    total = sums_ref[0] + sums_ref[1] + sums_ref[2] + sums_ref[3]
+    lifted = dot(modes_ref[...], smooth_of(total, bands_ref[...], w, members), TM)
+    count = obs_ref.shape[1]
+    values = values_ref[step * count : (step + 1) * count, :] if member else values_ref[0, step]
+    force = placed(values, hot_rows(core_ref[0], obs_ref[step : step + 1, :], (0, 1), w))
+    nu = nu_ref[...]
+    cut = lambda ref, m: ref[:, m * w : (m + 1) * w]
+    far, near, out_near, out_far = cut(far_sent, member), cut(near_sent, member), cut(near_ref, 1 - member), cut(far_ref, 1 - member)
+    v_far = far + nu * (out_far + near + beside(far, w) - 4.0 * far)
+    v_near = near + nu * (far + out_near + beside(near, w) - 4.0 * near)
+    out_ref[...] = jnp.concatenate([v_far, v_near], axis=1) + a_ref[...].astype(jnp.float32) * lifted + force
 
 
 def finish_kernel(width_y, core_ref, own_ref, back_ref, out_ref):
@@ -314,13 +322,16 @@
                 known + (physics[step - 1],) + tail,
                 [half, half, sums_shape],
             )
-        else:
-            own, other = call(
-                functools.partial(last_kernel, step, width_y, members),
-                "last",
-                known + tail,
-                [half, half],
-            )
+    ends = []
+    for member, values, a in ((1, other_innov, other_a), (0, mine, own_a)):
+        (end,) = call(
+            functools.partial(last_kernel, member, 0, width_y, members),
+            f"last{member}",
+            (core, obs_column, values, a) + tail,
+            [half],
+        )
+        ends.append(end)
+    other, own = ends
     back = lax.ppermute(other, "member", swap)
     return call(functools.partial(finish_kernel, width_y), "finish", (core, own, back), [(1, *anomalies.shape[1:])])[0]
 

time: 104 us -> 104 us (level)
    pallas_call x8 -> x9, Pallas kernels: 9.27 us -> 9.54 us  [call(): pl.pallas_call(kernel, in_specs=[pl.BlockSpec(memory_space=space) for spa...]
  transfers between devices with their start and end apart: 10 -> 10, of which waited for: 3 -> 3; matrix products, arithmetic and copies ran while one was open for 1% -> 1% of each run, Pallas kernels for 1% -> 2%
where the time goes in v9:
time: 104 us; the launch traced here: 103 us
  starting transfers between devices  52.8 us (51%)
  blocking collectives  28.2 us (27%)
  Pallas kernels  9.54 us (9%)
  waiting for transfers between devices  8.97 us (9%)
  local copies, waits for them, and re-layouts  3.46 us (3%)
    ppermute x2, starting transfers between devices, per_device(): near = lax.ppermute(near_sent, 'member', swap)  15.3 us
    all_to_all x2, blocking collectives, per_device(): lax.all_to_all(sums, 'member', 0, 0, tiled=True, axis_index_groups=y_groups)  14.3 us
    all_to_all x2, blocking collectives, per_device(): lax.all_to_all(sums, 'member', 0, 0, tiled=True, axis_index_groups=z_groups)  13.9 us
    pallas_call x9, Pallas kernels, call(): pl.pallas_call(kernel, in_specs=[pl.BlockSpec(memory_space=space) for spa...  9.54 us
    ppermute x1, starting transfers between devices, per_device(): other_late = lax.ppermute(late, 'member', swap)  8.75 us
    ppermute x2, starting transfers between devices, per_device(): far = lax.ppermute(far_sent, ('member', 'tile'), far_pairs)  8.1 us
    ppermute x1, starting transfers between devices, per_device(): beyond = lax.ppermute(beyond, ('member', 'tile'), far_pairs)  6.93 us
    ppermute x1, waiting for transfers between devices, per_device(): beyond = lax.ppermute(beyond, ('member', 'tile'), far_pairs)  6.04 us
  transfers between devices with their start and end apart: 10, of which 3 were waited for; matrix products, arithmetic and copies ran while one was open for 1% of the time, Pallas kernels for 2%

profile of v9, /device:TPU:1, one launch (start us, length us, event | category | flops | bytes accessed | tf_op | source)
XLA Modules:
  0.0 103.2 jit_solution(11901786528935390170)
XLA Ops:
  0.0 3.1 %shard_map.73 = (f32[64,256]{1,0:T(8,128)}, f32[4,16,512]{2,1,0:T(8,128)}) custom-call(s32[1]{0:T(128)} %bitcast.core_ref, s32[4,64]{1,0:T(4,128)} %obs_ref.11, bf16[1,4,64,256]{3,2,1,0:T(8,128)(2,1)} %bitcast.11, bf16[1,256,4,128]{3,2,1,0:T(4,128)(2,1)} %anomalies_ref, f32[16,256]{1,0:T(8,128)} %bitcast.16), custom_call_target="tpu_custom_call" | custom-call | flops 400000000 | bytes 2000000 | tf_op jit(solution)/shard_map/pallas_call | solution.py:239
  3.1 8.7 %collective-permute-start = (f32[64,256]{1,0:T(8,128)}, f32[64,256]{1,0:T(8,128)S(1)}, u32[]{:S(2)}, u32[]{:S(2)}) collective-permute-start(f32[64,256]{1,0:T(8,128)} %get-tuple-element.19.late_ref), channel_id=1, source_target_pairs={{0,16},{16,0},{32,48},{48,32},{64,80},{80,64},{96,112},{112,96},{1... | collective-permute-start | bytes 196616 | tf_op jit(solution)/shard_map/ppermute | solution.py:288
  11.8 3.5 %all-to-all-start = ((f32[4,16,512]{2,1,0:T(8,128)}), f32[4,16,512]{2,1,0:T(8,128)S(1)}, u32[]{:S(2)}, u32[]{:S(2)}) async-start(f32[4,16,512]{2,1,0:T(8,128)} %get-tuple-element.24), calls=%async_computation | async-start | bytes 262144 | tf_op jit(solution)/shard_map/all_to_all | solution.py:287
  15.4 0.8 shard_map.74
  16.1 1.9 %collective-permute-start.1 = (f32[448,256]{1,0:T(8,128)S(1)}, f32[448,256]{1,0:T(8,128)S(1)}, u32[]{:S(2)}, u32[]{:S(2)}) collective-permute-start(f32[448,256]{1,0:T(8,128)S(1)} %get-tuple-element.23), channel_id=1, source_target_pairs={{0,16},{16,0},{32,48},{48,32},{64,80},{80,64},{96,112},{112,96},{1... | collective-permute-start | bytes 1376264 | tf_op jit(solution)/shard_map/ppermute | solution.py:301
  18.1 2.3 %all-to-all-done.sums_ref = f32[4,16,512]{2,1,0:T(8,128)S(1)} async-done(((f32[4,16,512]{2,1,0:T(8,128)}), f32[4,16,512]{2,1,0:T(8,128)S(1)}, u32[]{:S(2)}, u32[]{:S(2)}) %all-to-all-start) | async-done | bytes 131104 | tf_op jit(solution)/shard_map/all_to_all | solution.py:287
  20.3 0.7 shard_map.76
  21.0 4.4 %all-to-all-start.1 = ((f32[8,16,256]{2,1,0:T(8,128)}), f32[8,16,256]{2,1,0:T(8,128)S(1)}, u32[]{:S(2)}, u32[]{:S(2)}) async-start(f32[8,16,256]{2,1,0:T(8,128)} %shard_map.76), calls=%async_computation.1 | async-start | bytes 262144 | tf_op jit(solution)/shard_map/all_to_all | solution.py:292
  25.5 0.7 copy-done.6
  26.1 0.1 copy.16.bands_ref
  26.2 0.7 copy-done.5
  26.9 0.1 copy.17.nu_ref
  27.0 0.5 copy-done.2
  27.6 0.2 copy-done.4
  27.7 6.9 %collective-permute-start.2 = (f32[136,256]{1,0:T(8,128)S(1)}, f32[136,256]{1,0:T(8,128)S(1)}, u32[]{:S(2)}, u32[]{:S(2)}) collective-permute-start(f32[136,256]{1,0:T(8,128)S(1)} %shard_map.75), channel_id=1, source_target_pairs={{0,31},{1,16},{2,17},{3,18},{4,19},{5,20},{6,21},{7,22},{8,23},{9,... | collective-permute-start | bytes 417800 | tf_op jit(solution)/shard_map/ppermute | solution.py:290
  34.7 1.2 %slice_bitcast_fusion = (f32[256,256]{1,0:T(8,128)S(1)}, f32[256,256]{1,0:T(8,128)S(1)}, f32[256,256]{1,0:T(8,128)S(1)}) fusion(f32[4,256,256]{2,1,0:T(8,128)} %param.9), kind=kLoop, calls=%fused_computation | loop fusion | bytes 1572864 | tf_op jit(solution)/shard_map/squeeze | solution.py:322
  35.9 6.0 %collective-permute-done.2.beyond_ref = f32[136,256]{1,0:T(8,128)S(1)} collective-permute-done((f32[136,256]{1,0:T(8,128)S(1)}, f32[136,256]{1,0:T(8,128)S(1)}, u32[]{:S(2)}, u32[]{:S(2)}) %collective-permute-start.2) | collective-permute-done | bytes 139296 | tf_op jit(solution)/shard_map/ppermute | solution.py:290
  41.9 1.8 %shard_map.77 = (f32[256,256]{1,0:T(8,128)S(1)}, f32[256,256]{1,0:T(8,128)S(1)}, f32[4,16,256]{2,1,0:T(8,128)S(1)}, bf16[256,256]{1,0:T(8,128)(2,1)S(1)}, bf16[192,256]{1,0:T(8,128)(2,1)S(1)}) custom-call(s32[1]{0:T(128)} %bitcast.core_ref, s32[4,64]{1,0:T(4,128)S(1)} %copy-done.2, bf16[1,4,64,256]{3,2,1,0:T(8,128)(2,1)S(1)} %bitcast.13, ...), custom_call_target="tpu_custom_call" | custom-call | flops 400000000 | bytes 2000000 | tf_op jit(solution)/shard_map/pallas_call | solution.py:239
  43.7 3.4 %collective-permute-start.3 = (f32[256,256]{1,0:T(8,128)S(1)}, f32[256,256]{1,0:T(8,128)S(1)}, u32[]{:S(2)}, u32[]{:S(2)}) collective-permute-start(f32[256,256]{1,0:T(8,128)S(1)} %get-tuple-element.28.far_sent), channel_id=1, source_target_pairs={{0,31},{1,16},{2,17},{3,18},{4,19},{5,20},{6,21},{7,22},{8,23},{9,... | collective-permute-start | bytes 786440 | tf_op jit(solution)/shard_map/ppermute | solution.py:312
  47.0 12.0 %collective-permute-start.4 = (f32[256,256]{1,0:T(8,128)S(1)}, f32[256,256]{1,0:T(8,128)S(1)}, u32[]{:S(2)}, u32[]{:S(2)}) collective-permute-start(f32[256,256]{1,0:T(8,128)S(1)} %get-tuple-element.29.near_sent), channel_id=1, source_target_pairs={{0,16},{16,0},{32,48},{48,32},{64,80},{80,64},{96,112},{112,96},{1... | collective-permute-start | bytes 786440 | tf_op jit(solution)/shard_map/ppermute | solution.py:314
  59.0 7.1 %all_to_all.30 = f32[4,16,256]{2,1,0:T(8,128)S(1)} all-to-all(f32[4,16,256]{2,1,0:T(8,128)S(1)} %get-tuple-element.27), channel_id=1, replica_groups={{0,128,256,384},{16,144,272,400},{32,160,288,416},{48,176,304,432},{64,..., dimensions={0} | all-to-all | bytes 131072 | tf_op jit(solution)/shard_map/all_to_all | solution.py:313
  66.2 7.0 %all_to_all.31.sums_ref = f32[4,16,256]{2,1,0:T(8,128)S(1)} all-to-all(f32[4,16,256]{2,1,0:T(8,128)S(1)} %broadcast_in_dim.24), channel_id=1, replica_groups={{0,32,64,96},{16,48,80,112},{128,160,192,224},{144,176,208,240},{256,28..., dimensions={0} | all-to-all | bytes 131072 | tf_op jit(solution)/shard_map/all_to_all | solution.py:316
  73.2 1.2 %shard_map.78 = (f32[256,256]{1,0:T(8,128)S(1)}, f32[256,256]{1,0:T(8,128)S(1)}, f32[4,16,256]{2,1,0:T(8,128)S(1)}) custom-call(s32[1]{0:T(128)} %bitcast.core_ref, s32[4,64]{1,0:T(4,128)S(1)} %copy-done.2, bf16[1,4,64,256]{3,2,1,0:T(8,128)(2,1)S(1)} %bitcast.14, bf16[256,256]{1,0:T(8,128)(2,1)S(1)} %get-tuple-element.22.own_a_ref.a_ref, ...), custom_call_target="tpu_custom_call" | custom-call | flops 400000000 | bytes 2000000 | tf_op jit(solution)/shard_map/pallas_call | solution.py:239
  74.3 4.8 %collective-permute-start.5 = (f32[256,256]{1,0:T(8,128)S(1)}, f32[256,256]{1,0:T(8,128)S(1)}, u32[]{:S(2)}, u32[]{:S(2)}) collective-permute-start(f32[256,256]{1,0:T(8,128)S(1)} %get-tuple-element.31.far_sent), channel_id=1, source_target_pairs={{0,31},{1,16},{2,17},{3,18},{4,19},{5,20},{6,21},{7,22},{8,23},{9,... | collective-permute-start | bytes 786440 | tf_op jit(solution)/shard_map/ppermute | solution.py:312
  79.1 3.3 %collective-permute-start.6 = (f32[256,256]{1,0:T(8,128)S(1)}, f32[256,256]{1,0:T(8,128)S(1)}, u32[]{:S(2)}, u32[]{:S(2)}) collective-permute-start(f32[256,256]{1,0:T(8,128)S(1)} %get-tuple-element.32.near_sent), channel_id=1, source_target_pairs={{0,16},{16,0},{32,48},{48,32},{64,80},{80,64},{96,112},{112,96},{1... | collective-permute-start | bytes 786440 | tf_op jit(solution)/shard_map/ppermute | solution.py:314
  82.4 7.1 %all_to_all.32 = f32[4,16,256]{2,1,0:T(8,128)S(1)} all-to-all(f32[4,16,256]{2,1,0:T(8,128)S(1)} %get-tuple-element.30), channel_id=1, replica_groups={{0,128,256,384},{16,144,272,400},{32,160,288,416},{48,176,304,432},{64,..., dimensions={0} | all-to-all | bytes 131072 | tf_op jit(solution)/shard_map/all_to_all | solution.py:313
  89.6 7.0 %all_to_all.33.sums_ref = f32[4,16,256]{2,1,0:T(8,128)S(1)} all-to-all(f32[4,16,256]{2,1,0:T(8,128)S(1)} %broadcast_in_dim.25), channel_id=1, replica_groups={{0,32,64,96},{16,48,80,112},{128,160,192,224},{144,176,208,240},{256,28..., dimensions={0} | all-to-all | bytes 131072 | tf_op jit(solution)/shard_map/all_to_all | solution.py:316
  96.5 0.5 shard_map.80
  97.0 3.9 %collective-permute-start.7 = (f32[256,256]{1,0:T(8,128)S(1)}, f32[256,256]{1,0:T(8,128)S(1)}, u32[]{:S(2)}, u32[]{:S(2)}) collective-permute-start(f32[256,256]{1,0:T(8,128)S(1)} %shard_map.80), channel_id=1, source_target_pairs={{0,16},{16,0},{32,48},{48,32},{64,80},{80,64},{96,112},{112,96},{1... | collective-permute-start | bytes 786440 | tf_op jit(solution)/shard_map/ppermute | solution.py:335
  101.0 0.5 shard_map.79.own_ref
  101.5 0.6 collective-permute-done.7.back_ref
  102.1 1.1 %shard_map.81 = f32[1,256,4,128]{3,2,1,0:T(4,128)} custom-call(s32[1]{0:T(128)} %bitcast.core_ref, f32[256,256]{1,0:T(8,128)S(1)} %shard_map.79.own_ref, f32[256,256]{1,0:T(8,128)S(1)} %collective-permute-done.7.back_ref), custom_call_target="tpu_custom_call" | custom-call | flops 400000000 | bytes 2000000 | tf_op jit(solution)/shard_map/pallas_call | solution.py:239
  (22 shorter events, 0.1 us)
Async XLA Ops:
  0.0 15.3 %copy-start.3 = (bf16[1,256,4,128]{3,2,1,0:T(4,128)(2,1)S(1)}, bf16[1,256,4,128]{3,2,1,0:T(4,128)(2,1)}, u32[]{:S(2)}) copy-start(bf16[1,256,4,128]{3,2,1,0:T(4,128)(2,1)} %anomalies_ref) | copy-start | bytes 786436
  3.1 12.2 %collective-permute-start = (f32[64,256]{1,0:T(8,128)}, f32[64,256]{1,0:T(8,128)S(1)}, u32[]{:S(2)}, u32[]{:S(2)}) collective-permute-start(f32[64,256]{1,0:T(8,128)} %get-tuple-element.19.late_ref), channel_id=1, source_target_pairs={{0,16},{16,0},{32,48},{48,32},{64,80},{80,64},{96,112},{112,96},{1... | collective-permute-start | bytes 196616 | tf_op jit(solution)/shard_map/ppermute | solution.py:288
  11.8 3.5 %copy-start = (bf16[1,4,256,64]{2,3,1,0:T(8,128)(2,1)S(1)}, bf16[1,4,256,64]{2,3,1,0:T(8,128)(2,1)}, u32[]{:S(2)}) copy-start(bf16[1,4,256,64]{2,3,1,0:T(8,128)(2,1)} %param.7) | copy-start | bytes 393220
  11.8 8.5 %all-to-all-start = ((f32[4,16,512]{2,1,0:T(8,128)}), f32[4,16,512]{2,1,0:T(8,128)S(1)}, u32[]{:S(2)}, u32[]{:S(2)}) async-start(f32[4,16,512]{2,1,0:T(8,128)} %get-tuple-element.24), calls=%async_computation | async-start | bytes 262144 | tf_op jit(solution)/shard_map/all_to_all | solution.py:287
  16.1 25.8 %collective-permute-start.1 = (f32[448,256]{1,0:T(8,128)S(1)}, f32[448,256]{1,0:T(8,128)S(1)}, u32[]{:S(2)}, u32[]{:S(2)}) collective-permute-start(f32[448,256]{1,0:T(8,128)S(1)} %get-tuple-element.23), channel_id=1, source_target_pairs={{0,16},{16,0},{32,48},{48,32},{64,80},{80,64},{96,112},{112,96},{1... | collective-permute-start | bytes 1376264 | tf_op jit(solution)/shard_map/ppermute | solution.py:301
  21.0 20.9 %all-to-all-start.1 = ((f32[8,16,256]{2,1,0:T(8,128)}), f32[8,16,256]{2,1,0:T(8,128)S(1)}, u32[]{:S(2)}, u32[]{:S(2)}) async-start(f32[8,16,256]{2,1,0:T(8,128)} %shard_map.76), calls=%async_computation.1 | async-start | bytes 262144 | tf_op jit(solution)/shard_map/all_to_all | solution.py:292
  25.5 0.7 copy-start.6
  26.2 0.7 copy-start.5
  26.9 0.7 copy-start.2
  26.9 0.9 copy-start.4
  27.7 14.2 %collective-permute-start.2 = (f32[136,256]{1,0:T(8,128)S(1)}, f32[136,256]{1,0:T(8,128)S(1)}, u32[]{:S(2)}, u32[]{:S(2)}) collective-permute-start(f32[136,256]{1,0:T(8,128)S(1)} %shard_map.75), channel_id=1, source_target_pairs={{0,31},{1,16},{2,17},{3,18},{4,19},{5,20},{6,21},{7,22},{8,23},{9,... | collective-permute-start | bytes 417800 | tf_op jit(solution)/shard_map/ppermute | solution.py:290
  34.7 7.2 %copy-start.1 = (f32[256,16]{0,1:T(8,128)S(1)}, f32[256,16]{0,1:T(8,128)}, u32[]{:S(2)}) copy-start(f32[256,16]{0,1:T(8,128)} %param.12) | copy-start | bytes 49156
  43.7 29.5 %collective-permute-start.3 = (f32[256,256]{1,0:T(8,128)S(1)}, f32[256,256]{1,0:T(8,128)S(1)}, u32[]{:S(2)}, u32[]{:S(2)}) collective-permute-start(f32[256,256]{1,0:T(8,128)S(1)} %get-tuple-element.28.far_sent), channel_id=1, source_target_pairs={{0,31},{1,16},{2,17},{3,18},{4,19},{5,20},{6,21},{7,22},{8,23},{9,... | collective-permute-start | bytes 786440 | tf_op jit(solution)/shard_map/ppermute | solution.py:312
  47.0 26.1 %collective-permute-start.4 = (f32[256,256]{1,0:T(8,128)S(1)}, f32[256,256]{1,0:T(8,128)S(1)}, u32[]{:S(2)}, u32[]{:S(2)}) collective-permute-start(f32[256,256]{1,0:T(8,128)S(1)} %get-tuple-element.29.near_sent), channel_id=1, source_target_pairs={{0,16},{16,0},{32,48},{48,32},{64,80},{80,64},{96,112},{112,96},{1... | collective-permute-start | bytes 786440 | tf_op jit(solution)/shard_map/ppermute | solution.py:314
  74.3 22.2 %collective-permute-start.5 = (f32[256,256]{1,0:T(8,128)S(1)}, f32[256,256]{1,0:T(8,128)S(1)}, u32[]{:S(2)}, u32[]{:S(2)}) collective-permute-start(f32[256,256]{1,0:T(8,128)S(1)} %get-tuple-element.31.far_sent), channel_id=1, source_target_pairs={{0,31},{1,16},{2,17},{3,18},{4,19},{5,20},{6,21},{7,22},{8,23},{9,... | collective-permute-start | bytes 786440 | tf_op jit(solution)/shard_map/ppermute | solution.py:312
  79.1 17.4 %collective-permute-start.6 = (f32[256,256]{1,0:T(8,128)S(1)}, f32[256,256]{1,0:T(8,128)S(1)}, u32[]{:S(2)}, u32[]{:S(2)}) collective-permute-start(f32[256,256]{1,0:T(8,128)S(1)} %get-tuple-element.32.near_sent), channel_id=1, source_target_pairs={{0,16},{16,0},{32,48},{48,32},{64,80},{80,64},{96,112},{112,96},{1... | collective-permute-start | bytes 786440 | tf_op jit(solution)/shard_map/ppermute | solution.py:314
  97.0 5.1 %collective-permute-start.7 = (f32[256,256]{1,0:T(8,128)S(1)}, f32[256,256]{1,0:T(8,128)S(1)}, u32[]{:S(2)}, u32[]{:S(2)}) collective-permute-start(f32[256,256]{1,0:T(8,128)S(1)} %shard_map.80), channel_id=1, source_target_pairs={{0,16},{16,0},{32,48},{48,32},{64,80},{80,64},{96,112},{112,96},{1... | collective-permute-start | bytes 786440 | tf_op jit(solution)/shard_map/ppermute | solution.py:335
